TPU v7x, 128 devices: a whole 4x4x4 slice. The times are simulated.
128 devices in a mesh: row: 16 (over y, x), col: 8 (over z, core).
Axes of the slice: x: 4, y: 4, z: 4, core: 2. Of those that a mesh axis runs over, the one named last changes fastest.
Arguments:
- field: float32 [64, 256, 1024], P(None, 'row', 'col'), may hold values from -4 to 6.5, as said below
- conductivity: float32 [64, 256, 1024], P(None, 'row', 'col'), may hold values from 35 to 5600, as said below
Outputs:
- new_field: float32 [64, 256, 1024], P(None, 'row', 'col')
Inputs may be any that keep to these rules, and one draw needn't show every extreme that they name: `field`: finite values. `conductivity`: positive in every cell.
All inputs are finite; a program needn't handle non-finite values.
Results may differ from a plain program's by a relative error of at most 0.0003.
Values sent between devices are 32-bit elements; how exact they have to be, the bound alone decides.
No kernel may reach another device: no remote copies, remote signals or barrier semaphores. Data moves between devices by JAX's collectives and lax.ppermute only.
A program may use at most 64 MiB of HBM per device.

v0:
```python
import jax
import jax.numpy as jnp
from jax import lax
from jax.sharding import PartitionSpec as P

z_weight = 0.02


def padded_2(array, sides, width):
    edges = {}
    for axis, dim in sides:
        peers, length = (lax.axis_size(axis), array.shape[dim])
        up = [(i, (i + 1) % peers) for i in range(peers - 1)]
        last = lax.slice_in_dim(array, length - width, length, axis=dim)
        initial = lax.slice_in_dim(array, 0, width, axis=dim)
        edges[dim] = (
            lax.ppermute(last, axis, up),
            lax.ppermute(initial, axis, [(b, a) for a, b in up]),
        )
    done = []
    for _, dim in sides:
        low, high = edges[dim]
        around = [(width, width) if d in done else (0, 0) for d in range(array.ndim)]
        array = jnp.concatenate([jnp.pad(low, around), array, jnp.pad(high, around)], axis=dim)
        done.append(dim)
    return array


def neighbour(values, line_axis, offset):
    length = values.shape[line_axis]
    widths = [(0, 0)] * values.ndim
    widths[line_axis] = (1, 1)
    padded = jnp.pad(values, widths)
    return lax.slice_in_dim(padded, 1 + offset, 1 + offset + length, axis=line_axis)


def shifted(values, line_axis, stride, fill):
    length = values.shape[line_axis]
    pad_shape = list(values.shape)
    pad_shape[line_axis] = abs(stride)
    padding = jnp.full(pad_shape, fill, values.dtype)
    if stride > 0:
        kept_part = lax.slice_in_dim(values, 0, length - stride, axis=line_axis)
        return jnp.concatenate((padding, kept_part), axis=line_axis)
    kept_part = lax.slice_in_dim(values, -stride, length, axis=line_axis)
    return jnp.concatenate((kept_part, padding), axis=line_axis)


def reduce_lines(below_diag, diagonal, above_diag, columns, line_axis):
    length = diagonal.shape[line_axis]
    stride = 1
    while stride < length:
        left_factor = -below_diag / shifted(diagonal, line_axis, stride, 1.0)
        right_factor = -above_diag / shifted(diagonal, line_axis, -stride, 1.0)
        new_diag = (
            diagonal
            + left_factor * shifted(above_diag, line_axis, stride, 0.0)
            + right_factor * shifted(below_diag, line_axis, -stride, 0.0)
        )
        new_below = left_factor * shifted(below_diag, line_axis, stride, 0.0)
        new_above = right_factor * shifted(above_diag, line_axis, -stride, 0.0)
        columns = [
            column
            + left_factor * shifted(column, line_axis, stride, 0.0)
            + right_factor * shifted(column, line_axis, -stride, 0.0)
            for column in columns
        ]
        below_diag, diagonal, above_diag = (new_below, new_diag, new_above)
        stride = stride * 2
    return (diagonal, columns)


def solve_whole(below_diag, above_diag, right_side, line_axis):
    diagonal = 1.0 - below_diag - above_diag
    diagonal, columns = reduce_lines(below_diag, diagonal, above_diag, [right_side], line_axis)
    return columns[0] / diagonal


def on_device(field, conductivity):
    stacked = jnp.stack((field, conductivity))
    padded = padded_2(stacked, (("row", 2), ("col", 3)), 1)
    field_pad = padded[0]
    cond_pad = padded[1]
    west_cond = cond_pad[:, :-2, 1:-1]
    east_cond = cond_pad[:, 2:, 1:-1]
    south_cond = cond_pad[:, 1:-1, :-2]
    north_cond = cond_pad[:, 1:-1, 2:]
    west_field = field_pad[:, :-2, 1:-1]
    east_field = field_pad[:, 2:, 1:-1]
    south_field = field_pad[:, 1:-1, :-2]
    north_field = field_pad[:, 1:-1, 2:]
    east_xdir = 0.5 * 1.0 * (conductivity + east_cond)
    west_xdir = 0.5 * 1.0 * (conductivity + west_cond)
    east_ydir = 0.5 * 1.0 * (conductivity + north_cond)
    west_ydir = 0.5 * 1.0 * (conductivity + south_cond)
    flux_xdir = east_xdir * (east_field - field) - west_xdir * (field - west_field)
    flux_ydir = east_ydir * (north_field - field) - west_ydir * (field - south_field)
    east_zdir = 0.5 * z_weight * (conductivity + neighbour(conductivity, 0, 1))
    west_zdir = 0.5 * z_weight * (conductivity + neighbour(conductivity, 0, -1))
    flux_zdir = east_zdir * (neighbour(field, 0, 1) - field) - west_zdir * (
        field - neighbour(field, 0, -1)
    )
    explicit = flux_xdir + flux_ydir + flux_zdir
    pieces = (
        lax.all_to_all(-west_xdir, "row", split_axis=0, concat_axis=1, tiled=True),
        lax.all_to_all(-east_xdir, "row", split_axis=0, concat_axis=1, tiled=True),
        lax.all_to_all(explicit, "row", split_axis=0, concat_axis=1, tiled=True),
    )
    solved = solve_whole(pieces[0], pieces[1], pieces[2], 1)
    delta_xdir = lax.all_to_all(solved, "row", split_axis=1, concat_axis=0, tiled=True)
    pieces = (
        lax.all_to_all(-west_ydir, "col", split_axis=0, concat_axis=2, tiled=True),
        lax.all_to_all(-east_ydir, "col", split_axis=0, concat_axis=2, tiled=True),
        lax.all_to_all(delta_xdir, "col", split_axis=0, concat_axis=2, tiled=True),
    )
    solved = solve_whole(pieces[0], pieces[1], pieces[2], 2)
    delta_ydir = lax.all_to_all(solved, "col", split_axis=2, concat_axis=0, tiled=True)
    return field + delta_ydir


def solution(mesh):
    in_specs = (P(None, "row", "col"), P(None, "row", "col"))
    out_specs = P(None, "row", "col")
    return jax.shard_map(
        on_device, mesh=mesh, in_specs=in_specs, out_specs=out_specs, check_vma=False
    )
```

profile of v0, /device:TPU:0, one launch (start us, length us, event | category | flops | bytes accessed | tf_op | source)
XLA Modules:
  0.0 184.1 jit_solution(7060141232085229688)
XLA Ops:
  1.3 3.5 %collective-permute-start.1 = (f32[2,64,1,128]{3,2,1,0:T(1,128)S(1)}, f32[2,64,1,128]{3,2,1,0:T(1,128)S(1)}, u32[]{:S(2)}, u32[]{:S(2)}) collective-permute-start(f32[2,64,1,128]{3,2,1,0:T(1,128)S(1)} %get-tuple-element.58), channel_id=1, source_target_pairs={{0,8},{8,16},{16,24},{24,32},{32,40},{40,48},{48,56},{56,64},{64,7... | collective-permute-start | bytes 196616 | tf_op jit(solution)/shard_map/ppermute | solution.py:17
  6.3 1.9 %fusion = (f32[2,64,16,1]{3,2,1,0:T(8,128)S(1)}, f32[2,64,16,1]{3,2,1,0:T(8,128)S(1)}) fusion(f32[1,64,16,128]{3,2,1,0:T(8,128)} %bitcast.72, f32[1,64,16,128]{3,2,1,0:T(8,128)} %bitcast.76), kind=kLoop, calls=%fused_computation.12 | loop fusion | flops 4096 | bytes 1064960 | tf_op jit(solution)/shard_map/stack | solution.py:80
  8.6 1.5 collective-permute-start
  12.4 3.2 %collective-permute-done.3 = f32[2,64,16,1]{1,2,3,0:T(8,128)S(1)} collective-permute-done((f32[2,64,16,1]{1,2,3,0:T(8,128)S(1)}, f32[2,64,16,1]{1,2,3,0:T(8,128)S(1)}, u32[]{:S(2)}, u32[]{:S(2)}) %collective-permute-start.3) | collective-permute-done | bytes 8224 | tf_op jit(solution)/shard_map/ppermute | solution.py:18
  16.2 1.8 %select_maximum_fusion = f32[2,64,18,130]{3,2,1,0:T(8,128)S(1)} fusion(f32[2,64,16,1]{3,2,1,0:T(8,128)S(1)} %copy.32, f32[2,64,16,1]{3,2,1,0:T(8,128)S(1)} %copy.30, f32[2,64,1,128]{3,2,1,0:T(1,128)S(1)} %collective-permute-done.2, f32[1,64,16,128]{3,2,1,0:T(8,128)S(1)} %bitcast.77, f32[1,64,16,128]{3,2,1,0:T(8,128)S(1)} %bitcast.73, ...), kind=kLoop, calls=%fused_computation | loop fusion | flops 2695680 | bytes 2394112 | tf_op jit(solution)/shard_map/concatenate | solution.py:24
  18.2 1.9 %fusion.16 = (f32[64,16,128]{2,1,0:T(8,128)S(1)}, f32[64,16,128]{2,1,0:T(8,128)S(1)}, f32[64,16,128]{2,1,0:T(8,128)S(1)}, f32[64,16,128]{2,1,0:T(8,128)}, f32[64,16,128]{2,1,0:T(8,128)}) fusion(f32[64,16,128]{2,1,0:T(8,128)S(1)} %copy-done.1, f32[64,18,130]{2,1,0:T(8,128)S(1)} %get-tuple-element.47, f32[64,16,128]{2,1,0:T(8,128)S(1)} %copy-done, ...), kind=kLoop, calls=%fused_computation.141 | loop fusion | flops 4325376 | bytes 7864320 | tf_op jit(solution)/shard_map/neg | solution.py:112
  20.2 17.1 %all_to_all.144 = f32[64,16,128]{2,1,0:T(8,128)S(1)} all-to-all(f32[64,16,128]{2,1,0:T(8,128)S(1)} %get-tuple-element.51), channel_id=1, replica_groups=mesh['row'=16,'col'=8] {'col'}, dimensions={0} | all-to-all | bytes 1048576 | tf_op jit(solution)/shard_map/all_to_all | solution.py:112
  37.2 12.8 %all_to_all.145 = f32[64,16,128]{2,1,0:T(8,128)S(1)} all-to-all(f32[64,16,128]{2,1,0:T(8,128)S(1)} %get-tuple-element.52), channel_id=1, replica_groups=mesh['row'=16,'col'=8] {'col'}, dimensions={0} | all-to-all | bytes 1048576 | tf_op jit(solution)/shard_map/all_to_all | solution.py:113
  50.0 19.1 %all_to_all.146 = f32[64,16,128]{2,1,0:T(8,128)S(1)} all-to-all(f32[64,16,128]{2,1,0:T(8,128)S(1)} %get-tuple-element.53), channel_id=1, replica_groups=mesh['row'=16,'col'=8] {'row'}, dimensions={0} | all-to-all | bytes 1048576 | tf_op jit(solution)/shard_map/all_to_all | solution.py:105
  69.1 3.6 %all-to-all-start.2 = ((f32[64,16,128]{2,1,0:T(8,128)}), f32[64,16,128]{2,1,0:T(8,128)S(1)}, u32[]{:S(2)}, u32[]{:S(2)}) async-start(f32[64,16,128]{2,1,0:T(8,128)} %get-tuple-element.54), calls=%async_computation.2 | async-start | bytes 1048576 | tf_op jit(solution)/shard_map/all_to_all | solution.py:106
  73.6 9.5 %all-to-all-done.2 = f32[64,16,128]{2,1,0:T(8,128)S(1)} async-done(((f32[64,16,128]{2,1,0:T(8,128)}), f32[64,16,128]{2,1,0:T(8,128)S(1)}, u32[]{:S(2)}, u32[]{:S(2)}) %all-to-all-start.2) | async-done | bytes 524320 | tf_op jit(solution)/shard_map/all_to_all | solution.py:106
  83.1 4.4 %all-to-all-start = ((f32[64,16,128]{2,1,0:T(8,128)}), f32[64,16,128]{2,1,0:T(8,128)}, u32[]{:S(2)}, u32[]{:S(2)}) async-start(f32[64,16,128]{2,1,0:T(8,128)} %get-tuple-element.55), calls=%async_computation | async-start | bytes 1048576 | tf_op jit(solution)/shard_map/all_to_all | solution.py:107
  90.8 6.7 %all-to-all-done = f32[64,16,128]{2,1,0:T(8,128)} async-done(((f32[64,16,128]{2,1,0:T(8,128)}), f32[64,16,128]{2,1,0:T(8,128)}, u32[]{:S(2)}, u32[]{:S(2)}) %all-to-all-start) | async-done | bytes 524320 | tf_op jit(solution)/shard_map/all_to_all | solution.py:107
  107.6 3.6 %all-to-all-start.3 = ((f32[4,256,128]{2,0,1:T(4,128)}), f32[4,256,128]{2,0,1:T(4,128)S(1)}, u32[]{:S(2)}, u32[]{:S(2)}) async-start(f32[4,256,128]{2,0,1:T(4,128)} %copy.36), calls=%async_computation.3 | async-start | bytes 1048576 | tf_op jit(solution)/shard_map/all_to_all | solution.py:110
  112.4 8.9 %all-to-all-done.3 = f32[4,256,128]{2,0,1:T(4,128)S(1)} async-done(((f32[4,256,128]{2,0,1:T(4,128)}), f32[4,256,128]{2,0,1:T(4,128)S(1)}, u32[]{:S(2)}, u32[]{:S(2)}) %all-to-all-start.3) | async-done | bytes 524320 | tf_op jit(solution)/shard_map/all_to_all | solution.py:110
  122.2 3.7 %all-to-all-start.4 = ((f32[64,16,128]{2,1,0:T(8,128)}), f32[64,16,128]{2,1,0:T(8,128)S(1)}, u32[]{:S(2)}, u32[]{:S(2)}) async-start(f32[64,16,128]{2,1,0:T(8,128)} %bitcast.15), calls=%async_computation.4 | async-start | bytes 1048576 | tf_op jit(solution)/shard_map/all_to_all | solution.py:114
  128.0 7.9 %all-to-all-done.4 = f32[64,16,128]{2,1,0:T(8,128)S(1)} async-done(((f32[64,16,128]{2,1,0:T(8,128)}), f32[64,16,128]{2,1,0:T(8,128)S(1)}, u32[]{:S(2)}, u32[]{:S(2)}) %all-to-all-start.4) | async-done | bytes 524320 | tf_op jit(solution)/shard_map/all_to_all | solution.py:114
  138.4 1.9 %multiply_add_fusion.16 = (f32[8,16,1024]{2,1,0:T(8,128)S(1)}, f32[8,16,1024]{2,1,0:T(8,128)S(1)}) fusion(f32[8,16,1023]{2,1,0:T(8,128)} %get-tuple-element.133, f32[8,16,1024]{2,1,0:T(8,128)S(1)} %subtract_subtract_fusion, f32[8,16,1023]{2,1,0:T(8,128)} %get-tuple-element.135, f32[8,16,1023]{2,1,0:T(8,128)} %get-tuple-element.141, ...), kind=kLoop, calls=%fused_computation.88 | loop fusion | flops 1572864 | bytes 6288384 | tf_op jit(solution)/shard_map/add | solution.py:56
  155.5 2.7 %copy.42 = f32[8,16,1024]{1,0,2:T(8,128)} copy(f32[8,16,1024]{2,1,0:T(8,128)S(1)} %add_divide_fusion) | data formatting | bytes 1048576 | tf_op jit(solution)/shard_map/div | solution.py:76
  158.2 3.7 %reshape = f32[8,1,16384]{2,1,0:T(1,128)S(1)} reshape(f32[1024,8,16]{2,1,0:T(8,128)} %bitcast.69) | data formatting | bytes 1048576
  161.9 12.8 %all_to_all.147 = f32[8,1,16384]{2,1,0:T(1,128)S(1)} all-to-all(f32[8,1,16384]{2,1,0:T(1,128)S(1)} %reshape), channel_id=1, replica_groups=mesh['row'=16,'col'=8] {'col'}, dimensions={0} | all-to-all | bytes 1048576 | tf_op jit(solution)/shard_map/all_to_all | solution.py:117
  175.2 1.9 %reduce = f32[8,16384]{1,0:T(8,128)S(1)} reduce(f32[8,1,16384]{2,1,0:T(1,128)S(1)} %all_to_all.147, f32[]{:T(128)} %broadcast.360), dimensions={1}, to_apply=%all_to_all.132.reduce_sub_computation | reduce | bytes 1048580 | tf_op jit(solution)/shard_map/all_to_all | solution.py:117
  177.1 3.4 %reshape.1 = f32[1024,8,16]{2,1,0:T(8,128)} reshape(f32[8,16384]{1,0:T(8,128)S(1)} %reduce) | data formatting | bytes 1048576
  180.5 2.8 %copy.44 = f32[8,8,16,128]{3,2,1,0:T(8,128)S(1)} copy(f32[8,8,16,128]{2,1,3,0:T(8,128)} %bitcast.70) | data formatting | bytes 1048576 | tf_op jit(solution)/shard_map/all_to_all | solution.py:117
  (151 shorter events, 43.0 us)
Async XLA Ops:
  1.3 14.9 %collective-permute-start.1 = (f32[2,64,1,128]{3,2,1,0:T(1,128)S(1)}, f32[2,64,1,128]{3,2,1,0:T(1,128)S(1)}, u32[]{:S(2)}, u32[]{:S(2)}) collective-permute-start(f32[2,64,1,128]{3,2,1,0:T(1,128)S(1)} %get-tuple-element.58), channel_id=1, source_target_pairs={{0,8},{8,16},{16,24},{24,32},{32,40},{40,48},{48,56},{56,64},{64,7... | collective-permute-start | bytes 196616 | tf_op jit(solution)/shard_map/ppermute | solution.py:17
  4.8 11.4 %copy-start = (f32[64,16,128]{2,1,0:T(8,128)S(1)}, f32[64,16,128]{2,1,0:T(8,128)}, u32[]{:S(2)}) copy-start(f32[64,16,128]{2,1,0:T(8,128)} %param.2) | copy-start | bytes 1572868
  4.8 11.4 %copy-start.1 = (f32[64,16,128]{2,1,0:T(8,128)S(1)}, f32[64,16,128]{2,1,0:T(8,128)}, u32[]{:S(2)}) copy-start(f32[64,16,128]{2,1,0:T(8,128)} %param.3) | copy-start | bytes 1572868
  4.8 11.3 %collective-permute-start.2 = (f32[2,64,1,128]{3,2,1,0:T(1,128)S(1)}, f32[2,64,1,128]{3,2,1,0:T(1,128)S(1)}, u32[]{:S(2)}, u32[]{:S(2)}) collective-permute-start(f32[2,64,1,128]{3,2,1,0:T(1,128)S(1)} %get-tuple-element.59), channel_id=1, source_target_pairs={{8,0},{16,8},{24,16},{32,24},{40,32},{48,40},{56,48},{64,56},{72,6... | collective-permute-start | bytes 196616 | tf_op jit(solution)/shard_map/ppermute | solution.py:18
  8.6 3.2 %collective-permute-start = (f32[2,64,16,1]{1,2,3,0:T(8,128)S(1)}, f32[2,64,16,1]{1,2,3,0:T(8,128)S(1)}, u32[]{:S(2)}, u32[]{:S(2)}) collective-permute-start(f32[2,64,16,1]{1,2,3,0:T(8,128)S(1)} %copy.29), channel_id=1, source_target_pairs={{0,1},{1,2},{2,3},{3,4},{4,5},{5,6},{6,7},{8,9},{9,10},{10,11},{11... | collective-permute-start | bytes 24584 | tf_op jit(solution)/shard_map/ppermute | solution.py:17
  10.5 5.0 %collective-permute-start.3 = (f32[2,64,16,1]{1,2,3,0:T(8,128)S(1)}, f32[2,64,16,1]{1,2,3,0:T(8,128)S(1)}, u32[]{:S(2)}, u32[]{:S(2)}) collective-permute-start(f32[2,64,16,1]{1,2,3,0:T(8,128)S(1)} %copy.31), channel_id=1, source_target_pairs={{1,0},{2,1},{3,2},{4,3},{5,4},{6,5},{7,6},{9,8},{10,9},{11,10},{12... | collective-permute-start | bytes 24584 | tf_op jit(solution)/shard_map/ppermute | solution.py:18
  69.1 13.9 %all-to-all-start.2 = ((f32[64,16,128]{2,1,0:T(8,128)}), f32[64,16,128]{2,1,0:T(8,128)S(1)}, u32[]{:S(2)}, u32[]{:S(2)}) async-start(f32[64,16,128]{2,1,0:T(8,128)} %get-tuple-element.54), calls=%async_computation.2 | async-start | bytes 1048576 | tf_op jit(solution)/shard_map/all_to_all | solution.py:106
  83.1 14.4 %all-to-all-start = ((f32[64,16,128]{2,1,0:T(8,128)}), f32[64,16,128]{2,1,0:T(8,128)}, u32[]{:S(2)}, u32[]{:S(2)}) async-start(f32[64,16,128]{2,1,0:T(8,128)} %get-tuple-element.55), calls=%async_computation | async-start | bytes 1048576 | tf_op jit(solution)/shard_map/all_to_all | solution.py:107
  97.5 1.3 copy-start.2
  97.5 1.4 copy-start.3
  97.5 1.5 copy-start.9
  97.5 1.7 copy-start.10
  99.6 1.0 copy-start.7
  99.6 1.2 copy-start.8
  107.6 13.7 %all-to-all-start.3 = ((f32[4,256,128]{2,0,1:T(4,128)}), f32[4,256,128]{2,0,1:T(4,128)S(1)}, u32[]{:S(2)}, u32[]{:S(2)}) async-start(f32[4,256,128]{2,0,1:T(4,128)} %copy.36), calls=%async_computation.3 | async-start | bytes 1048576 | tf_op jit(solution)/shard_map/all_to_all | solution.py:110
  122.2 13.7 %all-to-all-start.4 = ((f32[64,16,128]{2,1,0:T(8,128)}), f32[64,16,128]{2,1,0:T(8,128)S(1)}, u32[]{:S(2)}, u32[]{:S(2)}) async-start(f32[64,16,128]{2,1,0:T(8,128)} %bitcast.15), calls=%async_computation.4 | async-start | bytes 1048576 | tf_op jit(solution)/shard_map/all_to_all | solution.py:114
  140.3 1.0 copy-start.4
  140.3 1.2 copy-start.5
  140.3 1.3 copy-start.6
where the time goes:
time: 185 us; the launch traced here: 184 us
  blocking collectives  61.7 us (33%)
  local copies, waits for them, and re-layouts  37.8 us (20%)
  waiting for transfers between devices  36.3 us (20%)
  other arithmetic  24.6 us (13%)
  starting transfers between devices  22.9 us (12%)
    all_to_all x1, blocking collectives, on_device(): lax.all_to_all(-west_xdir, 'row', split_axis=0, concat_axis=1, tiled=True)  19.1 us
    all_to_all x1, blocking collectives, on_device(): lax.all_to_all(-west_ydir, 'col', split_axis=0, concat_axis=2, tiled=True)  17.1 us
    all_to_all x1, blocking collectives, on_device(): lax.all_to_all(solved, 'col', split_axis=2, concat_axis=0, tiled=True)  12.8 us
    all_to_all x1, blocking collectives, on_device(): lax.all_to_all(-east_ydir, 'col', split_axis=0, concat_axis=2, tiled=True)  12.8 us
    all_to_all x1, waiting for transfers between devices, on_device(): lax.all_to_all(-east_xdir, 'row', split_axis=0, concat_axis=1, tiled=True)  9.5 us
    unnamed x24, local copies, waits for them, and re-layouts  9.38 us
    all_to_all x1, waiting for transfers between devices, on_device(): lax.all_to_all(solved, 'row', split_axis=1, concat_axis=0, tiled=True)  8.9 us
    slice x36, local copies, waits for them, and re-layouts, shifted(): kept_part = lax.slice_in_dim(values, -stride, length, axis=line_axis)  7.94 us
  transfers between devices with their start and end apart: 8, of which 5 were waited for; matrix products, arithmetic and copies ran while one was open for 6% of the time, Pallas kernels for 0%

commit v1 on v0

v1 whole, which is shorter than its diff:
```python
import functools

import jax
import jax.numpy as jnp
from jax import lax
from jax.experimental import pallas as pl
from jax.experimental.pallas import tpu as pltpu
from jax.sharding import PartitionSpec as P

z_weight = 0.02
F32 = jnp.float32
VMEM = pl.BlockSpec(memory_space=pltpu.VMEM)
SMEM = pl.BlockSpec(memory_space=pltpu.SMEM)


def call(kernel, outs, args, flops, scratch=(), scalars=0):
    specs = [SMEM] * scalars + [VMEM] * (len(args) - scalars)
    return pl.pallas_call(
        kernel,
        out_shape=[jax.ShapeDtypeStruct(s, F32) for s in outs],
        in_specs=specs,
        out_specs=[VMEM] * len(outs),
        scratch_shapes=[pltpu.VMEM(s, F32) for s in scratch],
        cost_estimate=pl.CostEstimate(flops=flops, bytes_accessed=1 << 20, transcendentals=0),
    )(*args)


def turn(source, target, lines):
    blocks = source.shape[0] // lines
    for b in range(blocks):
        block = source[b * lines : (b + 1) * lines, :]
        target[pl.ds(b, lines, stride=blocks), :] = block.T


def edges_kernel(u, k, kt, low, high, ut):
    turn(k, kt, 128)
    turn(u, ut, 128)
    n = kt.shape[0]
    low[0:8, :] = kt[0:8, :]
    low[8:16, :] = ut[0:8, :]
    high[0:8, :] = kt[n - 8 : n, :]
    high[8:16, :] = ut[n - 8 : n, :]


def x_factor_kernel(nx, u, k, m, p, g0, gl, r):
    rows = u.shape[0]
    nz = rows // nx
    lane = lax.broadcasted_iota(jnp.int32, (nx, 128), 1)
    inner = lane < 127

    def at(ref, z):
        return ref[z * nx : (z + 1) * nx, :]

    uz, kz = at(u, 0), at(k, 0)
    below = (0.5 * z_weight) * kz * uz
    for z in range(nz):
        if z + 1 < nz:
            un, kn = at(u, z + 1), at(k, z + 1)
            above = (0.5 * z_weight) * (kz + kn) * (un - uz)
        else:
            un = kn = None
            above = -(0.5 * z_weight) * kz * uz
        flux = 0.5 * (kz + pltpu.roll(kz, 127, 1)) * (pltpu.roll(uz, 127, 1) - uz)
        flux = jnp.where(inner, flux, 0.0)
        r[z * nx : (z + 1) * nx, :] = uz + (above - below) + (flux - pltpu.roll(flux, 1, 1))
        uz, kz, below = un, kn, above

    def kx(i):
        return k[pl.ds(i, nz, stride=nx), :]

    s = jnp.ones((nz, 128), F32)
    w = s
    here = kx(0)
    for i in range(nx - 1):
        after = kx(i + 1)
        e = 0.5 * (here + after)
        inv = 1.0 / (s + e)
        mi = e * inv
        p[i] = inv
        m[i] = mi
        g0[i] = w * inv
        w = w * mi
        s = 1.0 + s * mi
        here = after
    inv = 1.0 / s
    p[nx - 1] = inv
    m[nx - 1] = jnp.zeros_like(inv)
    g = w * inv
    h = inv
    g0[nx - 1] = g
    gl[nx - 1] = h
    for i in range(nx - 2, -1, -1):
        mi = m[i]
        g = g0[i] + mi * g
        h = mi * h
        g0[i] = g
        gl[i] = h


def x_send_kernel(nx, col, low, high, from_left, from_right, r, k, g0, gl, send, rx, turned, full):
    rows = r.shape[0]
    nz = rows // nx
    first = col[0] == 0
    last = col[0] == col[1] - 1
    left = jnp.where(first, 0.0, from_left[...])
    right = jnp.where(last, 0.0, from_right[...])
    k_low, u_low = low[0:8, :], low[8:16, :]
    k_high, u_high = high[0:8, :], high[8:16, :]
    turned[0:8, :] = 0.5 * (k_low + left[0:8, :]) * (left[8:16, :] - u_low)
    turned[8:16, :] = 0.5 * (k_high + right[0:8, :]) * (right[8:16, :] - u_high)
    turned[16:128, :] = jnp.zeros((112, 128), F32)
    corr = turned[...].T
    lane = lax.broadcasted_iota(jnp.int32, (128, 128), 1)
    for b in range(rows // 128):
        west = jnp.where(lane == 0, corr[:, b : b + 1], 0.0)
        both = jnp.where(lane == 127, corr[:, 8 + b : 9 + b], west)
        full[b * 128 : (b + 1) * 128, :] = r[b * 128 : (b + 1) * 128, :] + both
    b0 = jnp.zeros((nz, 128), F32)
    bl = jnp.zeros((nz, 128), F32)
    for i in range(nx):
        ri = full[pl.ds(i, nz, stride=nx), :]
        rx[i] = ri
        b0 = b0 + g0[i] * ri
        bl = bl + gl[i] * ri
    k0 = k[pl.ds(0, nz, stride=nx), :]
    kl = k[pl.ds(nx - 1, nz, stride=nx), :]
    parts = [g0[0], g0[nx - 1], gl[nx - 1], b0, bl, k0, kl]
    peers = send.shape[0]
    own = nz // peers
    for q, part in enumerate(parts):
        for d in range(peers):
            send[d, q * own : (q + 1) * own, :] = part[d * own : (d + 1) * own, :]
    for d in range(peers):
        send[d, 7 * own : 8 * own, :] = jnp.zeros((own, 128), F32)


def x_inner_kernel(nx, rx, m, p, u, base, y):
    nz = rx.shape[1]
    v = rx[0]
    y[0] = v
    for i in range(1, nx):
        v = rx[i] + m[i - 1] * v
        y[i] = v
    b = v * p[nx - 1]
    base[nx - 1] = b - u[pl.ds(nx - 1, nz, stride=nx), :]
    for i in range(nx - 2, -1, -1):
        b = y[i] * p[i] + m[i] * b
        base[i] = b - u[pl.ds(i, nz, stride=nx), :]


def reduced(peers, take):
    zero = jnp.zeros_like(take(0)[0])
    nothing = (zero,) * 7
    before = nothing
    cp = zero
    y = zero
    cps, ys = [], []
    for i in range(peers + 1):
        after = take(i) if i < peers else nothing
        e = 0.5 * (before[6] + after[5])
        low = e * before[1]
        diag = 1.0 + e * (before[2] + after[0])
        inv = 1.0 / (diag - low * cp)
        y = (e * (after[3] - before[4]) + low * y) * inv
        cp = e * after[1] * inv
        cps.append(cp)
        ys.append(y)
        before = after
    q = ys[peers]
    out = [q]
    for i in range(peers - 1, -1, -1):
        q = ys[i] + cps[i] * q
        out.append(q)
    return out[::-1]


def x_reduced_kernel(recv, send):
    peers = recv.shape[0]
    own = recv.shape[1] // 8

    def take(d):
        return tuple(recv[d, q * own : (q + 1) * own, :] for q in range(7))

    flux = reduced(peers, take)
    for d in range(peers):
        send[d, 0:own, :] = flux[d]
        send[d, own : 2 * own, :] = flux[d + 1]


def y_factor_kernel(ny, kt, m, p, g0, gl):
    def row(ref, j):
        return ref[pl.ds(pl.multiple_of(j * 8, 8), 8), :]

    def put(ref, j, value):
        ref[pl.ds(pl.multiple_of(j * 8, 8), 8), :] = value

    one = jnp.ones((8, 128), F32)

    def forward(j, state):
        s, w, here = state
        after = row(kt, j + 1)
        e = 0.5 * (here + after)
        inv = 1.0 / (s + e)
        mi = e * inv
        put(p, j, inv)
        put(m, j, mi)
        put(g0, j, w * inv)
        return 1.0 + s * mi, w * mi, after

    s, w, unused = lax.fori_loop(0, ny - 1, forward, (one, one, row(kt, 0)))
    inv = 1.0 / s
    put(p, ny - 1, inv)
    put(m, ny - 1, jnp.zeros_like(inv))
    g = w * inv
    put(g0, ny - 1, g)
    put(gl, ny - 1, inv)

    def backward(i, state):
        g, h = state
        j = ny - 2 - i
        mi = row(m, j)
        g = row(g0, j) + mi * g
        h = mi * h
        put(g0, j, g)
        put(gl, j, h)
        return g, h

    lax.fori_loop(0, ny - 1, backward, (g, inv))


def y_send_kernel(nx, recv, base, g0x, glx, g0, gl, low, high, send, dt, ql, qr, dx):
    peers = recv.shape[0]
    own = recv.shape[1] // 2
    nz = peers * own
    for d in range(peers):
        ql[d * own : (d + 1) * own, :] = recv[d, 0:own, :]
        qr[d * own : (d + 1) * own, :] = recv[d, own : 2 * own, :]
    left, right = ql[...], qr[...]
    for i in range(nx):
        dx[pl.ds(i, nz, stride=nx), :] = base[i] + (glx[i] * right - g0x[i] * left)
    turn(dx, dt, 128)
    ny = dt.shape[0] // 8
    zero = jnp.zeros((8, 128), F32)
    b0, bl = [zero] * 4, [zero] * 4
    for j in range(ny):
        dj = dt[j * 8 : (j + 1) * 8, :]
        b0[j % 4] = b0[j % 4] + g0[j * 8 : (j + 1) * 8, :] * dj
        bl[j % 4] = bl[j % 4] + gl[j * 8 : (j + 1) * 8, :] * dj
    end = (ny - 1) * 8
    parts = [
        g0[0:8, :],
        g0[end : end + 8, :],
        gl[end : end + 8, :],
        (b0[0] + b0[1]) + (b0[2] + b0[3]),
        (bl[0] + bl[1]) + (bl[2] + bl[3]),
        low[0:8, :],
        high[0:8, :],
    ]
    for d in range(send.shape[0]):
        for q, part in enumerate(parts):
            send[d, q * 8 : (q + 1) * 8, :] = part


def y_inner_kernel(ny, dt, m, p, b, y):
    def row(ref, j):
        return ref[pl.ds(pl.multiple_of(j * 8, 8), 8), :]

    def put(ref, j, value):
        ref[pl.ds(pl.multiple_of(j * 8, 8), 8), :] = value

    put(y, 0, row(dt, 0))

    def forward(j, v):
        v = row(dt, j + 1) + row(m, j) * v
        put(y, j + 1, v)
        return v

    v = lax.fori_loop(0, ny - 1, forward, row(dt, 0), unroll=8)
    v = v * row(p, ny - 1)
    put(b, ny - 1, v)

    def backward(i, v):
        j = ny - 2 - i
        v = row(y, j) * row(p, j) + row(m, j) * v
        put(b, j, v)
        return v

    lax.fori_loop(0, ny - 1, backward, v, unroll=8)


def finish_kernel(col, recv, b, g0, gl, u, out, flux, whole):
    peers = recv.shape[0]

    def take(d):
        return tuple(recv[d, q * 8 : (q + 1) * 8, :] for q in range(7))

    q = reduced(peers, take)
    for i in range(peers + 1):
        flux[i] = q[i]
    left = flux[col[0]]
    right = flux[col[0] + 1]
    ny = b.shape[0] // 8
    for j in range(ny):
        sl = slice(j * 8, (j + 1) * 8)
        whole[sl, :] = b[sl, :] + (gl[sl, :] * right - g0[sl, :] * left)
    for i in range(8):
        rows = slice(i * 128, (i + 1) * 128)
        out[rows, :] = u[rows, :] + whole[pl.ds(i, 128, stride=8), :].T


def on_device(field, conductivity):
    nz, nx, ny = field.shape
    rows = nz * nx
    rowp, colp = lax.axis_size("row"), lax.axis_size("col")
    own = nz // rowp
    u = field.reshape(rows, ny)
    k = conductivity.reshape(rows, ny)
    col = jnp.stack([lax.axis_index("col"), jnp.int32(colp)]).astype(jnp.int32)
    flat, cube = (rows, ny), (nx, nz, ny)
    kt, low, high = call(edges_kernel, [flat, (16, 128), (16, 128)], (u, k), 1 << 20, [flat])
    up = [(i, (i + 1) % colp) for i in range(colp)]
    from_left = lax.ppermute(high, "col", up)
    from_right = lax.ppermute(low, "col", [(b, a) for a, b in up])
    m, p, g0, gl, r = call(
        functools.partial(x_factor_kernel, nx), [cube] * 4 + [flat], (u, k), 1 << 23
    )
    send, rx = call(
        functools.partial(x_send_kernel, nx),
        [(rowp, 8 * own, ny), cube],
        (col, low, high, from_left, from_right, r, k, g0, gl),
        1 << 22,
        [(128, 128), flat],
        1,
    )
    recv = lax.all_to_all(send, "row", 0, 0, tiled=True)
    (base,) = call(functools.partial(x_inner_kernel, nx), [cube], (rx, m, p, u), 1 << 22, [cube])
    my, py, g0y, gly = call(functools.partial(y_factor_kernel, ny), [flat] * 4, (kt,), 1 << 23)
    (back,) = call(x_reduced_kernel, [(rowp, 2 * own, ny)], (recv,), 1 << 21)
    recv = lax.all_to_all(back, "row", 0, 0, tiled=True)
    send, dt = call(
        functools.partial(y_send_kernel, nx),
        [(colp, 56, 128), flat],
        (recv, base, g0, gl, g0y, gly, low, high),
        1 << 22,
        [(nz, ny), (nz, ny), flat],
    )
    recv = lax.all_to_all(send, "col", 0, 0, tiled=True)
    (b,) = call(functools.partial(y_inner_kernel, ny), [flat], (dt, my, py), 1 << 22, [flat])
    (out,) = call(
        finish_kernel, [flat], (col, recv, b, g0y, gly, u), 1 << 22, [(colp + 1, 8, 128), flat], 1
    )
    return out.reshape(nz, nx, ny)


def solution(mesh):
    in_specs = (P(None, "row", "col"), P(None, "row", "col"))
    out_specs = P(None, "row", "col")
    return jax.shard_map(
        on_device, mesh=mesh, in_specs=in_specs, out_specs=out_specs, check_vma=False
    )
```

time: 185 us -> 63.5 us (0.34)
  blocking collectives: 61.7 us -> 15.8 us
  local copies, waits for them, and re-layouts: 37.8 us -> 1.9 us
  waiting for transfers between devices: 36.3 us -> 4.68 us
  Pallas kernels: 0 us -> 28.9 us
  other arithmetic: 24.6 us -> 0.55 us
  starting transfers between devices: 22.9 us -> 10.7 us
    all_to_all x4 -> x1, blocking collectives: 61.7 us -> 15.8 us  [on_device(): recv = lax.all_to_all(send, 'row', 0, 0, tiled=True)]
    pallas_call x0 -> x9, Pallas kernels: none -> 28.9 us  [call(): pl.pallas_call(kernel, out_shape=[jax.ShapeDtypeStruct(s, F32) for s in o...]
    all_to_all x4 -> x2, waiting for transfers between devices: 33 us -> 4.67 us  [the longest x1 4.35 us: on_device(): recv = lax.all_to_all(send, 'col', 0, 0, tiled=True)]
    slice x73 -> x0, local copies, waits for them, and re-layouts: 14.8 us -> none  [the longest x36 7.94 us: shifted(): kept_part = lax.slice_in_dim(values, -stride, length, axis=line_axis)]
    add x29 -> x0, other arithmetic: 14.4 us -> none  [the longest x14 7.51 us: reduce_lines(): column + left_factor * shifted(column, line_axis, stride, 0.0)]
    all_to_all x13 -> x0, local copies, waits for them, and re-layouts: 8.48 us -> none  [the longest x2 3.3 us: on_device(): lax.all_to_all(solved, 'col', split_axis=2, concat_axis=0, tiled=True)]
    all_to_all x4 -> x2, starting transfers between devices: 15.3 us -> 7.07 us  [the longest x1 3.58 us: on_device(): recv = lax.all_to_all(send, 'col', 0, 0, tiled=True)]
    unnamed x24 -> x8, local copies, waits for them, and re-layouts: 9.38 us -> 1.9 us
  transfers between devices with their start and end apart: 8 -> 4, of which waited for: 5 -> 2; matrix products, arithmetic and copies ran while one was open for 6% -> 1% of each run, Pallas kernels for 0% -> 26%
where the time goes in v1:
time: 63.5 us; the launch traced here: 62.5 us
  Pallas kernels  28.9 us (46%)
  blocking collectives  15.8 us (25%)
  starting transfers between devices  10.7 us (17%)
  waiting for transfers between devices  4.68 us (7%)
  local copies, waits for them, and re-layouts  1.9 us (3%)
    pallas_call x9, Pallas kernels, call(): pl.pallas_call(kernel, out_shape=[jax.ShapeDtypeStruct(s, F32) for s in o...  28.9 us
    all_to_all x1, blocking collectives, on_device(): recv = lax.all_to_all(send, 'row', 0, 0, tiled=True)  15.8 us
    all_to_all x1, waiting for transfers between devices, on_device(): recv = lax.all_to_all(send, 'col', 0, 0, tiled=True)  4.35 us
    ppermute x1, starting transfers between devices, on_device(): from_right = lax.ppermute(low, 'col', [(b, a) for a, b in up])  3.59 us
    all_to_all x1, starting transfers between devices, on_device(): recv = lax.all_to_all(send, 'col', 0, 0, tiled=True)  3.58 us
    all_to_all x1, starting transfers between devices, on_device(): recv = lax.all_to_all(back, 'row', 0, 0, tiled=True)  3.49 us
    unnamed x8, local copies, waits for them, and re-layouts  1.9 us
  transfers between devices with their start and end apart: 4, of which 2 were waited for; matrix products, arithmetic and copies ran while one was open for 1% of the time, Pallas kernels for 26%

profile of v1, /device:TPU:0, one launch (start us, length us, event | category | flops | bytes accessed | tf_op | source)
XLA Modules:
  0.0 62.5 jit_solution(15199244400019192214)
XLA Ops:
  0.0 2.2 %shard_map.28 = (f32[1024,128]{1,0:T(8,128)}, f32[16,128]{1,0:T(8,128)}, f32[16,128]{1,0:T(8,128)}) custom-call(f32[1024,128]{1,0:T(8,128)} %bitcast.4, f32[1024,128]{1,0:T(8,128)} %bitcast.8), custom_call_target="tpu_custom_call" | custom-call | flops 1048576 | bytes 1048576 | tf_op jit(solution)/shard_map/pallas_call | solution.py:18
  2.2 0.0 collective-permute-start
  2.2 3.6 %collective-permute-start.1 = (f32[16,128]{1,0:T(8,128)}, f32[16,128]{1,0:T(8,128)S(1)}, u32[]{:S(2)}, u32[]{:S(2)}) collective-permute-start(f32[16,128]{1,0:T(8,128)} %get-tuple-element.21.low), channel_id=1, source_target_pairs={{1,0},{2,1},{3,2},{4,3},{5,4},{6,5},{7,6},{0,7},{9,8},{10,9},{11,1... | collective-permute-start | bytes 24584 | tf_op jit(solution)/shard_map/ppermute | solution.py:323
  5.8 0.6 pad_add_fusion.col
  6.3 6.0 %shard_map.29 = (f32[16,64,128]{2,1,0:T(8,128)}, f32[16,64,128]{2,1,0:T(8,128)}, f32[16,64,128]{2,1,0:T(8,128)}, f32[16,64,128]{2,1,0:T(8,128)}, f32[1024,128]{1,0:T(8,128)}) custom-call(f32[1024,128]{1,0:T(8,128)} %bitcast.5, f32[1024,128]{1,0:T(8,128)} %bitcast.9), custom_call_target="tpu_custom_call" | custom-call | flops 8388608 | bytes 1048576 | tf_op jit(solution)/shard_map/pallas_call | solution.py:18
  12.4 0.0 collective-permute-done.from_left
  12.4 0.0 collective-permute-done.1.from_right
  12.4 0.0 copy-start.3
  12.4 0.6 copy-done.2
  13.0 0.0 copy-done.3
  13.0 3.1 %shard_map.30 = (f32[16,32,128]{2,1,0:T(8,128)}, f32[16,64,128]{2,1,0:T(8,128)}) custom-call(s32[2]{0:T(128)} %pad_add_fusion.col, f32[16,128]{1,0:T(8,128)} %get-tuple-element.21.low, f32[16,128]{1,0:T(8,128)} %get-tuple-element.22.high, f32[16,128]{1,0:T(8,128)} %copy-done.2, f32[16,128]{1,0:T(8,128)} %copy-done.3, f32[1024,128]{1,0:T(8,128)} %get-tuple-element.23.r, ...), custom_call_target="tpu_custom_call" | custom-call | flops 4194304 | bytes 1048576 | tf_op jit(solution)/shard_map/pallas_call | solution.py:18
  16.1 15.8 %all_to_all.15.recv = f32[16,32,128]{2,1,0:T(8,128)} all-to-all(f32[16,32,128]{2,1,0:T(8,128)} %get-tuple-element.26), channel_id=1, replica_groups=mesh['row'=16,'col'=8] {'row'}, dimensions={0} | all-to-all | bytes 524288 | tf_op jit(solution)/shard_map/all_to_all | solution.py:335
  31.9 1.8 %shard_map.31 = f32[16,8,128]{2,1,0:T(8,128)} custom-call(f32[16,32,128]{2,1,0:T(8,128)} %all_to_all.15.recv), custom_call_target="tpu_custom_call" | custom-call | flops 2097152 | bytes 1048576 | tf_op jit(solution)/shard_map/pallas_call | solution.py:18
  33.7 3.5 %all-to-all-start.1 = ((f32[16,8,128]{2,1,0:T(8,128)}), f32[16,8,128]{2,1,0:T(8,128)S(1)}, u32[]{:S(2)}, u32[]{:S(2)}) async-start(f32[16,8,128]{2,1,0:T(8,128)} %shard_map.31), calls=%async_computation.1 | async-start | bytes 131072 | tf_op jit(solution)/shard_map/all_to_all | solution.py:339
  37.2 4.7 %shard_map.33 = (f32[1024,128]{1,0:T(8,128)}, f32[1024,128]{1,0:T(8,128)}, f32[1024,128]{1,0:T(8,128)}, f32[1024,128]{1,0:T(8,128)}) custom-call(f32[1024,128]{1,0:T(8,128)} %get-tuple-element.30.kt), custom_call_target="tpu_custom_call" | custom-call | flops 8388608 | bytes 1048576 | tf_op jit(solution)/shard_map/pallas_call | solution.py:18
  41.9 2.6 %shard_map.32.base = f32[16,64,128]{2,1,0:T(8,128)} custom-call(f32[16,64,128]{2,1,0:T(8,128)} %get-tuple-element.27.rx, f32[16,64,128]{2,1,0:T(8,128)} %get-tuple-element.28.m, f32[16,64,128]{2,1,0:T(8,128)} %get-tuple-element.29.p, f32[1024,128]{1,0:T(8,128)} %bitcast.6), custom_call_target="tpu_custom_call" | custom-call | flops 4194304 | bytes 1048576 | tf_op jit(solution)/shard_map/pallas_call | solution.py:18
  44.5 0.3 all-to-all-done.1.recv
  44.8 0.6 copy-done.1
  45.4 2.9 %shard_map.34 = (f32[8,56,128]{2,1,0:T(8,128)}, f32[1024,128]{1,0:T(8,128)}) custom-call(f32[16,8,128]{2,1,0:T(8,128)} %copy-done.1, f32[16,64,128]{2,1,0:T(8,128)} %shard_map.32.base, f32[16,64,128]{2,1,0:T(8,128)} %get-tuple-element.24.g0.g0x, f32[16,64,128]{2,1,0:T(8,128)} %get-tuple-element.25.gl.glx, f32[1024,128]{1,0:T(8,128)} %get-tuple-element.31.g0, ...), custom_call_target="tpu_custom_call" | custom-call | flops 4194304 | bytes 1048576 | tf_op jit(solution)/shard_map/pallas_call | solution.py:18
  48.4 3.6 %all-to-all-start.2 = ((f32[8,56,128]{2,1,0:T(8,128)}), f32[8,56,128]{2,1,0:T(8,128)S(1)}, u32[]{:S(2)}, u32[]{:S(2)}) async-start(f32[8,56,128]{2,1,0:T(8,128)} %get-tuple-element.33), calls=%async_computation.2 | async-start | bytes 458752 | tf_op jit(solution)/shard_map/all_to_all | solution.py:347
  51.9 2.8 %shard_map.35.b = f32[1024,128]{1,0:T(8,128)} custom-call(f32[1024,128]{1,0:T(8,128)} %get-tuple-element.34.dt, f32[1024,128]{1,0:T(8,128)} %get-tuple-element.35.m, f32[1024,128]{1,0:T(8,128)} %get-tuple-element.36.p), custom_call_target="tpu_custom_call" | custom-call | flops 4194304 | bytes 1048576 | tf_op jit(solution)/shard_map/pallas_call | solution.py:18
  54.7 4.3 %all-to-all-done.2.recv = f32[8,56,128]{2,1,0:T(8,128)S(1)} async-done(((f32[8,56,128]{2,1,0:T(8,128)}), f32[8,56,128]{2,1,0:T(8,128)S(1)}, u32[]{:S(2)}, u32[]{:S(2)}) %all-to-all-start.2) | async-done | bytes 229408 | tf_op jit(solution)/shard_map/all_to_all | solution.py:347
  59.1 0.7 %copy-done = f32[8,56,128]{2,1,0:T(8,128)} copy-done((f32[8,56,128]{2,1,0:T(8,128)}, f32[8,56,128]{2,1,0:T(8,128)S(1)}, u32[]{:S(2)}) %copy-start) | copy-done | bytes 229400
  59.8 2.8 %shard_map.36 = f32[1024,128]{1,0:T(8,128)} custom-call(s32[2]{0:T(128)} %pad_add_fusion.col, f32[8,56,128]{2,1,0:T(8,128)} %copy-done, f32[1024,128]{1,0:T(8,128)} %shard_map.35.b, f32[1024,128]{1,0:T(8,128)} %get-tuple-element.31.g0, f32[1024,128]{1,0:T(8,128)} %get-tuple-element.32.gl, f32[1024,128]{1,0:T(8,128)} %bitcast.7), custom_call_target="tpu_custom_call" | custom-call | flops 4194304 | bytes 1048576 | tf_op jit(solution)/shard_map/pallas_call | solution.py:18
  (3 shorter events, 0.0 us)
Async XLA Ops:
  2.2 10.2 %collective-permute-start = (f32[16,128]{1,0:T(8,128)}, f32[16,128]{1,0:T(8,128)S(1)}, u32[]{:S(2)}, u32[]{:S(2)}) collective-permute-start(f32[16,128]{1,0:T(8,128)} %get-tuple-element.22.high), channel_id=1, source_target_pairs={{0,1},{1,2},{2,3},{3,4},{4,5},{5,6},{6,7},{7,0},{8,9},{9,10},{10,1... | collective-permute-start | bytes 24584 | tf_op jit(solution)/shard_map/ppermute | solution.py:322
  2.2 10.2 %collective-permute-start.1 = (f32[16,128]{1,0:T(8,128)}, f32[16,128]{1,0:T(8,128)S(1)}, u32[]{:S(2)}, u32[]{:S(2)}) collective-permute-start(f32[16,128]{1,0:T(8,128)} %get-tuple-element.21.low), channel_id=1, source_target_pairs={{1,0},{2,1},{3,2},{4,3},{5,4},{6,5},{7,6},{0,7},{9,8},{10,9},{11,1... | collective-permute-start | bytes 24584 | tf_op jit(solution)/shard_map/ppermute | solution.py:323
  12.4 0.6 copy-start.2
  12.4 0.6 copy-start.3
  33.7 11.1 %all-to-all-start.1 = ((f32[16,8,128]{2,1,0:T(8,128)}), f32[16,8,128]{2,1,0:T(8,128)S(1)}, u32[]{:S(2)}, u32[]{:S(2)}) async-start(f32[16,8,128]{2,1,0:T(8,128)} %shard_map.31), calls=%async_computation.1 | async-start | bytes 131072 | tf_op jit(solution)/shard_map/all_to_all | solution.py:339
  44.8 0.6 copy-start.1
  48.4 10.7 %all-to-all-start.2 = ((f32[8,56,128]{2,1,0:T(8,128)}), f32[8,56,128]{2,1,0:T(8,128)S(1)}, u32[]{:S(2)}, u32[]{:S(2)}) async-start(f32[8,56,128]{2,1,0:T(8,128)} %get-tuple-element.33), calls=%async_computation.2 | async-start | bytes 458752 | tf_op jit(solution)/shard_map/all_to_all | solution.py:347
  59.1 0.7 %copy-start = (f32[8,56,128]{2,1,0:T(8,128)}, f32[8,56,128]{2,1,0:T(8,128)S(1)}, u32[]{:S(2)}) copy-start(f32[8,56,128]{2,1,0:T(8,128)S(1)} %all-to-all-done.2.recv) | copy-start | bytes 688132

commit v2 on v1

v2 whole, which is shorter than its diff:
```python
import functools

import jax
import jax.numpy as jnp
from jax import lax
from jax.experimental import pallas as pl
from jax.experimental.pallas import tpu as pltpu
from jax.sharding import PartitionSpec as P

z_weight = 0.02
F32 = jnp.float32
VMEM = pl.BlockSpec(memory_space=pltpu.VMEM)
HBM = pl.BlockSpec(memory_space=pltpu.HBM)
CHUNKS = 4


def call(kernel, outs, args, flops, scratch=(), specs=None):
    return pl.pallas_call(
        kernel,
        out_shape=[jax.ShapeDtypeStruct(s, F32) for s in outs],
        in_specs=specs or [VMEM] * len(args),
        out_specs=[VMEM] * len(outs),
        scratch_shapes=[pltpu.VMEM(s, F32) if isinstance(s, tuple) else s for s in scratch],
        compiler_params=pltpu.CompilerParams(vmem_limit_bytes=12 << 20),
        cost_estimate=pl.CostEstimate(flops=flops, bytes_accessed=1 << 20, transcendentals=0),
    )(*args)


def row(ref, j):
    start = j * 8 if isinstance(j, int) else pl.multiple_of(j * 8, 8)
    return ref[pl.ds(start, 8), :]


def put(ref, j, value):
    start = j * 8 if isinstance(j, int) else pl.multiple_of(j * 8, 8)
    ref[pl.ds(start, 8), :] = value


def turn(source, target, b):
    target[pl.ds(b, 128, stride=8), :] = source[b * 128 : (b + 1) * 128, :].T


def turn_back(source, b):
    return source[pl.ds(b, 128, stride=8), :].T


def load_kernel(u_hbm, k_hbm, u, k, ut, kt, low, high, sems):
    rows = u.shape[0] // CHUNKS
    copies = []
    for c in range(CHUNKS):
        part = pl.ds(c * rows, rows)
        for a, (src, dst) in enumerate(((k_hbm, k), (u_hbm, u))):
            copy = pltpu.make_async_copy(src.at[part], dst.at[part], sems.at[2 * c + a])
            copy.start()
            copies.append(copy)
    for c in range(CHUNKS):
        for a, (src, dst) in enumerate(((k, kt), (u, ut))):
            copies[2 * c + a].wait()
            for b in range(c * rows // 128, (c + 1) * rows // 128):
                turn(src, dst, b)
    n = kt.shape[0] // 8
    low[0:8, :] = row(kt, 0)
    low[8:16, :] = row(ut, 0)
    high[0:8, :] = row(kt, n - 1)
    high[8:16, :] = row(ut, n - 1)


def pivots_kernel(nx, u, k, ut, kt, mx, px, r, ends, my, py, lt):
    rows = u.shape[0]
    nz = rows // nx
    ny = lt.shape[0] // 8
    half = ny // 2

    def both(i, state):
        s, t, k_left, k_right = state
        j = ny - 1 - i
        next_left, next_right = row(kt, i + 1), row(kt, j - 1)
        e = 0.5 * (k_left + next_left)
        f = 0.5 * (k_right + next_right)
        inv_e = 1.0 / (s + e)
        inv_f = 1.0 / (t + f)
        m_left, m_right = e * inv_e, f * inv_f
        put(py, i, inv_e)
        put(py, j, inv_f)
        put(my, i, m_left)
        put(my, j, m_right)
        return 1.0 + s * m_left, 1.0 + t * m_right, next_left, next_right

    one = jnp.ones((8, 128), F32)
    s, t, k_left, k_right = lax.fori_loop(
        0, half - 1, both, (one, one, row(kt, 0), row(kt, ny - 1)), unroll=7
    )
    e = 0.5 * (k_left + k_right)
    inv = 1.0 / (s * t + e * (s + t))
    put(py, half - 1, (t + e) * inv)
    put(py, half, (s + e) * inv)
    put(my, half - 1, e * inv)
    put(my, half, e * inv)

    here_k, here_u = row(kt, 0), row(ut, 0)
    before = None
    for j in range(ny):
        if j + 1 < ny:
            next_k, next_u = row(kt, j + 1), row(ut, j + 1)
            flux = 0.5 * (here_k + next_k) * (next_u - here_u)
            put(lt, j, flux if before is None else flux - before)
            before, here_k, here_u = flux, next_k, next_u
        else:
            put(lt, j, -before)

    def at(ref, z):
        return ref[z * nx : (z + 1) * nx, :]

    uz, kz = at(u, 0), at(k, 0)
    below = (0.5 * z_weight) * kz * uz
    side = None
    for z in range(nz):
        if z * nx % 128 == 0:
            side = turn_back(lt, z * nx // 128)
        if z + 1 < nz:
            un, kn = at(u, z + 1), at(k, z + 1)
            above = (0.5 * z_weight) * (kz + kn) * (un - uz)
        else:
            un = kn = None
            above = -(0.5 * z_weight) * kz * uz
        part = z * nx % 128
        r[z * nx : (z + 1) * nx, :] = uz + (above - below) + side[part : part + nx, :]
        uz, kz, below = un, kn, above

    def kx(i):
        return k[pl.ds(i, nz, stride=nx), :]

    s = jnp.ones((nz, 128), F32)
    here = kx(0)
    ends[0] = here
    for i in range(nx - 1):
        after = kx(i + 1)
        e = 0.5 * (here + after)
        inv = 1.0 / (s + e)
        m = e * inv
        px[i] = inv
        mx[i] = m
        s = 1.0 + s * m
        here = after
    px[nx - 1] = 1.0 / s
    ends[1] = here


def x_send_kernel(nx, peers_y, low, high, from_left, from_right, r, ends, m, p, send, b, g0, gl, turned, full):
    rows = r.shape[0]
    nz = rows // nx
    col = lax.axis_index("col")
    left = jnp.where(col == 0, 0.0, from_left[...])
    right = jnp.where(col == peers_y - 1, 0.0, from_right[...])
    k_low, u_low = low[0:8, :], low[8:16, :]
    k_high, u_high = high[0:8, :], high[8:16, :]
    turned[0:8, :] = 0.5 * (k_low + left[0:8, :]) * (left[8:16, :] - u_low)
    turned[8:16, :] = 0.5 * (k_high + right[0:8, :]) * (right[8:16, :] - u_high)
    turned[16:128, :] = jnp.zeros((112, 128), F32)
    corr = turned[...].T
    lane = lax.broadcasted_iota(jnp.int32, (128, 128), 1)
    for i in range(rows // 128):
        west = jnp.where(lane == 0, corr[:, i : i + 1], 0.0)
        both = jnp.where(lane == 127, corr[:, 8 + i : 9 + i], west)
        full[i * 128 : (i + 1) * 128, :] = r[i * 128 : (i + 1) * 128, :] + both
    y = full[pl.ds(0, nz, stride=nx), :]
    w = jnp.ones((nz, 128), F32)
    for i in range(nx - 1):
        mi, pi = m[i], p[i]
        b[i] = y * pi
        g0[i] = w * pi
        y = full[pl.ds(i + 1, nz, stride=nx), :] + mi * y
        w = w * mi
    h = p[nx - 1]
    v = y * h
    g = w * h
    b[nx - 1] = v
    g0[nx - 1] = g
    gl[nx - 1] = h
    parts = [None, g, h, None, v, ends[0], ends[1]]
    for i in range(nx - 2, -1, -1):
        mi = m[i]
        v = b[i] + mi * v
        g = g0[i] + mi * g
        h = mi * h
        b[i] = v
        g0[i] = g
        gl[i] = h
    parts[0] = g
    parts[3] = v
    peers = send.shape[0]
    own = nz // peers
    for q, part in enumerate(parts):
        for d in range(peers):
            send[d, q * own : (q + 1) * own, :] = part[d * own : (d + 1) * own, :]
    for d in range(peers):
        send[d, 7 * own : 8 * own, :] = jnp.zeros((own, 128), F32)


def reduced(peers, take):
    zero = jnp.zeros_like(take(0)[0])
    nothing = (zero,) * 7
    before = nothing
    cp = zero
    y = zero
    cps, ys = [], []
    for i in range(peers + 1):
        after = take(i) if i < peers else nothing
        e = 0.5 * (before[6] + after[5])
        low = e * before[1]
        diag = 1.0 + e * (before[2] + after[0])
        inv = 1.0 / (diag - low * cp)
        y = (e * (after[3] - before[4]) + low * y) * inv
        cp = e * after[1] * inv
        cps.append(cp)
        ys.append(y)
        before = after
    q = ys[peers]
    out = [q]
    for i in range(peers - 1, -1, -1):
        q = ys[i] + cps[i] * q
        out.append(q)
    return out[::-1]


def x_reduced_kernel(recv, send):
    peers = recv.shape[0]
    own = recv.shape[1] // 8

    def take(d):
        return tuple(recv[d, q * own : (q + 1) * own, :] for q in range(7))

    flux = reduced(peers, take)
    for d in range(peers):
        send[d, 0:own, :] = flux[d]
        send[d, own : 2 * own, :] = flux[d + 1]


def y_send_kernel(nx, recv, bx, g0x, glx, u, m, p, low, high, send, b, g0, gl, dt, ql, qr, dx):
    peers = recv.shape[0]
    own = recv.shape[1] // 2
    nz = peers * own
    ny = dt.shape[0] // 8
    half = ny // 2
    for d in range(peers):
        ql[d * own : (d + 1) * own, :] = recv[d, 0:own, :]
        qr[d * own : (d + 1) * own, :] = recv[d, own : 2 * own, :]
    left, right = ql[...], qr[...]
    for i in range(nx):
        part = pl.ds(i, nz, stride=nx)
        dx[part, :] = (bx[i] - u[part, :]) + (glx[i] * right - g0x[i] * left)
    for i in range(8):
        turn(dx, dt, i)

    def forward(i, state):
        y, w, z, x = state
        j = ny - 1 - i
        m_left, p_left = row(m, i), row(p, i)
        m_right, p_right = row(m, j), row(p, j)
        put(b, i, y * p_left)
        put(g0, i, w * p_left)
        put(b, j, z * p_right)
        put(gl, j, x * p_right)
        return (
            row(dt, i + 1) + m_left * y,
            w * m_left,
            row(dt, j - 1) + m_right * z,
            x * m_right,
        )

    one = jnp.ones((8, 128), F32)
    y, w, z, x = lax.fori_loop(
        0, half - 1, forward, (row(dt, 0), one, row(dt, ny - 1), one), unroll=7
    )
    c_left, c_right, c_mid = row(p, half - 1), row(p, half), row(m, half)
    state = (
        c_left * y + c_mid * z,
        c_left * w,
        c_mid * x,
        c_right * z + c_mid * y,
        c_mid * w,
        c_right * x,
    )

    def save(i, j, state):
        put(b, i, state[0])
        put(g0, i, state[1])
        put(gl, i, state[2])
        put(b, j, state[3])
        put(g0, j, state[4])
        put(gl, j, state[5])

    save(half - 1, half, state)

    def backward(n, state):
        i = half - 2 - n
        j = ny - 1 - i
        m_left, m_right = row(m, i), row(m, j)
        state = (
            row(b, i) + m_left * state[0],
            row(g0, i) + m_left * state[1],
            m_left * state[2],
            row(b, j) + m_right * state[3],
            m_right * state[4],
            row(gl, j) + m_right * state[5],
        )
        save(i, j, state)
        return state

    state = lax.fori_loop(0, half - 1, backward, state, unroll=7)
    parts = [state[1], state[4], state[5], state[0], state[3], low[0:8, :], high[0:8, :]]
    for d in range(send.shape[0]):
        for q, part in enumerate(parts):
            send[d, q * 8 : (q + 1) * 8, :] = part


def finish_kernel(recv, b, g0, gl, u, out, flux, whole):
    peers = recv.shape[0]

    def take(d):
        return tuple(recv[d, q * 8 : (q + 1) * 8, :] for q in range(7))

    q = reduced(peers, take)
    for i in range(peers + 1):
        flux[i] = q[i]
    col = lax.axis_index("col")
    left = flux[col]
    right = flux[col + 1]
    for j in range(b.shape[0] // 8):
        put(whole, j, row(b, j) + (row(gl, j) * right - row(g0, j) * left))
    for i in range(8):
        rows = slice(i * 128, (i + 1) * 128)
        out[rows, :] = u[rows, :] + turn_back(whole, i)


def on_device(field, conductivity):
    nz, nx, ny = field.shape
    rows = nz * nx
    rowp, colp = lax.axis_size("row"), lax.axis_size("col")
    own = nz // rowp
    u = field.reshape(rows, ny)
    k = conductivity.reshape(rows, ny)
    flat, cube = (rows, ny), (nx, nz, ny)
    uv, kv, ut, kt, low, high = call(
        load_kernel,
        [flat] * 4 + [(16, 128)] * 2,
        tuple(pltpu.with_memory_space_constraint(a, pltpu.HBM) for a in (u, k)),
        1 << 20,
        [pltpu.SemaphoreType.DMA((2 * CHUNKS,))],
        [HBM, HBM],
    )
    up = [(i, (i + 1) % colp) for i in range(colp)]
    from_left = lax.ppermute(high, "col", up)
    from_right = lax.ppermute(low, "col", [(b, a) for a, b in up])
    mx, px, r, ends, my, py = call(
        functools.partial(pivots_kernel, nx),
        [cube] * 2 + [flat, (2, nz, ny)] + [flat] * 2,
        (uv, kv, ut, kt),
        1 << 23,
        [flat],
    )
    send, bx, g0x, glx = call(
        functools.partial(x_send_kernel, nx, colp),
        [(rowp, 8 * own, ny)] + [cube] * 3,
        (low, high, from_left, from_right, r, ends, mx, px),
        1 << 22,
        [(128, 128), flat],
    )
    recv = lax.all_to_all(send, "row", 0, 0, tiled=True)
    (back,) = call(x_reduced_kernel, [(rowp, 2 * own, ny)], (recv,), 1 << 21)
    recv = lax.all_to_all(back, "row", 0, 0, tiled=True)
    send, b, g0y, gly = call(
        functools.partial(y_send_kernel, nx),
        [(colp, 56, 128)] + [flat] * 3,
        (recv, bx, g0x, glx, u, my, py, low, high),
        1 << 22,
        [flat, (nz, ny), (nz, ny), flat],
    )
    recv = lax.all_to_all(send, "col", 0, 0, tiled=True)
    (out,) = call(
        finish_kernel, [flat], (recv, b, g0y, gly, u), 1 << 22, [(colp + 1, 8, 128), flat]
    )
    return out.reshape(nz, nx, ny)


def solution(mesh):
    in_specs = (P(None, "row", "col"), P(None, "row", "col"))
    out_specs = P(None, "row", "col")
    return jax.shard_map(
        on_device, mesh=mesh, in_specs=in_specs, out_specs=out_specs, check_vma=False
    )
```

time: 63.5 us -> 48.6 us (0.77)
  Pallas kernels: 28.9 us -> 6.12 us
  blocking collectives: 15.8 us -> 38 us
  starting transfers between devices: 10.7 us -> 3.62 us
  waiting for transfers between devices: 4.68 us -> 0.14 us
  local copies, waits for them, and re-layouts: 1.9 us -> 0.01 us
    pallas_call x9 -> x6, Pallas kernels: 28.9 us -> 6.12 us  [call(): pl.pallas_call(kernel, out_shape=[jax.ShapeDtypeStruct(s, F32) for s in o...]
    all_to_all x0 -> x2, blocking collectives: none -> 22 us  [the longest x1 11.4 us: on_device(): recv = lax.all_to_all(send, 'col', 0, 0, tiled=True)]
    all_to_all x2 -> x0, starting transfers between devices: 7.07 us -> none  [the longest x1 3.58 us: on_device(): recv = lax.all_to_all(send, 'col', 0, 0, tiled=True)]
    all_to_all x2 -> x0, waiting for transfers between devices: 4.67 us -> none  [the longest x1 4.35 us: on_device(): recv = lax.all_to_all(send, 'col', 0, 0, tiled=True)]
    unnamed x8 -> x2, local copies, waits for them, and re-layouts: 1.9 us -> 0.01 us
  transfers between devices with their start and end apart: 4 -> 2, of which waited for: 2 -> 2; matrix products, arithmetic and copies ran while one was open for 1% -> 0% of each run, Pallas kernels for 26% -> 3%
where the time goes in v2:
time: 48.6 us; the launch traced here: 48 us
  blocking collectives  38 us (78%)
  Pallas kernels  6.12 us (13%)
  starting transfers between devices  3.62 us (7%)
    all_to_all x1, blocking collectives, on_device(): recv = lax.all_to_all(send, 'row', 0, 0, tiled=True)  16.1 us
    all_to_all x1, blocking collectives, on_device(): recv = lax.all_to_all(send, 'col', 0, 0, tiled=True)  11.4 us
    all_to_all x1, blocking collectives, on_device(): recv = lax.all_to_all(back, 'row', 0, 0, tiled=True)  10.6 us
    pallas_call x6, Pallas kernels, call(): pl.pallas_call(kernel, out_shape=[jax.ShapeDtypeStruct(s, F32) for s in o...  6.12 us
    ppermute x1, starting transfers between devices, on_device(): from_right = lax.ppermute(low, 'col', [(b, a) for a, b in up])  3.6 us
  transfers between devices with their start and end apart: 2, of which 2 were waited for; matrix products, arithmetic and copies ran while one was open for 0% of the time, Pallas kernels for 3%

profile of v2, /device:TPU:0, one launch (start us, length us, event | category | flops | bytes accessed | tf_op | source)
XLA Modules:
  0.0 48.0 jit_solution(8270330974273705350)
XLA Ops:
  0.0 1.8 %shard_map.28 = (f32[1024,128]{1,0:T(8,128)S(1)}, f32[1024,128]{1,0:T(8,128)S(1)}, f32[1024,128]{1,0:T(8,128)S(1)}, f32[1024,128]{1,0:T(8,128)S(1)}, f32[16,128]{1,0:T(8,128)S(1)}, /*index=5*/f32[16,128]{1,0:T(8,128)S(1)}) custom-call(f32[1024,128]{1,0:T(8,128)} %bitcast.3, f32[1024,128]{1,0:T(8,128)} %bitcast.6), custom_call_target="tpu_custom_call" | custom-call | flops 1048576 | bytes 1048576 | tf_op jit(solution)/shard_map/pallas_call | solution.py:18
  1.8 0.0 collective-permute-start
  1.8 3.6 %collective-permute-start.1 = (f32[16,128]{1,0:T(8,128)S(1)}, f32[16,128]{1,0:T(8,128)S(1)}, u32[]{:S(2)}, u32[]{:S(2)}) collective-permute-start(f32[16,128]{1,0:T(8,128)S(1)} %get-tuple-element.25.low), channel_id=1, source_target_pairs={{1,0},{2,1},{3,2},{4,3},{5,4},{6,5},{7,6},{0,7},{9,8},{10,9},{11,1... | collective-permute-start | bytes 24584 | tf_op jit(solution)/shard_map/ppermute | solution.py:354
  5.4 1.2 %shard_map.29 = (f32[16,64,128]{2,1,0:T(8,128)S(1)}, f32[16,64,128]{2,1,0:T(8,128)S(1)}, f32[1024,128]{1,0:T(8,128)S(1)}, f32[2,64,128]{2,1,0:T(8,128)S(1)}, f32...) custom-call(f32[1024,128]{1,0:T(8,128)S(1)} %get-tuple-element.27.u, f32[1024,128]{1,0:T(8,128)S(1)} %get-tuple-element.28.k, ...), custom_call_target="tpu_custom_call" | custom-call | flops 8388608 | bytes 1048576 | tf_op jit(solution)/shard_map/pallas_call | solution.py:18
  6.7 0.1 collective-permute-done.from_left
  6.7 0.1 collective-permute-done.1.from_right
  6.8 0.7 %shard_map.30 = (f32[16,32,128]{2,1,0:T(8,128)S(1)}, f32[16,64,128]{2,1,0:T(8,128)S(1)}, f32[16,64,128]{2,1,0:T(8,128)S(1)}, f32[16,64,128]{2,1,0:T(8,128)S(1)}) custom-call(f32[16,128]{1,0:T(8,128)S(1)} %get-tuple-element.25.low, f32[16,128]{1,0:T(8,128)S(1)} %get-tuple-element.26.high, f32[16,128]{1,0:T(8,128)S(1)} %collective-permute-done.from_left, ...), custom_call_target="tpu_custom_call" | custom-call | flops 4194304 | bytes 1048576 | tf_op jit(solution)/shard_map/pallas_call | solution.py:18
  7.5 0.0 copy-start
  7.5 16.1 %all_to_all.15.recv = f32[16,32,128]{2,1,0:T(8,128)S(1)} all-to-all(f32[16,32,128]{2,1,0:T(8,128)S(1)} %get-tuple-element.35), channel_id=1, replica_groups=mesh['row'=16,'col'=8] {'row'}, dimensions={0} | all-to-all | bytes 524288 | tf_op jit(solution)/shard_map/all_to_all | solution.py:369
  23.5 0.2 shard_map.31
  23.7 10.6 %all_to_all.16.recv = f32[16,8,128]{2,1,0:T(8,128)S(1)} all-to-all(f32[16,8,128]{2,1,0:T(8,128)S(1)} %shard_map.31), channel_id=1, replica_groups=mesh['row'=16,'col'=8] {'row'}, dimensions={0} | all-to-all | bytes 131072 | tf_op jit(solution)/shard_map/all_to_all | solution.py:371
  34.3 0.0 copy-done
  34.3 1.1 %shard_map.32 = (f32[8,56,128]{2,1,0:T(8,128)S(1)}, f32[1024,128]{1,0:T(8,128)S(1)}, f32[1024,128]{1,0:T(8,128)S(1)}, f32[1024,128]{1,0:T(8,128)S(1)}) custom-call(f32[16,8,128]{2,1,0:T(8,128)S(1)} %all_to_all.16.recv, f32[16,64,128]{2,1,0:T(8,128)S(1)} %get-tuple-element.36.bx, f32[16,64,128]{2,1,0:T(8,128)S(1)} %get-tuple-element.37.g0x, ...), custom_call_target="tpu_custom_call" | custom-call | flops 4194304 | bytes 1048576 | tf_op jit(solution)/shard_map/pallas_call | solution.py:18
  35.4 11.4 %all_to_all.17.recv = f32[8,56,128]{2,1,0:T(8,128)S(1)} all-to-all(f32[8,56,128]{2,1,0:T(8,128)S(1)} %get-tuple-element.41), channel_id=1, replica_groups=mesh['row'=16,'col'=8] {'col'}, dimensions={0} | all-to-all | bytes 458752 | tf_op jit(solution)/shard_map/all_to_all | solution.py:379
  46.8 1.2 %shard_map.33 = f32[1024,128]{1,0:T(8,128)} custom-call(f32[8,56,128]{2,1,0:T(8,128)S(1)} %all_to_all.17.recv, f32[1024,128]{1,0:T(8,128)S(1)} %get-tuple-element.42.b, f32[1024,128]{1,0:T(8,128)S(1)} %get-tuple-element.43.g0, f32[1024,128]{1,0:T(8,128)S(1)} %get-tuple-element.44.gl, f32[1024,128]{1,0:T(8,128)S(1)} %bitcast.5), custom_call_target="tpu_custom_call" | custom-call | flops 4194304 | bytes 1048576 | tf_op jit(solution)/shard_map/pallas_call | solution.py:18
Async XLA Ops:
  1.8 4.9 %collective-permute-start = (f32[16,128]{1,0:T(8,128)S(1)}, f32[16,128]{1,0:T(8,128)S(1)}, u32[]{:S(2)}, u32[]{:S(2)}) collective-permute-start(f32[16,128]{1,0:T(8,128)S(1)} %get-tuple-element.26.high), channel_id=1, source_target_pairs={{0,1},{1,2},{2,3},{3,4},{4,5},{5,6},{6,7},{7,0},{8,9},{9,10},{10,1... | collective-permute-start | bytes 24584 | tf_op jit(solution)/shard_map/ppermute | solution.py:353
  1.8 5.0 %collective-permute-start.1 = (f32[16,128]{1,0:T(8,128)S(1)}, f32[16,128]{1,0:T(8,128)S(1)}, u32[]{:S(2)}, u32[]{:S(2)}) collective-permute-start(f32[16,128]{1,0:T(8,128)S(1)} %get-tuple-element.25.low), channel_id=1, source_target_pairs={{1,0},{2,1},{3,2},{4,3},{5,4},{6,5},{7,6},{0,7},{9,8},{10,9},{11,1... | collective-permute-start | bytes 24584 | tf_op jit(solution)/shard_map/ppermute | solution.py:354
  7.5 26.8 %copy-start = (f32[64,16,128]{2,1,0:T(8,128)S(1)}, f32[64,16,128]{2,1,0:T(8,128)}, u32[]{:S(2)}) copy-start(f32[64,16,128]{2,1,0:T(8,128)} %param.2) | copy-start | bytes 1572868

commit v3 on v2

--- a/solution.py
+++ b/solution.py
@@ -14,12 +14,12 @@
 CHUNKS = 4
 
 
-def call(kernel, outs, args, flops, scratch=(), specs=None):
+def call(kernel, outs, args, flops, scratch=(), specs=None, out_specs=None):
     return pl.pallas_call(
         kernel,
         out_shape=[jax.ShapeDtypeStruct(s, F32) for s in outs],
         in_specs=specs or [VMEM] * len(args),
-        out_specs=[VMEM] * len(outs),
+        out_specs=out_specs or [VMEM] * len(outs),
         scratch_shapes=[pltpu.VMEM(s, F32) if isinstance(s, tuple) else s for s in scratch],
         compiler_params=pltpu.CompilerParams(vmem_limit_bytes=12 << 20),
         cost_estimate=pl.CostEstimate(flops=flops, bytes_accessed=1 << 20, transcendentals=0),
@@ -146,7 +146,7 @@
     ends[1] = here
 
 
-def x_send_kernel(nx, peers_y, low, high, from_left, from_right, r, ends, m, p, send, b, g0, gl, turned, full):
+def x_send_kernel(nx, peers_y, low, high, from_left, from_right, r, ends, m, p, send, b, g0, gl, faces, turned, full):
     rows = r.shape[0]
     nz = rows // nx
     col = lax.axis_index("col")
@@ -154,8 +154,12 @@
     right = jnp.where(col == peers_y - 1, 0.0, from_right[...])
     k_low, u_low = low[0:8, :], low[8:16, :]
     k_high, u_high = high[0:8, :], high[8:16, :]
-    turned[0:8, :] = 0.5 * (k_low + left[0:8, :]) * (left[8:16, :] - u_low)
-    turned[8:16, :] = 0.5 * (k_high + right[0:8, :]) * (right[8:16, :] - u_high)
+    face_left = 0.5 * (k_low + left[0:8, :])
+    face_right = 0.5 * (k_high + right[0:8, :])
+    faces[0:8, :] = jnp.sqrt(face_left)
+    faces[8:16, :] = jnp.sqrt(face_right)
+    turned[0:8, :] = face_left * (left[8:16, :] - u_low)
+    turned[8:16, :] = face_right * (right[8:16, :] - u_high)
     turned[16:128, :] = jnp.zeros((112, 128), F32)
     corr = turned[...].T
     lane = lax.broadcasted_iota(jnp.int32, (128, 128), 1)
@@ -197,46 +201,57 @@
         send[d, 7 * own : 8 * own, :] = jnp.zeros((own, 128), F32)
 
 
-def reduced(peers, take):
-    zero = jnp.zeros_like(take(0)[0])
-    nothing = (zero,) * 7
-    before = nothing
-    cp = zero
-    y = zero
-    cps, ys = [], []
-    for i in range(peers + 1):
-        after = take(i) if i < peers else nothing
-        e = 0.5 * (before[6] + after[5])
-        low = e * before[1]
-        diag = 1.0 + e * (before[2] + after[0])
-        inv = 1.0 / (diag - low * cp)
-        y = (e * (after[3] - before[4]) + low * y) * inv
-        cp = e * after[1] * inv
-        cps.append(cp)
-        ys.append(y)
-        before = after
-    q = ys[peers]
-    out = [q]
-    for i in range(peers - 1, -1, -1):
-        q = ys[i] + cps[i] * q
-        out.append(q)
-    return out[::-1]
+def solve(low, diag, up, rhs):
+    n = len(diag)
+    mid = n // 2
+    c, q = [None] * n, [None] * n
+    for order, near, far in (
+        (range(mid), low, up),
+        (range(n - 1, mid, -1), up, low),
+    ):
+        last = None
+        for i in order:
+            if last is None:
+                inv = 1.0 / diag[i]
+                q[i] = rhs[i] * inv
+            else:
+                inv = 1.0 / (diag[i] - near[i] * c[last])
+                q[i] = (rhs[i] + near[i] * q[last]) * inv
+            c[i] = far[i] * inv
+            last = i
+    i = mid
+    inv = 1.0 / (diag[i] - low[i] * c[i - 1] - up[i] * c[i + 1])
+    q[i] = (rhs[i] + low[i] * q[i - 1] + up[i] * q[i + 1]) * inv
+    for i in range(mid - 1, -1, -1):
+        q[i] = q[i] + c[i] * q[i + 1]
+    for i in range(mid + 1, n):
+        q[i] = q[i] + c[i] * q[i - 1]
+    return q
 
 
 def x_reduced_kernel(recv, send):
     peers = recv.shape[0]
     own = recv.shape[1] // 8
-
-    def take(d):
-        return tuple(recv[d, q * own : (q + 1) * own, :] for q in range(7))
-
-    flux = reduced(peers, take)
+    nothing = (jnp.zeros((own, 128), F32),) * 7
+    low, diag, up, rhs = [], [], [], []
+    before = nothing
+    for i in range(peers + 1):
+        after = nothing
+        if i < peers:
+            after = tuple(recv[i, q * own : (q + 1) * own, :] for q in range(7))
+        e = 0.5 * (before[6] + after[5])
+        low.append(e * before[1])
+        diag.append(1.0 + e * (before[2] + after[0]))
+        up.append(e * after[1])
+        rhs.append(e * (after[3] - before[4]))
+        before = after
+    flux = solve(low, diag, up, rhs)
     for d in range(peers):
         send[d, 0:own, :] = flux[d]
         send[d, own : 2 * own, :] = flux[d + 1]
 
 
-def y_send_kernel(nx, recv, bx, g0x, glx, u, m, p, low, high, send, b, g0, gl, dt, ql, qr, dx):
+def y_send_kernel(nx, recv, bx, g0x, glx, u, m, p, faces, send, b, g0, gl, dt, ql, qr, dx):
     peers = recv.shape[0]
     own = recv.shape[1] // 2
     nz = peers * own
@@ -252,8 +267,9 @@
     for i in range(8):
         turn(dx, dt, i)
 
-    def forward(i, state):
-        y, w, z, x = state
+    w = x = jnp.ones((8, 128), F32)
+    y, z = row(dt, 0), row(dt, ny - 1)
+    for i in range(half - 1):
         j = ny - 1 - i
         m_left, p_left = row(m, i), row(p, i)
         m_right, p_right = row(m, j), row(p, j)
@@ -261,76 +277,74 @@
         put(g0, i, w * p_left)
         put(b, j, z * p_right)
         put(gl, j, x * p_right)
-        return (
-            row(dt, i + 1) + m_left * y,
-            w * m_left,
-            row(dt, j - 1) + m_right * z,
-            x * m_right,
-        )
-
-    one = jnp.ones((8, 128), F32)
-    y, w, z, x = lax.fori_loop(
-        0, half - 1, forward, (row(dt, 0), one, row(dt, ny - 1), one), unroll=7
-    )
+        y = row(dt, i + 1) + m_left * y
+        w = w * m_left
+        z = row(dt, j - 1) + m_right * z
+        x = x * m_right
     c_left, c_right, c_mid = row(p, half - 1), row(p, half), row(m, half)
-    state = (
-        c_left * y + c_mid * z,
-        c_left * w,
-        c_mid * x,
-        c_right * z + c_mid * y,
-        c_mid * w,
-        c_right * x,
-    )
-
-    def save(i, j, state):
-        put(b, i, state[0])
-        put(g0, i, state[1])
-        put(gl, i, state[2])
-        put(b, j, state[3])
-        put(g0, j, state[4])
-        put(gl, j, state[5])
-
-    save(half - 1, half, state)
-
-    def backward(n, state):
-        i = half - 2 - n
+    b_left, b_right = c_left * y + c_mid * z, c_right * z + c_mid * y
+    g_left, g_right = c_left * w, c_mid * w
+    h_left, h_right = c_mid * x, c_right * x
+    for i in range(half - 1, -1, -1):
         j = ny - 1 - i
-        m_left, m_right = row(m, i), row(m, j)
-        state = (
-            row(b, i) + m_left * state[0],
-            row(g0, i) + m_left * state[1],
-            m_left * state[2],
-            row(b, j) + m_right * state[3],
-            m_right * state[4],
-            row(gl, j) + m_right * state[5],
-        )
-        save(i, j, state)
-        return state
-
-    state = lax.fori_loop(0, half - 1, backward, state, unroll=7)
-    parts = [state[1], state[4], state[5], state[0], state[3], low[0:8, :], high[0:8, :]]
+        if i < half - 1:
+            m_left, m_right = row(m, i), row(m, j)
+            b_left = row(b, i) + m_left * b_left
+            g_left = row(g0, i) + m_left * g_left
+            h_left = m_left * h_left
+            b_right = row(b, j) + m_right * b_right
+            g_right = m_right * g_right
+            h_right = row(gl, j) + m_right * h_right
+        put(b, i, b_left)
+        put(g0, i, g_left)
+        put(gl, i, h_left)
+        put(b, j, b_right)
+        put(g0, j, g_right)
+        put(gl, j, h_right)
+    root_left, root_right = faces[0:8, :], faces[8:16, :]
+    parts = [
+        root_left * root_left * g_left,
+        root_left * root_right * g_right,
+        root_right * root_right * h_right,
+        root_left * b_left,
+        root_right * b_right,
+    ]
     for d in range(send.shape[0]):
         for q, part in enumerate(parts):
             send[d, q * 8 : (q + 1) * 8, :] = part
 
 
-def finish_kernel(recv, b, g0, gl, u, out, flux, whole):
+def finish_kernel(recv, b, g0, gl, u, faces, out, flux, done, sems):
     peers = recv.shape[0]
-
-    def take(d):
-        return tuple(recv[d, q * 8 : (q + 1) * 8, :] for q in range(7))
-
-    q = reduced(peers, take)
+    nothing = (jnp.zeros((8, 128), F32),) * 5
+    low, diag, up, rhs = [], [], [], []
+    before = nothing
+    for i in range(peers + 1):
+        after = nothing
+        if i < peers:
+            after = tuple(recv[i, q * 8 : (q + 1) * 8, :] for q in range(5))
+        low.append(before[1])
+        diag.append(1.0 + (before[2] + after[0]))
+        up.append(after[1])
+        rhs.append(after[3] - before[4])
+        before = after
+    q = solve(low, diag, up, rhs)
     for i in range(peers + 1):
         flux[i] = q[i]
     col = lax.axis_index("col")
-    left = flux[col]
-    right = flux[col + 1]
-    for j in range(b.shape[0] // 8):
-        put(whole, j, row(b, j) + (row(gl, j) * right - row(g0, j) * left))
+    left = flux[col] * faces[0:8, :]
+    right = flux[col + 1] * faces[8:16, :]
+    copies = []
     for i in range(8):
-        rows = slice(i * 128, (i + 1) * 128)
-        out[rows, :] = u[rows, :] + turn_back(whole, i)
+        part = pl.ds(i, 128, stride=8)
+        delta = b[part, :] + (gl[part, :] * right[i : i + 1, :] - g0[part, :] * left[i : i + 1, :])
+        rows = pl.ds(i * 128, 128)
+        done[rows, :] = u[rows, :] + delta.T
+        copy = pltpu.make_async_copy(done.at[rows], out.at[rows], sems.at[i])
+        copy.start()
+        copies.append(copy)
+    for copy in copies:
+        copy.wait()
 
 
 def on_device(field, conductivity):
@@ -359,9 +373,9 @@
         1 << 23,
         [flat],
     )
-    send, bx, g0x, glx = call(
+    send, bx, g0x, glx, faces = call(
         functools.partial(x_send_kernel, nx, colp),
-        [(rowp, 8 * own, ny)] + [cube] * 3,
+        [(rowp, 8 * own, ny)] + [cube] * 3 + [(16, 128)],
         (low, high, from_left, from_right, r, ends, mx, px),
         1 << 22,
         [(128, 128), flat],
@@ -371,14 +385,19 @@
     recv = lax.all_to_all(back, "row", 0, 0, tiled=True)
     send, b, g0y, gly = call(
         functools.partial(y_send_kernel, nx),
-        [(colp, 56, 128)] + [flat] * 3,
-        (recv, bx, g0x, glx, u, my, py, low, high),
+        [(colp, 40, 128)] + [flat] * 3,
+        (recv, bx, g0x, glx, u, my, py, faces),
         1 << 22,
         [flat, (nz, ny), (nz, ny), flat],
     )
     recv = lax.all_to_all(send, "col", 0, 0, tiled=True)
     (out,) = call(
-        finish_kernel, [flat], (recv, b, g0y, gly, u), 1 << 22, [(colp + 1, 8, 128), flat]
+        finish_kernel,
+        [flat],
+        (recv, b, g0y, gly, u, faces),
+        1 << 22,
+        [(colp + 1, 8, 128), flat, pltpu.SemaphoreType.DMA((8,))],
+        out_specs=[HBM],
     )
     return out.reshape(nz, nx, ny)
 

time: 48.6 us -> 47.6 us (0.979)
  blocking collectives: 38 us -> 37.3 us
    all_to_all x1, blocking collectives: 11.4 us -> 10.7 us  [on_device(): recv = lax.all_to_all(send, 'col', 0, 0, tiled=True)]
where the time goes in v3:
time: 47.6 us; the launch traced here: 46.9 us
  blocking collectives  37.3 us (78%)
  Pallas kernels  5.73 us (12%)
  starting transfers between devices  3.62 us (8%)
    all_to_all x1, blocking collectives, on_device(): recv = lax.all_to_all(send, 'row', 0, 0, tiled=True)  16.1 us
    all_to_all x1, blocking collectives, on_device(): recv = lax.all_to_all(send, 'col', 0, 0, tiled=True)  10.7 us
    all_to_all x1, blocking collectives, on_device(): recv = lax.all_to_all(back, 'row', 0, 0, tiled=True)  10.6 us
    pallas_call x6, Pallas kernels, call(): pl.pallas_call(kernel, out_shape=[jax.ShapeDtypeStruct(s, F32) for s in o...  5.73 us
    ppermute x1, starting transfers between devices, on_device(): from_right = lax.ppermute(low, 'col', [(b, a) for a, b in up])  3.6 us
  transfers between devices with their start and end apart: 2, of which 2 were waited for; matrix products, arithmetic and copies ran while one was open for 0% of the time, Pallas kernels for 3%

profile of v3, /device:TPU:0, one launch (start us, length us, event | category | flops | bytes accessed | tf_op | source)
XLA Modules:
  0.0 46.9 jit_solution(17934810121534966855)
XLA Ops:
  0.0 1.8 %shard_map.28 = (f32[1024,128]{1,0:T(8,128)S(1)}, f32[1024,128]{1,0:T(8,128)S(1)}, f32[1024,128]{1,0:T(8,128)S(1)}, f32[1024,128]{1,0:T(8,128)S(1)}, f32[16,128]{1,0:T(8,128)S(1)}, /*index=5*/f32[16,128]{1,0:T(8,128)S(1)}) custom-call(f32[1024,128]{1,0:T(8,128)} %bitcast.3, f32[1024,128]{1,0:T(8,128)} %bitcast.6), custom_call_target="tpu_custom_call" | custom-call | flops 1048576 | bytes 1048576 | tf_op jit(solution)/shard_map/pallas_call | solution.py:18
  1.8 0.0 collective-permute-start
  1.8 3.6 %collective-permute-start.1 = (f32[16,128]{1,0:T(8,128)S(1)}, f32[16,128]{1,0:T(8,128)S(1)}, u32[]{:S(2)}, u32[]{:S(2)}) collective-permute-start(f32[16,128]{1,0:T(8,128)S(1)} %get-tuple-element.26.low), channel_id=1, source_target_pairs={{1,0},{2,1},{3,2},{4,3},{5,4},{6,5},{7,6},{0,7},{9,8},{10,9},{11,1... | collective-permute-start | bytes 24584 | tf_op jit(solution)/shard_map/ppermute | solution.py:368
  5.4 1.2 %shard_map.29 = (f32[16,64,128]{2,1,0:T(8,128)S(1)}, f32[16,64,128]{2,1,0:T(8,128)S(1)}, f32[1024,128]{1,0:T(8,128)S(1)}, f32[2,64,128]{2,1,0:T(8,128)S(1)}, f32...) custom-call(f32[1024,128]{1,0:T(8,128)S(1)} %get-tuple-element.28.u, f32[1024,128]{1,0:T(8,128)S(1)} %get-tuple-element.29.k, ...), custom_call_target="tpu_custom_call" | custom-call | flops 8388608 | bytes 1048576 | tf_op jit(solution)/shard_map/pallas_call | solution.py:18
  6.7 0.1 collective-permute-done.from_left
  6.7 0.1 collective-permute-done.1.from_right
  6.8 0.7 %shard_map.30 = (f32[16,32,128]{2,1,0:T(8,128)S(1)}, f32[16,64,128]{2,1,0:T(8,128)S(1)}, f32[16,64,128]{2,1,0:T(8,128)S(1)}, f32[16,64,128]{2,1,0:T(8,128)S(1)}, f32[16,128]{1,0:T(8,128)S(1)}) custom-call(f32[16,128]{1,0:T(8,128)S(1)} %get-tuple-element.26.low, f32[16,128]{1,0:T(8,128)S(1)} %get-tuple-element.27.high, ...), custom_call_target="tpu_custom_call" | custom-call | flops 4194304 | bytes 1048576 | tf_op jit(solution)/shard_map/pallas_call | solution.py:18
  7.5 0.0 copy-start
  7.5 16.1 %all_to_all.15.recv = f32[16,32,128]{2,1,0:T(8,128)S(1)} all-to-all(f32[16,32,128]{2,1,0:T(8,128)S(1)} %get-tuple-element.36), channel_id=1, replica_groups=mesh['row'=16,'col'=8] {'row'}, dimensions={0} | all-to-all | bytes 524288 | tf_op jit(solution)/shard_map/all_to_all | solution.py:383
  23.5 0.1 shard_map.31
  23.7 10.6 %all_to_all.16.recv = f32[16,8,128]{2,1,0:T(8,128)S(1)} all-to-all(f32[16,8,128]{2,1,0:T(8,128)S(1)} %shard_map.31), channel_id=1, replica_groups=mesh['row'=16,'col'=8] {'row'}, dimensions={0} | all-to-all | bytes 131072 | tf_op jit(solution)/shard_map/all_to_all | solution.py:385
  34.2 0.0 copy-done
  34.2 0.9 %shard_map.32 = (f32[8,40,128]{2,1,0:T(8,128)S(1)}, f32[1024,128]{1,0:T(8,128)S(1)}, f32[1024,128]{1,0:T(8,128)S(1)}, f32[1024,128]{1,0:T(8,128)S(1)}) custom-call(f32[16,8,128]{2,1,0:T(8,128)S(1)} %all_to_all.16.recv, f32[16,64,128]{2,1,0:T(8,128)S(1)} %get-tuple-element.37.bx, f32[16,64,128]{2,1,0:T(8,128)S(1)} %get-tuple-element.38.g0x, ...), custom_call_target="tpu_custom_call" | custom-call | flops 4194304 | bytes 1048576 | tf_op jit(solution)/shard_map/pallas_call | solution.py:18
  35.1 10.7 %all_to_all.17.recv = f32[8,40,128]{2,1,0:T(8,128)S(1)} all-to-all(f32[8,40,128]{2,1,0:T(8,128)S(1)} %get-tuple-element.43), channel_id=1, replica_groups=mesh['row'=16,'col'=8] {'col'}, dimensions={0} | all-to-all | bytes 327680 | tf_op jit(solution)/shard_map/all_to_all | solution.py:393
  45.8 1.1 %shard_map.33 = f32[1024,128]{1,0:T(8,128)} custom-call(f32[8,40,128]{2,1,0:T(8,128)S(1)} %all_to_all.17.recv, f32[1024,128]{1,0:T(8,128)S(1)} %get-tuple-element.44.b, f32[1024,128]{1,0:T(8,128)S(1)} %get-tuple-element.45.g0, f32[1024,128]{1,0:T(8,128)S(1)} %get-tuple-element.46.gl, f32[1024,128]{1,0:T(8,128)S(1)} %bitcast.5, ...), custom_call_target="tpu_custom_call" | custom-call | flops 4194304 | bytes 1048576 | tf_op jit(solution)/shard_map/pallas_call | solution.py:18
Async XLA Ops:
  1.8 4.9 %collective-permute-start = (f32[16,128]{1,0:T(8,128)S(1)}, f32[16,128]{1,0:T(8,128)S(1)}, u32[]{:S(2)}, u32[]{:S(2)}) collective-permute-start(f32[16,128]{1,0:T(8,128)S(1)} %get-tuple-element.27.high), channel_id=1, source_target_pairs={{0,1},{1,2},{2,3},{3,4},{4,5},{5,6},{6,7},{7,0},{8,9},{9,10},{10,1... | collective-permute-start | bytes 24584 | tf_op jit(solution)/shard_map/ppermute | solution.py:367
  1.8 5.0 %collective-permute-start.1 = (f32[16,128]{1,0:T(8,128)S(1)}, f32[16,128]{1,0:T(8,128)S(1)}, u32[]{:S(2)}, u32[]{:S(2)}) collective-permute-start(f32[16,128]{1,0:T(8,128)S(1)} %get-tuple-element.26.low), channel_id=1, source_target_pairs={{1,0},{2,1},{3,2},{4,3},{5,4},{6,5},{7,6},{0,7},{9,8},{10,9},{11,1... | collective-permute-start | bytes 24584 | tf_op jit(solution)/shard_map/ppermute | solution.py:368
  7.5 26.8 %copy-start = (f32[64,16,128]{2,1,0:T(8,128)S(1)}, f32[64,16,128]{2,1,0:T(8,128)}, u32[]{:S(2)}) copy-start(f32[64,16,128]{2,1,0:T(8,128)} %param.2) | copy-start | bytes 1572868

commit v4 on v3

--- a/solution.py
+++ b/solution.py
@@ -11,7 +11,6 @@
 F32 = jnp.float32
 VMEM = pl.BlockSpec(memory_space=pltpu.VMEM)
 HBM = pl.BlockSpec(memory_space=pltpu.HBM)
-CHUNKS = 4
 
 
 def call(kernel, outs, args, flops, scratch=(), specs=None, out_specs=None):
@@ -36,28 +35,29 @@
     ref[pl.ds(start, 8), :] = value
 
 
-def turn(source, target, b):
-    target[pl.ds(b, 128, stride=8), :] = source[b * 128 : (b + 1) * 128, :].T
+def tile(ref, nx, b, x):
+    return ref[pl.ds(b * 8 * nx + x, 8, stride=nx), :]
+
+
+def turn(tiles, target, b):
+    target[pl.ds(b, 128, stride=8), :] = jnp.concatenate(tiles, axis=0).T
 
 
 def turn_back(source, b):
     return source[pl.ds(b, 128, stride=8), :].T
 
 
-def load_kernel(u_hbm, k_hbm, u, k, ut, kt, low, high, sems):
-    rows = u.shape[0] // CHUNKS
-    copies = []
-    for c in range(CHUNKS):
-        part = pl.ds(c * rows, rows)
-        for a, (src, dst) in enumerate(((k_hbm, k), (u_hbm, u))):
-            copy = pltpu.make_async_copy(src.at[part], dst.at[part], sems.at[2 * c + a])
-            copy.start()
-            copies.append(copy)
-    for c in range(CHUNKS):
-        for a, (src, dst) in enumerate(((k, kt), (u, ut))):
-            copies[2 * c + a].wait()
-            for b in range(c * rows // 128, (c + 1) * rows // 128):
-                turn(src, dst, b)
+def load_kernel(nx, u_hbm, k_hbm, u, k, ut, kt, low, high, sems):
+    copies = [
+        pltpu.make_async_copy(k_hbm, k, sems.at[0]),
+        pltpu.make_async_copy(u_hbm, u, sems.at[1]),
+    ]
+    for copy in copies:
+        copy.start()
+    for copy, src, dst in zip(copies, (k, u), (kt, ut)):
+        copy.wait()
+        for b in range(8):
+            turn([tile(src, nx, b, x) for x in range(nx)], dst, b)
     n = kt.shape[0] // 8
     low[0:8, :] = row(kt, 0)
     low[8:16, :] = row(ut, 0)
@@ -65,7 +65,7 @@
     high[8:16, :] = row(ut, n - 1)
 
 
-def pivots_kernel(nx, u, k, ut, kt, mx, px, r, ends, my, py, lt):
+def pivots_kernel(nx, u, k, ut, kt, mx, px, r, ends, my, py, lt, rz):
     rows = u.shape[0]
     nz = rows // nx
     ny = lt.shape[0] // 8
@@ -113,40 +113,48 @@
 
     uz, kz = at(u, 0), at(k, 0)
     below = (0.5 * z_weight) * kz * uz
-    side = None
     for z in range(nz):
-        if z * nx % 128 == 0:
-            side = turn_back(lt, z * nx // 128)
         if z + 1 < nz:
             un, kn = at(u, z + 1), at(k, z + 1)
             above = (0.5 * z_weight) * (kz + kn) * (un - uz)
         else:
             un = kn = None
             above = -(0.5 * z_weight) * kz * uz
-        part = z * nx % 128
-        r[z * nx : (z + 1) * nx, :] = uz + (above - below) + side[part : part + nx, :]
+        rz[z * nx : (z + 1) * nx, :] = uz + (above - below)
         uz, kz, below = un, kn, above
+    for b in range(8):
+        side = turn_back(lt, b)
+        for x in range(nx):
+            start = (b * nx + x) * 8
+            r[start : start + 8, :] = tile(rz, nx, b, x) + side[x * 8 : x * 8 + 8, :]
 
     def kx(i):
         return k[pl.ds(i, nz, stride=nx), :]
 
-    s = jnp.ones((nz, 128), F32)
-    here = kx(0)
-    ends[0] = here
-    for i in range(nx - 1):
-        after = kx(i + 1)
-        e = 0.5 * (here + after)
-        inv = 1.0 / (s + e)
-        m = e * inv
-        px[i] = inv
-        mx[i] = m
-        s = 1.0 + s * m
-        here = after
-    px[nx - 1] = 1.0 / s
-    ends[1] = here
-
-
-def x_send_kernel(nx, peers_y, low, high, from_left, from_right, r, ends, m, p, send, b, g0, gl, faces, turned, full):
+    mid = nx // 2
+    s = t = jnp.ones((nz, 128), F32)
+    k_left, k_right = kx(0), kx(nx - 1)
+    ends[0] = k_left
+    ends[1] = k_right
+    for i in range(mid - 1):
+        j = nx - 1 - i
+        next_left, next_right = kx(i + 1), kx(j - 1)
+        e = 0.5 * (k_left + next_left)
+        f = 0.5 * (k_right + next_right)
+        inv_e = 1.0 / (s + e)
+        inv_f = 1.0 / (t + f)
+        m_left, m_right = e * inv_e, f * inv_f
+        px[i], px[j] = inv_e, inv_f
+        mx[i], mx[j] = m_left, m_right
+        s, t = 1.0 + s * m_left, 1.0 + t * m_right
+        k_left, k_right = next_left, next_right
+    e = 0.5 * (k_left + k_right)
+    inv = 1.0 / (s * t + e * (s + t))
+    px[mid - 1], px[mid] = (t + e) * inv, (s + e) * inv
+    mx[mid - 1] = mx[mid] = e * inv
+
+
+def x_send_kernel(nx, peers_y, low, high, from_left, from_right, r, ends, m, p, send, b, g0, gl, faces, turned):
     rows = r.shape[0]
     nz = rows // nx
     col = lax.axis_index("col")
@@ -163,40 +171,54 @@
     turned[16:128, :] = jnp.zeros((112, 128), F32)
     corr = turned[...].T
     lane = lax.broadcasted_iota(jnp.int32, (128, 128), 1)
-    for i in range(rows // 128):
-        west = jnp.where(lane == 0, corr[:, i : i + 1], 0.0)
-        both = jnp.where(lane == 127, corr[:, 8 + i : 9 + i], west)
-        full[i * 128 : (i + 1) * 128, :] = r[i * 128 : (i + 1) * 128, :] + both
-    y = full[pl.ds(0, nz, stride=nx), :]
-    w = jnp.ones((nz, 128), F32)
-    for i in range(nx - 1):
-        mi, pi = m[i], p[i]
-        b[i] = y * pi
-        g0[i] = w * pi
-        y = full[pl.ds(i + 1, nz, stride=nx), :] + mi * y
-        w = w * mi
-    h = p[nx - 1]
-    v = y * h
-    g = w * h
-    b[nx - 1] = v
-    g0[nx - 1] = g
-    gl[nx - 1] = h
-    parts = [None, g, h, None, v, ends[0], ends[1]]
-    for i in range(nx - 2, -1, -1):
-        mi = m[i]
-        v = b[i] + mi * v
-        g = g0[i] + mi * g
-        h = mi * h
-        b[i] = v
-        g0[i] = g
-        gl[i] = h
-    parts[0] = g
-    parts[3] = v
     peers = send.shape[0]
     own = nz // peers
-    for q, part in enumerate(parts):
-        for d in range(peers):
-            send[d, q * own : (q + 1) * own, :] = part[d * own : (d + 1) * own, :]
+    for t in range(8):
+        zs = slice(t * 8, t * 8 + 8)
+        west = jnp.where(lane == 0, corr[:, t : t + 1], 0.0)
+        both = jnp.where(lane == 127, corr[:, 8 + t : 9 + t], west)
+
+        def source(i):
+            start = (t * nx + i) * 8
+            return r[start : start + 8, :] + both[i * 8 : i * 8 + 8, :]
+
+        mid = nx // 2
+        ys, ws = {}, {}
+        y, z = source(0), source(nx - 1)
+        w = v = None
+        for i in range(mid - 1):
+            j = nx - 1 - i
+            m_left, p_left = m[i, zs, :], p[i, zs, :]
+            m_right, p_right = m[j, zs, :], p[j, zs, :]
+            ys[i], ys[j] = y * p_left, z * p_right
+            ws[i] = p_left if w is None else w * p_left
+            ws[j] = p_right if v is None else v * p_right
+            w = m_left if w is None else w * m_left
+            v = m_right if v is None else v * m_right
+            y = source(i + 1) + m_left * y
+            z = source(j - 1) + m_right * z
+        c_left, c_right, c_mid = p[mid - 1, zs, :], p[mid, zs, :], m[mid, zs, :]
+        b_left, b_right = c_left * y + c_mid * z, c_right * z + c_mid * y
+        g_left, g_right = c_left * w, c_mid * w
+        h_left, h_right = c_mid * v, c_right * v
+        for i in range(mid - 1, -1, -1):
+            j = nx - 1 - i
+            if i < mid - 1:
+                m_left, m_right = m[i, zs, :], m[j, zs, :]
+                b_left = ys[i] + m_left * b_left
+                g_left = ws[i] + m_left * g_left
+                h_left = m_left * h_left
+                b_right = ys[j] + m_right * b_right
+                g_right = m_right * g_right
+                h_right = ws[j] + m_right * h_right
+            b[i, zs, :], b[j, zs, :] = b_left, b_right
+            g0[i, zs, :], g0[j, zs, :] = g_left, g_right
+            gl[i, zs, :], gl[j, zs, :] = h_left, h_right
+        parts = [g_left, g_right, h_right, b_left, b_right, ends[0, zs, :], ends[1, zs, :]]
+        for q, part in enumerate(parts):
+            for n in range(8 // own):
+                d = t * (8 // own) + n
+                send[d, q * own : (q + 1) * own, :] = part[n * own : (n + 1) * own, :]
     for d in range(peers):
         send[d, 7 * own : 8 * own, :] = jnp.zeros((own, 128), F32)
 
@@ -251,7 +273,7 @@
         send[d, own : 2 * own, :] = flux[d + 1]
 
 
-def y_send_kernel(nx, recv, bx, g0x, glx, u, m, p, faces, send, b, g0, gl, dt, ql, qr, dx):
+def y_send_kernel(nx, recv, bx, g0x, glx, u, m, p, faces, send, b, g0, gl, dt, ql, qr):
     peers = recv.shape[0]
     own = recv.shape[1] // 2
     nz = peers * own
@@ -260,12 +282,18 @@
     for d in range(peers):
         ql[d * own : (d + 1) * own, :] = recv[d, 0:own, :]
         qr[d * own : (d + 1) * own, :] = recv[d, own : 2 * own, :]
-    left, right = ql[...], qr[...]
-    for i in range(nx):
-        part = pl.ds(i, nz, stride=nx)
-        dx[part, :] = (bx[i] - u[part, :]) + (glx[i] * right - g0x[i] * left)
-    for i in range(8):
-        turn(dx, dt, i)
+    for t in range(8):
+        zs = slice(t * 8, t * 8 + 8)
+        left, right = ql[zs, :], qr[zs, :]
+        turn(
+            [
+                (bx[i, zs, :] - tile(u, nx, t, i))
+                + (glx[i, zs, :] * right - g0x[i, zs, :] * left)
+                for i in range(nx)
+            ],
+            dt,
+            t,
+        )
 
     w = x = jnp.ones((8, 128), F32)
     y, z = row(dt, 0), row(dt, ny - 1)
@@ -314,7 +342,7 @@
             send[d, q * 8 : (q + 1) * 8, :] = part
 
 
-def finish_kernel(recv, b, g0, gl, u, faces, out, flux, done, sems):
+def finish_kernel(nx, recv, b, g0, gl, u, faces, out, flux, whole, done, sems):
     peers = recv.shape[0]
     nothing = (jnp.zeros((8, 128), F32),) * 5
     low, diag, up, rhs = [], [], [], []
@@ -334,12 +362,16 @@
     col = lax.axis_index("col")
     left = flux[col] * faces[0:8, :]
     right = flux[col + 1] * faces[8:16, :]
+    for j in range(b.shape[0] // 8):
+        put(whole, j, row(b, j) + (row(gl, j) * right - row(g0, j) * left))
     copies = []
     for i in range(8):
-        part = pl.ds(i, 128, stride=8)
-        delta = b[part, :] + (gl[part, :] * right[i : i + 1, :] - g0[part, :] * left[i : i + 1, :])
+        delta = turn_back(whole, i)
+        for x in range(nx):
+            done[pl.ds(i * 128 + x, 8, stride=nx), :] = delta[x * 8 : x * 8 + 8, :]
+        span = slice(i * 128, (i + 1) * 128)
+        done[span, :] = u[span, :] + done[span, :]
         rows = pl.ds(i * 128, 128)
-        done[rows, :] = u[rows, :] + delta.T
         copy = pltpu.make_async_copy(done.at[rows], out.at[rows], sems.at[i])
         copy.start()
         copies.append(copy)
@@ -356,11 +388,11 @@
     k = conductivity.reshape(rows, ny)
     flat, cube = (rows, ny), (nx, nz, ny)
     uv, kv, ut, kt, low, high = call(
-        load_kernel,
+        functools.partial(load_kernel, nx),
         [flat] * 4 + [(16, 128)] * 2,
         tuple(pltpu.with_memory_space_constraint(a, pltpu.HBM) for a in (u, k)),
         1 << 20,
-        [pltpu.SemaphoreType.DMA((2 * CHUNKS,))],
+        [pltpu.SemaphoreType.DMA((2,))],
         [HBM, HBM],
     )
     up = [(i, (i + 1) % colp) for i in range(colp)]
@@ -371,14 +403,14 @@
         [cube] * 2 + [flat, (2, nz, ny)] + [flat] * 2,
         (uv, kv, ut, kt),
         1 << 23,
-        [flat],
+        [flat, flat],
     )
     send, bx, g0x, glx, faces = call(
         functools.partial(x_send_kernel, nx, colp),
         [(rowp, 8 * own, ny)] + [cube] * 3 + [(16, 128)],
         (low, high, from_left, from_right, r, ends, mx, px),
         1 << 22,
-        [(128, 128), flat],
+        [(128, 128)],
     )
     recv = lax.all_to_all(send, "row", 0, 0, tiled=True)
     (back,) = call(x_reduced_kernel, [(rowp, 2 * own, ny)], (recv,), 1 << 21)
@@ -388,15 +420,15 @@
         [(colp, 40, 128)] + [flat] * 3,
         (recv, bx, g0x, glx, u, my, py, faces),
         1 << 22,
-        [flat, (nz, ny), (nz, ny), flat],
+        [flat, (nz, ny), (nz, ny)],
     )
     recv = lax.all_to_all(send, "col", 0, 0, tiled=True)
     (out,) = call(
-        finish_kernel,
+        functools.partial(finish_kernel, nx),
         [flat],
         (recv, b, g0y, gly, u, faces),
         1 << 22,
-        [(colp + 1, 8, 128), flat, pltpu.SemaphoreType.DMA((8,))],
+        [(colp + 1, 8, 128), flat, flat, pltpu.SemaphoreType.DMA((8,))],
         out_specs=[HBM],
     )
     return out.reshape(nz, nx, ny)

time: 47.6 us -> 47.1 us (0.989)
  transfers between devices with their start and end apart: 2 -> 2, of which waited for: 2 -> 0; matrix products, arithmetic and copies ran while one was open for 0% -> 0% of each run, Pallas kernels for 3% -> 3%
where the time goes in v4:
time: 47.1 us; the launch traced here: 46.4 us
  blocking collectives  37.3 us (79%)
  Pallas kernels  5.41 us (11%)
  starting transfers between devices  3.62 us (8%)
    all_to_all x1, blocking collectives, on_device(): recv = lax.all_to_all(send, 'row', 0, 0, tiled=True)  16 us
    all_to_all x1, blocking collectives, on_device(): recv = lax.all_to_all(send, 'col', 0, 0, tiled=True)  10.7 us
    all_to_all x1, blocking collectives, on_device(): recv = lax.all_to_all(back, 'row', 0, 0, tiled=True)  10.6 us
    pallas_call x6, Pallas kernels, call(): pl.pallas_call(kernel, out_shape=[jax.ShapeDtypeStruct(s, F32) for s in o...  5.41 us
    ppermute x1, starting transfers between devices, on_device(): from_right = lax.ppermute(low, 'col', [(b, a) for a, b in up])  3.6 us
  transfers between devices with their start and end apart: 2, of which 0 were waited for; matrix products, arithmetic and copies ran while one was open for 0% of the time, Pallas kernels for 3%

profile of v4, /device:TPU:0, one launch (start us, length us, event | category | flops | bytes accessed | tf_op | source)
XLA Modules:
  0.0 46.4 jit_solution(17296382152078041308)
XLA Ops:
  0.0 1.5 %shard_map.28 = (f32[1024,128]{1,0:T(8,128)S(1)}, f32[1024,128]{1,0:T(8,128)S(1)}, f32[1024,128]{1,0:T(8,128)S(1)}, f32[1024,128]{1,0:T(8,128)S(1)}, f32[16,128]{1,0:T(8,128)S(1)}, /*index=5*/f32[16,128]{1,0:T(8,128)S(1)}) custom-call(f32[1024,128]{1,0:T(8,128)} %bitcast.3, f32[1024,128]{1,0:T(8,128)} %bitcast.6), custom_call_target="tpu_custom_call" | custom-call | flops 1048576 | bytes 1048576 | tf_op jit(solution)/shard_map/pallas_call | solution.py:17
  1.6 0.0 collective-permute-start
  1.6 3.6 %collective-permute-start.1 = (f32[16,128]{1,0:T(8,128)S(1)}, f32[16,128]{1,0:T(8,128)S(1)}, u32[]{:S(2)}, u32[]{:S(2)}) collective-permute-start(f32[16,128]{1,0:T(8,128)S(1)} %get-tuple-element.26.low), channel_id=1, source_target_pairs={{1,0},{2,1},{3,2},{4,3},{5,4},{6,5},{7,6},{0,7},{9,8},{10,9},{11,1... | collective-permute-start | bytes 24584 | tf_op jit(solution)/shard_map/ppermute | solution.py:400
  5.2 1.4 %shard_map.29 = (f32[16,64,128]{2,1,0:T(8,128)S(1)}, f32[16,64,128]{2,1,0:T(8,128)S(1)}, f32[1024,128]{1,0:T(8,128)S(1)}, f32[2,64,128]{2,1,0:T(8,128)S(1)}, f32...) custom-call(f32[1024,128]{1,0:T(8,128)S(1)} %get-tuple-element.28.u, f32[1024,128]{1,0:T(8,128)S(1)} %get-tuple-element.29.k, ...), custom_call_target="tpu_custom_call" | custom-call | flops 8388608 | bytes 1048576 | tf_op jit(solution)/shard_map/pallas_call | solution.py:17
  6.6 0.0 collective-permute-done.from_left
  6.6 0.0 collective-permute-done.1.from_right
  6.6 0.5 %shard_map.30 = (f32[16,32,128]{2,1,0:T(8,128)S(1)}, f32[16,64,128]{2,1,0:T(8,128)S(1)}, f32[16,64,128]{2,1,0:T(8,128)S(1)}, f32[16,64,128]{2,1,0:T(8,128)S(1)}, f32[16,128]{1,0:T(8,128)S(1)}) custom-call(f32[16,128]{1,0:T(8,128)S(1)} %get-tuple-element.26.low, f32[16,128]{1,0:T(8,128)S(1)} %get-tuple-element.27.high, ...), custom_call_target="tpu_custom_call" | custom-call | flops 4194304 | bytes 1048576 | tf_op jit(solution)/shard_map/pallas_call | solution.py:17
  7.1 0.0 copy-start
  7.1 16.0 %all_to_all.15.recv = f32[16,32,128]{2,1,0:T(8,128)S(1)} all-to-all(f32[16,32,128]{2,1,0:T(8,128)S(1)} %get-tuple-element.36), channel_id=1, replica_groups=mesh['row'=16,'col'=8] {'row'}, dimensions={0} | all-to-all | bytes 524288 | tf_op jit(solution)/shard_map/all_to_all | solution.py:415
  23.2 0.1 shard_map.31
  23.3 10.6 %all_to_all.16.recv = f32[16,8,128]{2,1,0:T(8,128)S(1)} all-to-all(f32[16,8,128]{2,1,0:T(8,128)S(1)} %shard_map.31), channel_id=1, replica_groups=mesh['row'=16,'col'=8] {'row'}, dimensions={0} | all-to-all | bytes 131072 | tf_op jit(solution)/shard_map/all_to_all | solution.py:417
  33.8 0.0 copy-done
  33.8 0.7 %shard_map.32 = (f32[8,40,128]{2,1,0:T(8,128)S(1)}, f32[1024,128]{1,0:T(8,128)S(1)}, f32[1024,128]{1,0:T(8,128)S(1)}, f32[1024,128]{1,0:T(8,128)S(1)}) custom-call(f32[16,8,128]{2,1,0:T(8,128)S(1)} %all_to_all.16.recv, f32[16,64,128]{2,1,0:T(8,128)S(1)} %get-tuple-element.37.bx, f32[16,64,128]{2,1,0:T(8,128)S(1)} %get-tuple-element.38.g0x, ...), custom_call_target="tpu_custom_call" | custom-call | flops 4194304 | bytes 1048576 | tf_op jit(solution)/shard_map/pallas_call | solution.py:17
  34.5 10.7 %all_to_all.17.recv = f32[8,40,128]{2,1,0:T(8,128)S(1)} all-to-all(f32[8,40,128]{2,1,0:T(8,128)S(1)} %get-tuple-element.43), channel_id=1, replica_groups=mesh['row'=16,'col'=8] {'col'}, dimensions={0} | all-to-all | bytes 327680 | tf_op jit(solution)/shard_map/all_to_all | solution.py:425
  45.2 1.1 %shard_map.33 = f32[1024,128]{1,0:T(8,128)} custom-call(f32[8,40,128]{2,1,0:T(8,128)S(1)} %all_to_all.17.recv, f32[1024,128]{1,0:T(8,128)S(1)} %get-tuple-element.44.b, f32[1024,128]{1,0:T(8,128)S(1)} %get-tuple-element.45.g0, f32[1024,128]{1,0:T(8,128)S(1)} %get-tuple-element.46.gl, f32[1024,128]{1,0:T(8,128)S(1)} %bitcast.5, ...), custom_call_target="tpu_custom_call" | custom-call | flops 4194304 | bytes 1048576 | tf_op jit(solution)/shard_map/pallas_call | solution.py:17
Async XLA Ops:
  1.6 5.0 %collective-permute-start = (f32[16,128]{1,0:T(8,128)S(1)}, f32[16,128]{1,0:T(8,128)S(1)}, u32[]{:S(2)}, u32[]{:S(2)}) collective-permute-start(f32[16,128]{1,0:T(8,128)S(1)} %get-tuple-element.27.high), channel_id=1, source_target_pairs={{0,1},{1,2},{2,3},{3,4},{4,5},{5,6},{6,7},{7,0},{8,9},{9,10},{10,1... | collective-permute-start | bytes 24584 | tf_op jit(solution)/shard_map/ppermute | solution.py:399
  1.6 5.0 %collective-permute-start.1 = (f32[16,128]{1,0:T(8,128)S(1)}, f32[16,128]{1,0:T(8,128)S(1)}, u32[]{:S(2)}, u32[]{:S(2)}) collective-permute-start(f32[16,128]{1,0:T(8,128)S(1)} %get-tuple-element.26.low), channel_id=1, source_target_pairs={{1,0},{2,1},{3,2},{4,3},{5,4},{6,5},{7,6},{0,7},{9,8},{10,9},{11,1... | collective-permute-start | bytes 24584 | tf_op jit(solution)/shard_map/ppermute | solution.py:400
  7.1 26.7 %copy-start = (f32[64,16,128]{2,1,0:T(8,128)S(1)}, f32[64,16,128]{2,1,0:T(8,128)}, u32[]{:S(2)}) copy-start(f32[64,16,128]{2,1,0:T(8,128)} %param.2) | copy-start | bytes 1572868

commit v5 on v4

--- a/solution.py
+++ b/solution.py
@@ -337,13 +337,22 @@
         root_left * b_left,
         root_right * b_right,
     ]
-    for d in range(send.shape[0]):
-        for q, part in enumerate(parts):
-            send[d, q * 8 : (q + 1) * 8, :] = part
-
-
-def finish_kernel(nx, recv, b, g0, gl, u, faces, out, flux, whole, done, sems):
-    peers = recv.shape[0]
+    for q, part in enumerate(parts):
+        send[q * 8 : (q + 1) * 8, :] = part
+
+
+def join_kernel(mine, other, both):
+    both[0:40, :] = mine[...]
+    both[40:80, :] = other[...]
+
+
+def finish_kernel(nx, peers, *refs):
+    got = refs[: peers // 2]
+    b, g0, gl, u, faces, out, recv, flux, whole, done, sems = refs[peers // 2 :]
+    col = lax.axis_index("col")
+    for n, ref in zip([0] + [a // 2 for a in [4, 2, 6]], got):
+        recv[lax.rem(col + peers - 2 * n, peers)] = ref[0:40, :]
+        recv[lax.bitwise_xor(lax.rem(col + peers - 2 * n, peers), 1)] = ref[40:80, :]
     nothing = (jnp.zeros((8, 128), F32),) * 5
     low, diag, up, rhs = [], [], [], []
     before = nothing
@@ -359,7 +368,6 @@
     q = solve(low, diag, up, rhs)
     for i in range(peers + 1):
         flux[i] = q[i]
-    col = lax.axis_index("col")
     left = flux[col] * faces[0:8, :]
     right = flux[col + 1] * faces[8:16, :]
     for j in range(b.shape[0] // 8):
@@ -417,18 +425,22 @@
     recv = lax.all_to_all(back, "row", 0, 0, tiled=True)
     send, b, g0y, gly = call(
         functools.partial(y_send_kernel, nx),
-        [(colp, 40, 128)] + [flat] * 3,
+        [(40, 128)] + [flat] * 3,
         (recv, bx, g0x, glx, u, my, py, faces),
         1 << 22,
         [flat, (nz, ny), (nz, ny)],
     )
-    recv = lax.all_to_all(send, "col", 0, 0, tiled=True)
+    other = lax.ppermute(send, "col", [(i, i ^ 1) for i in range(colp)])
+    (both,) = call(join_kernel, [(80, 128)], (send, other), 1 << 16)
+    got = [both]
+    for step in [4, 2, 6]:
+        got.append(lax.ppermute(both, "col", [(i, (i + step) % colp) for i in range(colp)]))
     (out,) = call(
-        functools.partial(finish_kernel, nx),
+        functools.partial(finish_kernel, nx, colp),
         [flat],
-        (recv, b, g0y, gly, u, faces),
+        (*got, b, g0y, gly, u, faces),
         1 << 22,
-        [(colp + 1, 8, 128), flat, flat, pltpu.SemaphoreType.DMA((8,))],
+        [(colp, 40, 128), (colp + 1, 8, 128), flat, flat, pltpu.SemaphoreType.DMA((8,))],
         out_specs=[HBM],
     )
     return out.reshape(nz, nx, ny)

time: 47.1 us -> 45.3 us (0.962); the launches traced: 46.4 us -> 45.1 us
  blocking collectives: 37.3 us -> 26.6 us
  starting transfers between devices: 3.62 us -> 9.82 us
  waiting for transfers between devices: 0.01 us -> 3.16 us
    all_to_all x1 -> x0, blocking collectives: 10.7 us -> none  [on_device(): recv = lax.all_to_all(send, 'col', 0, 0, tiled=True)]
    ppermute x0 -> x4, starting transfers between devices: none -> 6.2 us  [the longest x3 6.11 us: on_device(): lax.ppermute(both, 'col', [(i, (i + step) % colp) for i in range(colp)])]
    ppermute x0 -> x4, waiting for transfers between devices: none -> 3.15 us  [the longest x3 1.98 us: on_device(): lax.ppermute(both, 'col', [(i, (i + step) % colp) for i in range(colp)])]
    pallas_call x6 -> x7, Pallas kernels: 5.41 us -> 5.47 us  [call(): pl.pallas_call(kernel, out_shape=[jax.ShapeDtypeStruct(s, F32) for s in o...]
  transfers between devices with their start and end apart: 2 -> 6, of which waited for: 0 -> 2; matrix products, arithmetic and copies ran while one was open for 0% -> 0% of each run, Pallas kernels for 3% -> 3%
where the time goes in v5:
time: 45.3 us; the launch traced here: 45.1 us
  blocking collectives  26.6 us (59%)
  starting transfers between devices  9.82 us (22%)
  Pallas kernels  5.47 us (12%)
  waiting for transfers between devices  3.16 us (7%)
    all_to_all x1, blocking collectives, on_device(): recv = lax.all_to_all(send, 'row', 0, 0, tiled=True)  16 us
    all_to_all x1, blocking collectives, on_device(): recv = lax.all_to_all(back, 'row', 0, 0, tiled=True)  10.6 us
    ppermute x3, starting transfers between devices, on_device(): lax.ppermute(both, 'col', [(i, (i + step) % colp) for i in range(colp)])  6.11 us
    pallas_call x7, Pallas kernels, call(): pl.pallas_call(kernel, out_shape=[jax.ShapeDtypeStruct(s, F32) for s in o...  5.47 us
    ppermute x1, starting transfers between devices, on_device(): from_right = lax.ppermute(low, 'col', [(b, a) for a, b in up])  3.6 us
    ppermute x3, waiting for transfers between devices, on_device(): lax.ppermute(both, 'col', [(i, (i + step) % colp) for i in range(colp)])  1.98 us
    ppermute x1, waiting for transfers between devices, on_device(): other = lax.ppermute(send, 'col', [(i, i ^ 1) for i in range(colp)])  1.18 us
  transfers between devices with their start and end apart: 6, of which 2 were waited for; matrix products, arithmetic and copies ran while one was open for 0% of the time, Pallas kernels for 3%

profile of v5, /device:TPU:0, one launch (start us, length us, event | category | flops | bytes accessed | tf_op | source)
XLA Modules:
  0.0 45.1 jit_solution(17475726072761999542)
XLA Ops:
  0.0 1.5 %shard_map.28 = (f32[1024,128]{1,0:T(8,128)S(1)}, f32[1024,128]{1,0:T(8,128)S(1)}, f32[1024,128]{1,0:T(8,128)S(1)}, f32[1024,128]{1,0:T(8,128)S(1)}, f32[16,128]{1,0:T(8,128)S(1)}, /*index=5*/f32[16,128]{1,0:T(8,128)S(1)}) custom-call(f32[1024,128]{1,0:T(8,128)} %bitcast.3, f32[1024,128]{1,0:T(8,128)} %bitcast.6), custom_call_target="tpu_custom_call" | custom-call | flops 1048576 | bytes 1048576 | tf_op jit(solution)/shard_map/pallas_call | solution.py:17
  1.6 0.0 collective-permute-start
  1.6 3.6 %collective-permute-start.1 = (f32[16,128]{1,0:T(8,128)S(1)}, f32[16,128]{1,0:T(8,128)S(1)}, u32[]{:S(2)}, u32[]{:S(2)}) collective-permute-start(f32[16,128]{1,0:T(8,128)S(1)} %get-tuple-element.26.low), channel_id=1, source_target_pairs={{1,0},{2,1},{3,2},{4,3},{5,4},{6,5},{7,6},{0,7},{9,8},{10,9},{11,1... | collective-permute-start | bytes 24584 | tf_op jit(solution)/shard_map/ppermute | solution.py:408
  5.2 1.4 %shard_map.29 = (f32[16,64,128]{2,1,0:T(8,128)S(1)}, f32[16,64,128]{2,1,0:T(8,128)S(1)}, f32[1024,128]{1,0:T(8,128)S(1)}, f32[2,64,128]{2,1,0:T(8,128)S(1)}, f32...) custom-call(f32[1024,128]{1,0:T(8,128)S(1)} %get-tuple-element.28.u, f32[1024,128]{1,0:T(8,128)S(1)} %get-tuple-element.29.k, ...), custom_call_target="tpu_custom_call" | custom-call | flops 8388608 | bytes 1048576 | tf_op jit(solution)/shard_map/pallas_call | solution.py:17
  6.6 0.0 collective-permute-done.from_left
  6.6 0.0 collective-permute-done.1.from_right
  6.6 0.6 %shard_map.30 = (f32[16,32,128]{2,1,0:T(8,128)S(1)}, f32[16,64,128]{2,1,0:T(8,128)S(1)}, f32[16,64,128]{2,1,0:T(8,128)S(1)}, f32[16,64,128]{2,1,0:T(8,128)S(1)}, f32[16,128]{1,0:T(8,128)S(1)}) custom-call(f32[16,128]{1,0:T(8,128)S(1)} %get-tuple-element.26.low, f32[16,128]{1,0:T(8,128)S(1)} %get-tuple-element.27.high, ...), custom_call_target="tpu_custom_call" | custom-call | flops 4194304 | bytes 1048576 | tf_op jit(solution)/shard_map/pallas_call | solution.py:17
  7.1 0.0 copy-start
  7.1 16.0 %all_to_all.10.recv = f32[16,32,128]{2,1,0:T(8,128)S(1)} all-to-all(f32[16,32,128]{2,1,0:T(8,128)S(1)} %get-tuple-element.36), channel_id=1, replica_groups=mesh['row'=16,'col'=8] {'row'}, dimensions={0} | all-to-all | bytes 524288 | tf_op jit(solution)/shard_map/all_to_all | solution.py:423
  23.2 0.1 shard_map.31
  23.3 10.6 %all_to_all.11.recv = f32[16,8,128]{2,1,0:T(8,128)S(1)} all-to-all(f32[16,8,128]{2,1,0:T(8,128)S(1)} %shard_map.31), channel_id=1, replica_groups=mesh['row'=16,'col'=8] {'row'}, dimensions={0} | all-to-all | bytes 131072 | tf_op jit(solution)/shard_map/all_to_all | solution.py:425
  33.8 0.0 copy-done
  33.8 0.7 %shard_map.32 = (f32[40,128]{1,0:T(8,128)S(1)}, f32[1024,128]{1,0:T(8,128)S(1)}, f32[1024,128]{1,0:T(8,128)S(1)}, f32[1024,128]{1,0:T(8,128)S(1)}) custom-call(f32[16,8,128]{2,1,0:T(8,128)S(1)} %all_to_all.11.recv, f32[16,64,128]{2,1,0:T(8,128)S(1)} %get-tuple-element.37.bx, f32[16,64,128]{2,1,0:T(8,128)S(1)} %get-tuple-element.38.g0x, ...), custom_call_target="tpu_custom_call" | custom-call | flops 4194304 | bytes 1048576 | tf_op jit(solution)/shard_map/pallas_call | solution.py:17
  34.6 0.1 collective-permute-start.2
  34.7 1.2 %collective-permute-done.2.other = f32[40,128]{1,0:T(8,128)S(1)} collective-permute-done((f32[40,128]{1,0:T(8,128)S(1)}, f32[40,128]{1,0:T(8,128)S(1)}, u32[]{:S(2)}, u32[]{:S(2)}) %collective-permute-start.2) | collective-permute-done | bytes 20512 | tf_op jit(solution)/shard_map/ppermute | solution.py:433
  35.8 2.9 %collective-permute-start.3 = (f32[80,128]{1,0:T(8,128)S(1)}, f32[80,128]{1,0:T(8,128)S(1)}, u32[]{:S(2)}, u32[]{:S(2)}) collective-permute-start(f32[80,128]{1,0:T(8,128)S(1)} %shard_map.33.refs_0_), channel_id=1, source_target_pairs={{0,4},{1,5},{2,6},{3,7},{4,0},{5,1},{6,2},{7,3},{8,12},{9,13},{10,... | collective-permute-start | bytes 122888 | tf_op jit(solution)/shard_map/ppermute | solution.py:437
  38.7 1.1 %collective-permute-start.4 = (f32[80,128]{1,0:T(8,128)S(1)}, f32[80,128]{1,0:T(8,128)S(1)}, u32[]{:S(2)}, u32[]{:S(2)}) collective-permute-start(f32[80,128]{1,0:T(8,128)S(1)} %shard_map.33.refs_0_), channel_id=1, source_target_pairs={{0,2},{1,3},{2,4},{3,5},{4,6},{5,7},{6,0},{7,1},{8,10},{9,11},{10,... | collective-permute-start | bytes 122888 | tf_op jit(solution)/shard_map/ppermute | solution.py:437
  39.9 2.1 %collective-permute-start.5 = (f32[80,128]{1,0:T(8,128)S(1)}, f32[80,128]{1,0:T(8,128)S(1)}, u32[]{:S(2)}, u32[]{:S(2)}) collective-permute-start(f32[80,128]{1,0:T(8,128)S(1)} %shard_map.33.refs_0_), channel_id=1, source_target_pairs={{0,6},{1,7},{2,0},{3,1},{4,2},{5,3},{6,4},{7,5},{8,14},{9,15},{10,... | collective-permute-start | bytes 122888 | tf_op jit(solution)/shard_map/ppermute | solution.py:437
  41.9 0.0 collective-permute-done.3.refs_1_
  42.0 2.0 %collective-permute-done.4.refs_2_ = f32[80,128]{1,0:T(8,128)S(1)} collective-permute-done((f32[80,128]{1,0:T(8,128)S(1)}, f32[80,128]{1,0:T(8,128)S(1)}, u32[]{:S(2)}, u32[]{:S(2)}) %collective-permute-start.4) | collective-permute-done | bytes 40992 | tf_op jit(solution)/shard_map/ppermute | solution.py:437
  43.9 0.0 collective-permute-done.5.refs_3_
  43.9 1.2 %shard_map.34 = f32[1024,128]{1,0:T(8,128)} custom-call(f32[80,128]{1,0:T(8,128)S(1)} %shard_map.33.refs_0_, f32[80,128]{1,0:T(8,128)S(1)} %collective-permute-done.3.refs_1_, f32[80,128]{1,0:T(8,128)S(1)} %collective-permute-done.4.refs_2_, f32[80,128]{1,0:T(8,128)S(1)} %collective-permute-done.5.refs_3_, f32[1024,128]{1,0:T(8,128)S(1)} %get-tuple-element.44.refs_4_, ...), custom_call_target="tpu_custom_call" | custom-call | flops 4194304 | bytes 1048576 | tf_op jit(solution)/shard_map/pallas_call | solution.py:17
  (1 shorter events, 0.0 us)
Async XLA Ops:
  1.6 5.0 %collective-permute-start = (f32[16,128]{1,0:T(8,128)S(1)}, f32[16,128]{1,0:T(8,128)S(1)}, u32[]{:S(2)}, u32[]{:S(2)}) collective-permute-start(f32[16,128]{1,0:T(8,128)S(1)} %get-tuple-element.27.high), channel_id=1, source_target_pairs={{0,1},{1,2},{2,3},{3,4},{4,5},{5,6},{6,7},{7,0},{8,9},{9,10},{10,1... | collective-permute-start | bytes 24584 | tf_op jit(solution)/shard_map/ppermute | solution.py:407
  1.6 5.0 %collective-permute-start.1 = (f32[16,128]{1,0:T(8,128)S(1)}, f32[16,128]{1,0:T(8,128)S(1)}, u32[]{:S(2)}, u32[]{:S(2)}) collective-permute-start(f32[16,128]{1,0:T(8,128)S(1)} %get-tuple-element.26.low), channel_id=1, source_target_pairs={{1,0},{2,1},{3,2},{4,3},{5,4},{6,5},{7,6},{0,7},{9,8},{10,9},{11,1... | collective-permute-start | bytes 24584 | tf_op jit(solution)/shard_map/ppermute | solution.py:408
  7.1 26.7 %copy-start = (f32[64,16,128]{2,1,0:T(8,128)S(1)}, f32[64,16,128]{2,1,0:T(8,128)}, u32[]{:S(2)}) copy-start(f32[64,16,128]{2,1,0:T(8,128)} %param.2) | copy-start | bytes 1572868
  34.6 1.3 %collective-permute-start.2 = (f32[40,128]{1,0:T(8,128)S(1)}, f32[40,128]{1,0:T(8,128)S(1)}, u32[]{:S(2)}, u32[]{:S(2)}) collective-permute-start(f32[40,128]{1,0:T(8,128)S(1)} %get-tuple-element.43.mine), channel_id=1, source_target_pairs={{0,1},{1,0},{2,3},{3,2},{4,5},{5,4},{6,7},{7,6},{8,9},{9,8},{10,11... | collective-permute-start | bytes 61448 | tf_op jit(solution)/shard_map/ppermute | solution.py:433
  35.8 6.1 %collective-permute-start.3 = (f32[80,128]{1,0:T(8,128)S(1)}, f32[80,128]{1,0:T(8,128)S(1)}, u32[]{:S(2)}, u32[]{:S(2)}) collective-permute-start(f32[80,128]{1,0:T(8,128)S(1)} %shard_map.33.refs_0_), channel_id=1, source_target_pairs={{0,4},{1,5},{2,6},{3,7},{4,0},{5,1},{6,2},{7,3},{8,12},{9,13},{10,... | collective-permute-start | bytes 122888 | tf_op jit(solution)/shard_map/ppermute | solution.py:437
  38.7 5.2 %collective-permute-start.4 = (f32[80,128]{1,0:T(8,128)S(1)}, f32[80,128]{1,0:T(8,128)S(1)}, u32[]{:S(2)}, u32[]{:S(2)}) collective-permute-start(f32[80,128]{1,0:T(8,128)S(1)} %shard_map.33.refs_0_), channel_id=1, source_target_pairs={{0,2},{1,3},{2,4},{3,5},{4,6},{5,7},{6,0},{7,1},{8,10},{9,11},{10,... | collective-permute-start | bytes 122888 | tf_op jit(solution)/shard_map/ppermute | solution.py:437
  39.9 4.1 %collective-permute-start.5 = (f32[80,128]{1,0:T(8,128)S(1)}, f32[80,128]{1,0:T(8,128)S(1)}, u32[]{:S(2)}, u32[]{:S(2)}) collective-permute-start(f32[80,128]{1,0:T(8,128)S(1)} %shard_map.33.refs_0_), channel_id=1, source_target_pairs={{0,6},{1,7},{2,0},{3,1},{4,2},{5,3},{6,4},{7,5},{8,14},{9,15},{10,... | collective-permute-start | bytes 122888 | tf_op jit(solution)/shard_map/ppermute | solution.py:437

commit v6 on v5

--- a/solution.py
+++ b/solution.py
@@ -1,4 +1,5 @@
 import functools
+import math
 
 import jax
 import jax.numpy as jnp
@@ -154,7 +155,9 @@
     mx[mid - 1] = mx[mid] = e * inv
 
 
-def x_send_kernel(nx, peers_y, low, high, from_left, from_right, r, ends, m, p, send, b, g0, gl, faces, turned):
+def x_send_kernel(nx, peers_y, group, low, high, from_left, from_right, r, ends, m, p, *refs):
+    sends = refs[:group]
+    b, g0, gl, faces, turned, send = refs[group:]
     rows = r.shape[0]
     nz = rows // nx
     col = lax.axis_index("col")
@@ -171,8 +174,7 @@
     turned[16:128, :] = jnp.zeros((112, 128), F32)
     corr = turned[...].T
     lane = lax.broadcasted_iota(jnp.int32, (128, 128), 1)
-    peers = send.shape[0]
-    own = nz // peers
+    own = nz // group
     for t in range(8):
         zs = slice(t * 8, t * 8 + 8)
         west = jnp.where(lane == 0, corr[:, t : t + 1], 0.0)
@@ -216,11 +218,11 @@
             gl[i, zs, :], gl[j, zs, :] = h_left, h_right
         parts = [g_left, g_right, h_right, b_left, b_right, ends[0, zs, :], ends[1, zs, :]]
         for q, part in enumerate(parts):
-            for n in range(8 // own):
-                d = t * (8 // own) + n
-                send[d, q * own : (q + 1) * own, :] = part[n * own : (n + 1) * own, :]
-    for d in range(peers):
-        send[d, 7 * own : 8 * own, :] = jnp.zeros((own, 128), F32)
+            start = q * own + t * 8 % own
+            send[t * 8 // own, start : start + 8, :] = part
+    mine = lax.rem(lax.axis_index("row"), group)
+    for step, out in enumerate(sends):
+        out[...] = send[lax.rem(mine + step, group)]
 
 
 def solve(low, diag, up, rhs):
@@ -251,37 +253,92 @@
     return q
 
 
-def x_reduced_kernel(recv, send):
-    peers = recv.shape[0]
-    own = recv.shape[1] // 8
-    nothing = (jnp.zeros((own, 128), F32),) * 7
+def system(blocks, nothing):
     low, diag, up, rhs = [], [], [], []
-    before = nothing
-    for i in range(peers + 1):
-        after = nothing
-        if i < peers:
-            after = tuple(recv[i, q * own : (q + 1) * own, :] for q in range(7))
+    for before, after in zip([nothing] + blocks, blocks + [nothing]):
         e = 0.5 * (before[6] + after[5])
         low.append(e * before[1])
         diag.append(1.0 + e * (before[2] + after[0]))
         up.append(e * after[1])
         rhs.append(e * (after[3] - before[4]))
-        before = after
-    flux = solve(low, diag, up, rhs)
-    for d in range(peers):
-        send[d, 0:own, :] = flux[d]
-        send[d, own : 2 * own, :] = flux[d + 1]
-
-
-def y_send_kernel(nx, recv, bx, g0x, glx, u, m, p, faces, send, b, g0, gl, dt, ql, qr):
-    peers = recv.shape[0]
-    own = recv.shape[1] // 2
-    nz = peers * own
+    return low, diag, up, rhs
+
+
+def merge_kernel(group, *refs):
+    got, sup, inner, recv = refs[:group], refs[group], refs[group + 1], refs[group + 2]
+    own = sup.shape[0] // 7
+    mine = lax.rem(lax.axis_index("row"), group)
+    for step, ref in enumerate(got):
+        recv[lax.rem(mine + group - step, group)] = ref[...]
+    blocks = [tuple(recv[d, q * own : (q + 1) * own, :] for q in range(7)) for d in range(group)]
+    low, diag, up, rhs = system(blocks, blocks[0])
+    low, diag, up, rhs = low[1:group], diag[1:group], up[1:group], rhs[1:group]
+    inv = 1.0 / diag[0]
+    c_first, a_first, b_first = up[0] * inv, rhs[0] * inv, low[0] * inv
+    inv = 1.0 / diag[2]
+    c_last, a_last, g_last = low[2] * inv, rhs[2] * inv, up[2] * inv
+    inv = 1.0 / (diag[1] - low[1] * c_first - up[1] * c_last)
+    a_mid = (rhs[1] + low[1] * a_first + up[1] * a_last) * inv
+    b_mid = low[1] * b_first * inv
+    g_mid = up[1] * g_last * inv
+    a_first, b_first, g_first = a_first + c_first * a_mid, b_first + c_first * b_mid, c_first * g_mid
+    a_last, b_last, g_last = a_last + c_last * a_mid, c_last * b_mid, g_last + c_last * g_mid
+    first, last = blocks[0], blocks[group - 1]
+    parts = [
+        first[0] - first[1] * b_first,
+        first[1] * g_first,
+        last[2] - last[1] * g_last,
+        first[3] + first[1] * a_first,
+        last[4] - last[1] * a_last,
+        first[5],
+        last[6],
+    ]
+    for q, part in enumerate(parts):
+        sup[q * own : (q + 1) * own, :] = part
+    kept = [a_first, a_mid, a_last, b_first, b_mid, b_last, g_first, g_mid, g_last]
+    for q, part in enumerate(kept):
+        inner[q * own : (q + 1) * own, :] = part
+
+
+def flux_kernel(group, *refs):
+    got, inner, sends = refs[:group], refs[group], refs[group + 1 : 2 * group + 1]
+    recv, flux, send = refs[2 * group + 1 :]
+    own = got[0].shape[0] // 7
+    row_index = lax.axis_index("row")
+    mine, outer = lax.rem(row_index, group), lax.div(row_index, group)
+    for step, ref in enumerate(got):
+        recv[lax.rem(outer + group - step, group)] = ref[...]
+    blocks = [tuple(recv[d, q * own : (q + 1) * own, :] for q in range(7)) for d in range(group)]
+    q = solve(*system(blocks, (jnp.zeros((own, 128), F32),) * 7))
+    for i in range(group + 1):
+        flux[i] = q[i]
+    left, right = flux[outer], flux[outer + 1]
+
+    def kept(i):
+        return inner[i * own : (i + 1) * own, :]
+
+    q = [left]
+    for i in range(group - 1):
+        q.append(kept(i) + kept(group - 1 + i) * left + kept(2 * group - 2 + i) * right)
+    q.append(right)
+    for d in range(group):
+        send[d, 0:own, :] = q[d]
+        send[d, own : 2 * own, :] = q[d + 1]
+    for step, out in enumerate(sends):
+        out[...] = send[lax.rem(mine + step, group)]
+
+
+def y_send_kernel(nx, group, *refs):
+    got = refs[:group]
+    bx, g0x, glx, u, m, p, faces, send, b, g0, gl, dt, ql, qr = refs[group:]
+    own = got[0].shape[0] // 2
     ny = dt.shape[0] // 8
     half = ny // 2
-    for d in range(peers):
-        ql[d * own : (d + 1) * own, :] = recv[d, 0:own, :]
-        qr[d * own : (d + 1) * own, :] = recv[d, own : 2 * own, :]
+    mine = lax.rem(lax.axis_index("row"), group)
+    for step, ref in enumerate(got):
+        start = pl.multiple_of(lax.rem(mine + group - step, group) * own, own)
+        ql[pl.ds(start, own), :] = ref[0:own, :]
+        qr[pl.ds(start, own), :] = ref[own : 2 * own, :]
     for t in range(8):
         zs = slice(t * 8, t * 8 + 8)
         left, right = ql[zs, :], qr[zs, :]
@@ -391,7 +448,6 @@
     nz, nx, ny = field.shape
     rows = nz * nx
     rowp, colp = lax.axis_size("row"), lax.axis_size("col")
-    own = nz // rowp
     u = field.reshape(rows, ny)
     k = conductivity.reshape(rows, ny)
     flat, cube = (rows, ny), (nx, nz, ny)
@@ -413,20 +469,48 @@
         1 << 23,
         [flat, flat],
     )
-    send, bx, g0x, glx, faces = call(
-        functools.partial(x_send_kernel, nx, colp),
-        [(rowp, 8 * own, ny)] + [cube] * 3 + [(16, 128)],
+    group = math.isqrt(rowp)
+    own = nz // group
+    inside, across = {}, {}
+    for step in range(group):
+        inside[step] = [(i, i // group * group + (i + step) % group) for i in range(rowp)]
+        across[step] = [(i, (i + step * group) % rowp) for i in range(rowp)]
+    order = sorted(range(1, group), key=lambda step: abs(step - group // 2))
+
+    def exchange(arrays, pairs):
+        got = list(arrays)
+        for step in order:
+            got[step] = lax.ppermute(arrays[step], "row", pairs[step])
+        return got
+
+    *parts, bx, g0x, glx, faces = call(
+        functools.partial(x_send_kernel, nx, colp, group),
+        [(7 * own, ny)] * group + [cube] * 3 + [(16, 128)],
         (low, high, from_left, from_right, r, ends, mx, px),
         1 << 22,
-        [(128, 128)],
-    )
-    recv = lax.all_to_all(send, "row", 0, 0, tiled=True)
-    (back,) = call(x_reduced_kernel, [(rowp, 2 * own, ny)], (recv,), 1 << 21)
-    recv = lax.all_to_all(back, "row", 0, 0, tiled=True)
+        [(128, 128), (group, 7 * own, ny)],
+    )
+    parts = exchange(parts, inside)
+    merged, inner = call(
+        functools.partial(merge_kernel, group),
+        [(7 * own, ny), (9 * own, ny)],
+        parts,
+        1 << 20,
+        [(group, 7 * own, ny)],
+    )
+    parts = exchange([merged] * group, across)
+    parts = call(
+        functools.partial(flux_kernel, group),
+        [(2 * own, ny)] * group,
+        (*parts, inner),
+        1 << 20,
+        [(group, 7 * own, ny), (group + 1, own, ny), (group, 2 * own, ny)],
+    )
+    parts = exchange(parts, inside)
     send, b, g0y, gly = call(
-        functools.partial(y_send_kernel, nx),
+        functools.partial(y_send_kernel, nx, group),
         [(40, 128)] + [flat] * 3,
-        (recv, bx, g0x, glx, u, my, py, faces),
+        (*parts, bx, g0x, glx, u, my, py, faces),
         1 << 22,
         [flat, (nz, ny), (nz, ny)],
     )

time: 45.3 us -> 44 us (0.971)
  blocking collectives: 26.6 us -> 0 us
  starting transfers between devices: 9.82 us -> 25.4 us
  waiting for transfers between devices: 3.16 us -> 12.4 us
    all_to_all x2 -> x0, blocking collectives: 26.6 us -> none  [the longest x1 16 us: on_device(): recv = lax.all_to_all(send, 'row', 0, 0, tiled=True)]
    ppermute x0 -> x9, starting transfers between devices: none -> 15.9 us  [exchange(): got[step] = lax.ppermute(arrays[step], 'row', pairs[step])]
    ppermute x0 -> x9, waiting for transfers between devices: none -> 9.27 us  [exchange(): got[step] = lax.ppermute(arrays[step], 'row', pairs[step])]
    pallas_call x7 -> x8, Pallas kernels: 5.47 us -> 5.52 us  [call(): pl.pallas_call(kernel, out_shape=[jax.ShapeDtypeStruct(s, F32) for s in o...]
  transfers between devices with their start and end apart: 6 -> 15, of which waited for: 2 -> 8; matrix products, arithmetic and copies ran while one was open for 0% -> 0% of each run, Pallas kernels for 3% -> 3%
where the time goes in v6:
time: 44 us; the launch traced here: 43.5 us
  starting transfers between devices  25.4 us (58%)
  waiting for transfers between devices  12.4 us (28%)
  Pallas kernels  5.52 us (13%)
    ppermute x9, starting transfers between devices, exchange(): got[step] = lax.ppermute(arrays[step], 'row', pairs[step])  15.9 us
    ppermute x9, waiting for transfers between devices, exchange(): got[step] = lax.ppermute(arrays[step], 'row', pairs[step])  9.27 us
    ppermute x3, starting transfers between devices, on_device(): lax.ppermute(both, 'col', [(i, (i + step) % colp) for i in range(colp)])  5.84 us
    pallas_call x8, Pallas kernels, call(): pl.pallas_call(kernel, out_shape=[jax.ShapeDtypeStruct(s, F32) for s in o...  5.52 us
    ppermute x1, starting transfers between devices, on_device(): from_right = lax.ppermute(low, 'col', [(b, a) for a, b in up])  3.6 us
    ppermute x3, waiting for transfers between devices, on_device(): lax.ppermute(both, 'col', [(i, (i + step) % colp) for i in range(colp)])  1.98 us
    ppermute x1, waiting for transfers between devices, on_device(): other = lax.ppermute(send, 'col', [(i, i ^ 1) for i in range(colp)])  1.18 us
  transfers between devices with their start and end apart: 15, of which 8 were waited for; matrix products, arithmetic and copies ran while one was open for 0% of the time, Pallas kernels for 3%

profile of v6, /device:TPU:0, one launch (start us, length us, event | category | flops | bytes accessed | tf_op | source)
XLA Modules:
  0.0 43.5 jit_solution(1945585497912514419)
XLA Ops:
  0.0 1.5 %shard_map.28 = (f32[1024,128]{1,0:T(8,128)S(1)}, f32[1024,128]{1,0:T(8,128)S(1)}, f32[1024,128]{1,0:T(8,128)S(1)}, f32[1024,128]{1,0:T(8,128)S(1)}, f32[16,128]{1,0:T(8,128)S(1)}, /*index=5*/f32[16,128]{1,0:T(8,128)S(1)}) custom-call(f32[1024,128]{1,0:T(8,128)} %bitcast.3, f32[1024,128]{1,0:T(8,128)} %bitcast.6), custom_call_target="tpu_custom_call" | custom-call | flops 1048576 | bytes 1048576 | tf_op jit(solution)/shard_map/pallas_call | solution.py:18
  1.6 3.6 %collective-permute-start.1 = (f32[16,128]{1,0:T(8,128)S(1)}, f32[16,128]{1,0:T(8,128)S(1)}, u32[]{:S(2)}, u32[]{:S(2)}) collective-permute-start(f32[16,128]{1,0:T(8,128)S(1)} %get-tuple-element.35.low), channel_id=1, source_target_pairs={{1,0},{2,1},{3,2},{4,3},{5,4},{6,5},{7,6},{0,7},{9,8},{10,9},{11,1... | collective-permute-start | bytes 24584 | tf_op jit(solution)/shard_map/ppermute | solution.py:464
  5.2 1.4 %shard_map.29 = (f32[16,64,128]{2,1,0:T(8,128)S(1)}, f32[16,64,128]{2,1,0:T(8,128)S(1)}, f32[1024,128]{1,0:T(8,128)S(1)}, f32[2,64,128]{2,1,0:T(8,128)S(1)}, f32...) custom-call(f32[1024,128]{1,0:T(8,128)S(1)} %get-tuple-element.37.u, f32[1024,128]{1,0:T(8,128)S(1)} %get-tuple-element.38.k, ...), custom_call_target="tpu_custom_call" | custom-call | flops 8388608 | bytes 1048576 | tf_op jit(solution)/shard_map/pallas_call | solution.py:18
  6.6 0.6 %shard_map.30 = (f32[112,128]{1,0:T(8,128)S(1)}, f32[112,128]{1,0:T(8,128)S(1)}, f32[112,128]{1,0:T(8,128)S(1)}, f32[112,128]{1,0:T(8,128)S(1)}, f32[16,64,128]{...) custom-call(f32[16,128]{1,0:T(8,128)S(1)} %get-tuple-element.35.low, ...), custom_call_target="tpu_custom_call" | custom-call | flops 4194304 | bytes 1048576 | tf_op jit(solution)/shard_map/pallas_call | solution.py:18
  7.2 1.6 %collective-permute-start.2 = (f32[112,128]{1,0:T(8,128)S(1)}, f32[112,128]{1,0:T(8,128)S(1)}, u32[]{:S(2)}, u32[]{:S(2)}) collective-permute-start(f32[112,128]{1,0:T(8,128)S(1)} %get-tuple-element.46), channel_id=1, source_target_pairs={{0,8},{8,16},{16,24},{24,0},{32,40},{40,48},{48,56},{56,32},{64,72... | collective-permute-start | bytes 172040 | tf_op jit(solution)/shard_map/ppermute | solution.py:483
  8.7 2.7 %collective-permute-start.3 = (f32[112,128]{1,0:T(8,128)S(1)}, f32[112,128]{1,0:T(8,128)S(1)}, u32[]{:S(2)}, u32[]{:S(2)}) collective-permute-start(f32[112,128]{1,0:T(8,128)S(1)} %get-tuple-element.47), channel_id=1, source_target_pairs={{0,16},{8,24},{16,0},{24,8},{32,48},{40,56},{48,32},{56,40},{64,80... | collective-permute-start | bytes 172040 | tf_op jit(solution)/shard_map/ppermute | solution.py:483
  11.5 1.4 %collective-permute-start.4 = (f32[112,128]{1,0:T(8,128)S(1)}, f32[112,128]{1,0:T(8,128)S(1)}, u32[]{:S(2)}, u32[]{:S(2)}) collective-permute-start(f32[112,128]{1,0:T(8,128)S(1)} %get-tuple-element.48), channel_id=1, source_target_pairs={{0,24},{8,0},{16,8},{24,16},{32,56},{40,32},{48,40},{56,48},{64,88... | collective-permute-start | bytes 172040 | tf_op jit(solution)/shard_map/ppermute | solution.py:483
  12.9 1.8 %collective-permute-done.3.refs_2_ = f32[112,128]{1,0:T(8,128)S(1)} collective-permute-done((f32[112,128]{1,0:T(8,128)S(1)}, f32[112,128]{1,0:T(8,128)S(1)}, u32[]{:S(2)}, u32[]{:S(2)}) %collective-permute-start.3) | collective-permute-done | bytes 57376 | tf_op jit(solution)/shard_map/ppermute | solution.py:483
  14.7 1.0 %collective-permute-done.4.refs_3_ = f32[112,128]{1,0:T(8,128)S(1)} collective-permute-done((f32[112,128]{1,0:T(8,128)S(1)}, f32[112,128]{1,0:T(8,128)S(1)}, u32[]{:S(2)}, u32[]{:S(2)}) %collective-permute-start.4) | collective-permute-done | bytes 57376 | tf_op jit(solution)/shard_map/ppermute | solution.py:483
  15.7 1.6 %collective-permute-start.5 = (f32[112,128]{1,0:T(8,128)S(1)}, f32[112,128]{1,0:T(8,128)S(1)}, u32[]{:S(2)}, u32[]{:S(2)}) collective-permute-start(f32[112,128]{1,0:T(8,128)S(1)} %get-tuple-element.49.refs_0_), channel_id=1, source_target_pairs={{0,32},{8,40},{16,48},{24,56},{32,64},{40,72},{48,80},{56,88},{64,... | collective-permute-start | bytes 172040 | tf_op jit(solution)/shard_map/ppermute | solution.py:483
  17.4 2.9 %collective-permute-start.6 = (f32[112,128]{1,0:T(8,128)S(1)}, f32[112,128]{1,0:T(8,128)S(1)}, u32[]{:S(2)}, u32[]{:S(2)}) collective-permute-start(f32[112,128]{1,0:T(8,128)S(1)} %get-tuple-element.49.refs_0_), channel_id=1, source_target_pairs={{0,64},{8,72},{16,80},{24,88},{32,96},{40,104},{48,112},{56,120},{... | collective-permute-start | bytes 172040 | tf_op jit(solution)/shard_map/ppermute | solution.py:483
  20.3 1.3 %collective-permute-start.7 = (f32[112,128]{1,0:T(8,128)S(1)}, f32[112,128]{1,0:T(8,128)S(1)}, u32[]{:S(2)}, u32[]{:S(2)}) collective-permute-start(f32[112,128]{1,0:T(8,128)S(1)} %get-tuple-element.49.refs_0_), channel_id=1, source_target_pairs={{0,96},{8,104},{16,112},{24,120},{32,0},{40,8},{48,16},{56,24},{64... | collective-permute-start | bytes 172040 | tf_op jit(solution)/shard_map/ppermute | solution.py:483
  21.6 1.4 %collective-permute-done.6.refs_2_ = f32[112,128]{1,0:T(8,128)S(1)} collective-permute-done((f32[112,128]{1,0:T(8,128)S(1)}, f32[112,128]{1,0:T(8,128)S(1)}, u32[]{:S(2)}, u32[]{:S(2)}) %collective-permute-start.6) | collective-permute-done | bytes 57376 | tf_op jit(solution)/shard_map/ppermute | solution.py:483
  23.0 1.4 %collective-permute-done.7.refs_3_ = f32[112,128]{1,0:T(8,128)S(1)} collective-permute-done((f32[112,128]{1,0:T(8,128)S(1)}, f32[112,128]{1,0:T(8,128)S(1)}, u32[]{:S(2)}, u32[]{:S(2)}) %collective-permute-start.7) | collective-permute-done | bytes 57376 | tf_op jit(solution)/shard_map/ppermute | solution.py:483
  24.5 2.7 %collective-permute-start.10 = (f32[32,128]{1,0:T(8,128)S(1)}, f32[32,128]{1,0:T(8,128)S(1)}, u32[]{:S(2)}, u32[]{:S(2)}) collective-permute-start(f32[32,128]{1,0:T(8,128)S(1)} %get-tuple-element.54), channel_id=1, source_target_pairs={{0,24},{8,0},{16,8},{24,16},{32,56},{40,32},{48,40},{56,48},{64,88... | collective-permute-start | bytes 49160 | tf_op jit(solution)/shard_map/ppermute | solution.py:483
  27.2 1.5 %collective-permute-start.9 = (f32[32,128]{1,0:T(8,128)S(1)}, f32[32,128]{1,0:T(8,128)S(1)}, u32[]{:S(2)}, u32[]{:S(2)}) collective-permute-start(f32[32,128]{1,0:T(8,128)S(1)} %get-tuple-element.53), channel_id=1, source_target_pairs={{0,16},{8,24},{16,0},{24,8},{32,48},{40,56},{48,32},{56,40},{64,80... | collective-permute-start | bytes 49160 | tf_op jit(solution)/shard_map/ppermute | solution.py:483
  28.8 3.4 %collective-permute-done.8.refs_1_ = f32[32,128]{1,0:T(8,128)S(1)} collective-permute-done((f32[32,128]{1,0:T(8,128)S(1)}, f32[32,128]{1,0:T(8,128)S(1)}, u32[]{:S(2)}, u32[]{:S(2)}) %collective-permute-start.8) | collective-permute-done | bytes 16416 | tf_op jit(solution)/shard_map/ppermute | solution.py:483
  32.5 0.7 %shard_map.33 = (f32[40,128]{1,0:T(8,128)S(1)}, f32[1024,128]{1,0:T(8,128)S(1)}, f32[1024,128]{1,0:T(8,128)S(1)}, f32[1024,128]{1,0:T(8,128)S(1)}) custom-call(f32[32,128]{1,0:T(8,128)S(1)} %get-tuple-element.51.refs_0_, f32[32,128]{1,0:T(8,128)S(1)} %collective-permute-done.8.refs_1_, f32[32,128]{1,0:T(8,128)S(1)} %collective-permute-done.9.refs_2_, ...), custom_call_target="tpu_custom_call" | custom-call | flops 4194304 | bytes 1048576 | tf_op jit(solution)/shard_map/pallas_call | solution.py:18
  33.3 1.2 %collective-permute-done.11.other = f32[40,128]{1,0:T(8,128)S(1)} collective-permute-done((f32[40,128]{1,0:T(8,128)S(1)}, f32[40,128]{1,0:T(8,128)S(1)}, u32[]{:S(2)}, u32[]{:S(2)}) %collective-permute-start.11) | collective-permute-done | bytes 20512 | tf_op jit(solution)/shard_map/ppermute | solution.py:517
  34.5 2.6 %collective-permute-start.12 = (f32[80,128]{1,0:T(8,128)S(1)}, f32[80,128]{1,0:T(8,128)S(1)}, u32[]{:S(2)}, u32[]{:S(2)}) collective-permute-start(f32[80,128]{1,0:T(8,128)S(1)} %shard_map.34.refs_0_), channel_id=1, source_target_pairs={{0,4},{1,5},{2,6},{3,7},{4,0},{5,1},{6,2},{7,3},{8,12},{9,13},{10,... | collective-permute-start | bytes 122888 | tf_op jit(solution)/shard_map/ppermute | solution.py:521
  37.1 0.6 %collective-permute-start.13 = (f32[80,128]{1,0:T(8,128)S(1)}, f32[80,128]{1,0:T(8,128)S(1)}, u32[]{:S(2)}, u32[]{:S(2)}) collective-permute-start(f32[80,128]{1,0:T(8,128)S(1)} %shard_map.34.refs_0_), channel_id=1, source_target_pairs={{0,2},{1,3},{2,4},{3,5},{4,6},{5,7},{6,0},{7,1},{8,10},{9,11},{10,... | collective-permute-start | bytes 122888 | tf_op jit(solution)/shard_map/ppermute | solution.py:521
  37.7 2.6 %collective-permute-start.14 = (f32[80,128]{1,0:T(8,128)S(1)}, f32[80,128]{1,0:T(8,128)S(1)}, u32[]{:S(2)}, u32[]{:S(2)}) collective-permute-start(f32[80,128]{1,0:T(8,128)S(1)} %shard_map.34.refs_0_), channel_id=1, source_target_pairs={{0,6},{1,7},{2,0},{3,1},{4,2},{5,3},{6,4},{7,5},{8,14},{9,15},{10,... | collective-permute-start | bytes 122888 | tf_op jit(solution)/shard_map/ppermute | solution.py:521
  40.3 2.0 %collective-permute-done.13.refs_2_ = f32[80,128]{1,0:T(8,128)S(1)} collective-permute-done((f32[80,128]{1,0:T(8,128)S(1)}, f32[80,128]{1,0:T(8,128)S(1)}, u32[]{:S(2)}, u32[]{:S(2)}) %collective-permute-start.13) | collective-permute-done | bytes 40992 | tf_op jit(solution)/shard_map/ppermute | solution.py:521
  42.3 1.2 %shard_map.35 = f32[1024,128]{1,0:T(8,128)} custom-call(f32[80,128]{1,0:T(8,128)S(1)} %shard_map.34.refs_0_, f32[80,128]{1,0:T(8,128)S(1)} %collective-permute-done.12.refs_1_, f32[80,128]{1,0:T(8,128)S(1)} %collective-permute-done.13.refs_2_, f32[80,128]{1,0:T(8,128)S(1)} %collective-permute-done.14.refs_3_, f32[1024,128]{1,0:T(8,128)S(1)} %get-tuple-element.62.refs_4_, ...), custom_call_target="tpu_custom_call" | custom-call | flops 4194304 | bytes 1048576 | tf_op jit(solution)/shard_map/pallas_call | solution.py:18
  (16 shorter events, 0.6 us)
Async XLA Ops:
  1.6 5.0 %collective-permute-start = (f32[16,128]{1,0:T(8,128)S(1)}, f32[16,128]{1,0:T(8,128)S(1)}, u32[]{:S(2)}, u32[]{:S(2)}) collective-permute-start(f32[16,128]{1,0:T(8,128)S(1)} %get-tuple-element.36.high), channel_id=1, source_target_pairs={{0,1},{1,2},{2,3},{3,4},{4,5},{5,6},{6,7},{7,0},{8,9},{9,10},{10,1... | collective-permute-start | bytes 24584 | tf_op jit(solution)/shard_map/ppermute | solution.py:463
  1.6 5.0 %collective-permute-start.1 = (f32[16,128]{1,0:T(8,128)S(1)}, f32[16,128]{1,0:T(8,128)S(1)}, u32[]{:S(2)}, u32[]{:S(2)}) collective-permute-start(f32[16,128]{1,0:T(8,128)S(1)} %get-tuple-element.35.low), channel_id=1, source_target_pairs={{1,0},{2,1},{3,2},{4,3},{5,4},{6,5},{7,6},{0,7},{9,8},{10,9},{11,1... | collective-permute-start | bytes 24584 | tf_op jit(solution)/shard_map/ppermute | solution.py:464
  7.2 25.3 %copy-start = (f32[64,16,128]{2,1,0:T(8,128)S(1)}, f32[64,16,128]{2,1,0:T(8,128)}, u32[]{:S(2)}) copy-start(f32[64,16,128]{2,1,0:T(8,128)} %param.2) | copy-start | bytes 1572868
  7.2 5.7 %collective-permute-start.2 = (f32[112,128]{1,0:T(8,128)S(1)}, f32[112,128]{1,0:T(8,128)S(1)}, u32[]{:S(2)}, u32[]{:S(2)}) collective-permute-start(f32[112,128]{1,0:T(8,128)S(1)} %get-tuple-element.46), channel_id=1, source_target_pairs={{0,8},{8,16},{16,24},{24,0},{32,40},{40,48},{48,56},{56,32},{64,72... | collective-permute-start | bytes 172040 | tf_op jit(solution)/shard_map/ppermute | solution.py:483
  8.7 6.0 %collective-permute-start.3 = (f32[112,128]{1,0:T(8,128)S(1)}, f32[112,128]{1,0:T(8,128)S(1)}, u32[]{:S(2)}, u32[]{:S(2)}) collective-permute-start(f32[112,128]{1,0:T(8,128)S(1)} %get-tuple-element.47), channel_id=1, source_target_pairs={{0,16},{8,24},{16,0},{24,8},{32,48},{40,56},{48,32},{56,40},{64,80... | collective-permute-start | bytes 172040 | tf_op jit(solution)/shard_map/ppermute | solution.py:483
  11.5 4.2 %collective-permute-start.4 = (f32[112,128]{1,0:T(8,128)S(1)}, f32[112,128]{1,0:T(8,128)S(1)}, u32[]{:S(2)}, u32[]{:S(2)}) collective-permute-start(f32[112,128]{1,0:T(8,128)S(1)} %get-tuple-element.48), channel_id=1, source_target_pairs={{0,24},{8,0},{16,8},{24,16},{32,56},{40,32},{48,40},{56,48},{64,88... | collective-permute-start | bytes 172040 | tf_op jit(solution)/shard_map/ppermute | solution.py:483
  15.7 5.9 %collective-permute-start.5 = (f32[112,128]{1,0:T(8,128)S(1)}, f32[112,128]{1,0:T(8,128)S(1)}, u32[]{:S(2)}, u32[]{:S(2)}) collective-permute-start(f32[112,128]{1,0:T(8,128)S(1)} %get-tuple-element.49.refs_0_), channel_id=1, source_target_pairs={{0,32},{8,40},{16,48},{24,56},{32,64},{40,72},{48,80},{56,88},{64,... | collective-permute-start | bytes 172040 | tf_op jit(solution)/shard_map/ppermute | solution.py:483
  17.4 5.7 %collective-permute-start.6 = (f32[112,128]{1,0:T(8,128)S(1)}, f32[112,128]{1,0:T(8,128)S(1)}, u32[]{:S(2)}, u32[]{:S(2)}) collective-permute-start(f32[112,128]{1,0:T(8,128)S(1)} %get-tuple-element.49.refs_0_), channel_id=1, source_target_pairs={{0,64},{8,72},{16,80},{24,88},{32,96},{40,104},{48,112},{56,120},{... | collective-permute-start | bytes 172040 | tf_op jit(solution)/shard_map/ppermute | solution.py:483
  20.3 4.2 %collective-permute-start.7 = (f32[112,128]{1,0:T(8,128)S(1)}, f32[112,128]{1,0:T(8,128)S(1)}, u32[]{:S(2)}, u32[]{:S(2)}) collective-permute-start(f32[112,128]{1,0:T(8,128)S(1)} %get-tuple-element.49.refs_0_), channel_id=1, source_target_pairs={{0,96},{8,104},{16,112},{24,120},{32,0},{40,8},{48,16},{56,24},{64... | collective-permute-start | bytes 172040 | tf_op jit(solution)/shard_map/ppermute | solution.py:483
  24.5 4.3 %collective-permute-start.10 = (f32[32,128]{1,0:T(8,128)S(1)}, f32[32,128]{1,0:T(8,128)S(1)}, u32[]{:S(2)}, u32[]{:S(2)}) collective-permute-start(f32[32,128]{1,0:T(8,128)S(1)} %get-tuple-element.54), channel_id=1, source_target_pairs={{0,24},{8,0},{16,8},{24,16},{32,56},{40,32},{48,40},{56,48},{64,88... | collective-permute-start | bytes 49160 | tf_op jit(solution)/shard_map/ppermute | solution.py:483
  27.2 4.9 %collective-permute-start.8 = (f32[32,128]{1,0:T(8,128)S(1)}, f32[32,128]{1,0:T(8,128)S(1)}, u32[]{:S(2)}, u32[]{:S(2)}) collective-permute-start(f32[32,128]{1,0:T(8,128)S(1)} %get-tuple-element.52), channel_id=1, source_target_pairs={{0,8},{8,16},{16,24},{24,0},{32,40},{40,48},{48,56},{56,32},{64,72... | collective-permute-start | bytes 49160 | tf_op jit(solution)/shard_map/ppermute | solution.py:483
  27.2 5.2 %collective-permute-start.9 = (f32[32,128]{1,0:T(8,128)S(1)}, f32[32,128]{1,0:T(8,128)S(1)}, u32[]{:S(2)}, u32[]{:S(2)}) collective-permute-start(f32[32,128]{1,0:T(8,128)S(1)} %get-tuple-element.53), channel_id=1, source_target_pairs={{0,16},{8,24},{16,0},{24,8},{32,48},{40,56},{48,32},{56,40},{64,80... | collective-permute-start | bytes 49160 | tf_op jit(solution)/shard_map/ppermute | solution.py:483
  33.2 1.3 %collective-permute-start.11 = (f32[40,128]{1,0:T(8,128)S(1)}, f32[40,128]{1,0:T(8,128)S(1)}, u32[]{:S(2)}, u32[]{:S(2)}) collective-permute-start(f32[40,128]{1,0:T(8,128)S(1)} %get-tuple-element.61.mine), channel_id=1, source_target_pairs={{0,1},{1,0},{2,3},{3,2},{4,5},{5,4},{6,7},{7,6},{8,9},{9,8},{10,11... | collective-permute-start | bytes 61448 | tf_op jit(solution)/shard_map/ppermute | solution.py:517
  34.5 5.8 %collective-permute-start.12 = (f32[80,128]{1,0:T(8,128)S(1)}, f32[80,128]{1,0:T(8,128)S(1)}, u32[]{:S(2)}, u32[]{:S(2)}) collective-permute-start(f32[80,128]{1,0:T(8,128)S(1)} %shard_map.34.refs_0_), channel_id=1, source_target_pairs={{0,4},{1,5},{2,6},{3,7},{4,0},{5,1},{6,2},{7,3},{8,12},{9,13},{10,... | collective-permute-start | bytes 122888 | tf_op jit(solution)/shard_map/ppermute | solution.py:521
  37.1 5.2 %collective-permute-start.13 = (f32[80,128]{1,0:T(8,128)S(1)}, f32[80,128]{1,0:T(8,128)S(1)}, u32[]{:S(2)}, u32[]{:S(2)}) collective-permute-start(f32[80,128]{1,0:T(8,128)S(1)} %shard_map.34.refs_0_), channel_id=1, source_target_pairs={{0,2},{1,3},{2,4},{3,5},{4,6},{5,7},{6,0},{7,1},{8,10},{9,11},{10,... | collective-permute-start | bytes 122888 | tf_op jit(solution)/shard_map/ppermute | solution.py:521
  37.7 4.6 %collective-permute-start.14 = (f32[80,128]{1,0:T(8,128)S(1)}, f32[80,128]{1,0:T(8,128)S(1)}, u32[]{:S(2)}, u32[]{:S(2)}) collective-permute-start(f32[80,128]{1,0:T(8,128)S(1)} %shard_map.34.refs_0_), channel_id=1, source_target_pairs={{0,6},{1,7},{2,0},{3,1},{4,2},{5,3},{6,4},{7,5},{8,14},{9,15},{10,... | collective-permute-start | bytes 122888 | tf_op jit(solution)/shard_map/ppermute | solution.py:521

commit v7 on v6

--- a/solution.py
+++ b/solution.py
@@ -66,37 +66,10 @@
     high[8:16, :] = row(ut, n - 1)
 
 
-def pivots_kernel(nx, u, k, ut, kt, mx, px, r, ends, my, py, lt, rz):
+def pivots_kernel(nx, u, k, ut, kt, mx, px, g0, gl, r, ends, lt, rz):
     rows = u.shape[0]
     nz = rows // nx
     ny = lt.shape[0] // 8
-    half = ny // 2
-
-    def both(i, state):
-        s, t, k_left, k_right = state
-        j = ny - 1 - i
-        next_left, next_right = row(kt, i + 1), row(kt, j - 1)
-        e = 0.5 * (k_left + next_left)
-        f = 0.5 * (k_right + next_right)
-        inv_e = 1.0 / (s + e)
-        inv_f = 1.0 / (t + f)
-        m_left, m_right = e * inv_e, f * inv_f
-        put(py, i, inv_e)
-        put(py, j, inv_f)
-        put(my, i, m_left)
-        put(my, j, m_right)
-        return 1.0 + s * m_left, 1.0 + t * m_right, next_left, next_right
-
-    one = jnp.ones((8, 128), F32)
-    s, t, k_left, k_right = lax.fori_loop(
-        0, half - 1, both, (one, one, row(kt, 0), row(kt, ny - 1)), unroll=7
-    )
-    e = 0.5 * (k_left + k_right)
-    inv = 1.0 / (s * t + e * (s + t))
-    put(py, half - 1, (t + e) * inv)
-    put(py, half, (s + e) * inv)
-    put(my, half - 1, e * inv)
-    put(my, half, e * inv)
 
     here_k, here_u = row(kt, 0), row(ut, 0)
     before = None
@@ -151,13 +124,29 @@
         k_left, k_right = next_left, next_right
     e = 0.5 * (k_left + k_right)
     inv = 1.0 / (s * t + e * (s + t))
-    px[mid - 1], px[mid] = (t + e) * inv, (s + e) * inv
-    mx[mid - 1] = mx[mid] = e * inv
-
-
-def x_send_kernel(nx, peers_y, group, low, high, from_left, from_right, r, ends, m, p, *refs):
+    c_left, c_right, c_mid = (t + e) * inv, (s + e) * inv, e * inv
+    px[mid - 1], px[mid] = c_left, c_right
+    mx[mid - 1] = mx[mid] = c_mid
+    w = v = jnp.ones((nz, 128), F32)
+    for i in range(mid - 1):
+        j = nx - 1 - i
+        g0[i], gl[j] = w * px[i], v * px[j]
+        w, v = w * mx[i], v * mx[j]
+    g_left, g_right = c_left * w, c_mid * w
+    h_left, h_right = c_mid * v, c_right * v
+    for i in range(mid - 1, -1, -1):
+        j = nx - 1 - i
+        if i < mid - 1:
+            m_left, m_right = mx[i], mx[j]
+            g_left, h_left = g0[i] + m_left * g_left, m_left * h_left
+            g_right, h_right = m_right * g_right, gl[j] + m_right * h_right
+        g0[i], g0[j] = g_left, g_right
+        gl[i], gl[j] = h_left, h_right
+
+
+def x_send_kernel(nx, peers_y, group, low, high, from_left, from_right, r, ends, g0, gl, *refs):
     sends = refs[:group]
-    b, g0, gl, faces, turned, send = refs[group:]
+    full, faces, turned, send = refs[group:]
     rows = r.shape[0]
     nz = rows // nx
     col = lax.axis_index("col")
@@ -180,49 +169,140 @@
         west = jnp.where(lane == 0, corr[:, t : t + 1], 0.0)
         both = jnp.where(lane == 127, corr[:, 8 + t : 9 + t], west)
 
-        def source(i):
+        zero = jnp.zeros((8, 128), F32)
+        b0, bl = [zero, zero], [zero, zero]
+        for i in range(nx):
             start = (t * nx + i) * 8
-            return r[start : start + 8, :] + both[i * 8 : i * 8 + 8, :]
-
-        mid = nx // 2
-        ys, ws = {}, {}
-        y, z = source(0), source(nx - 1)
-        w = v = None
-        for i in range(mid - 1):
-            j = nx - 1 - i
-            m_left, p_left = m[i, zs, :], p[i, zs, :]
-            m_right, p_right = m[j, zs, :], p[j, zs, :]
-            ys[i], ys[j] = y * p_left, z * p_right
-            ws[i] = p_left if w is None else w * p_left
-            ws[j] = p_right if v is None else v * p_right
-            w = m_left if w is None else w * m_left
-            v = m_right if v is None else v * m_right
-            y = source(i + 1) + m_left * y
-            z = source(j - 1) + m_right * z
-        c_left, c_right, c_mid = p[mid - 1, zs, :], p[mid, zs, :], m[mid, zs, :]
-        b_left, b_right = c_left * y + c_mid * z, c_right * z + c_mid * y
-        g_left, g_right = c_left * w, c_mid * w
-        h_left, h_right = c_mid * v, c_right * v
-        for i in range(mid - 1, -1, -1):
-            j = nx - 1 - i
-            if i < mid - 1:
-                m_left, m_right = m[i, zs, :], m[j, zs, :]
-                b_left = ys[i] + m_left * b_left
-                g_left = ws[i] + m_left * g_left
-                h_left = m_left * h_left
-                b_right = ys[j] + m_right * b_right
-                g_right = m_right * g_right
-                h_right = ws[j] + m_right * h_right
-            b[i, zs, :], b[j, zs, :] = b_left, b_right
-            g0[i, zs, :], g0[j, zs, :] = g_left, g_right
-            gl[i, zs, :], gl[j, zs, :] = h_left, h_right
-        parts = [g_left, g_right, h_right, b_left, b_right, ends[0, zs, :], ends[1, zs, :]]
+            ri = r[start : start + 8, :] + both[i * 8 : i * 8 + 8, :]
+            full[start : start + 8, :] = ri
+            b0[i % 2] = b0[i % 2] + g0[i, zs, :] * ri
+            bl[i % 2] = bl[i % 2] + gl[i, zs, :] * ri
+        parts = [
+            g0[0, zs, :],
+            g0[nx - 1, zs, :],
+            gl[nx - 1, zs, :],
+            b0[0] + b0[1],
+            bl[0] + bl[1],
+            ends[0, zs, :],
+            ends[1, zs, :],
+        ]
         for q, part in enumerate(parts):
             start = q * own + t * 8 % own
             send[t * 8 // own, start : start + 8, :] = part
     mine = lax.rem(lax.axis_index("row"), group)
     for step, out in enumerate(sends):
         out[...] = send[lax.rem(mine + step, group)]
+
+
+def x_inner_kernel(nx, r, m, p, b):
+    mid = nx // 2
+    for t in range(8):
+        zs = slice(t * 8, t * 8 + 8)
+
+        def source(i):
+            start = (t * nx + i) * 8
+            return r[start : start + 8, :]
+
+        ys = {}
+        y, z = source(0), source(nx - 1)
+        for i in range(mid - 1):
+            j = nx - 1 - i
+            ys[i], ys[j] = y * p[i, zs, :], z * p[j, zs, :]
+            y = source(i + 1) + m[i, zs, :] * y
+            z = source(j - 1) + m[j, zs, :] * z
+        c_left, c_right, c_mid = p[mid - 1, zs, :], p[mid, zs, :], m[mid, zs, :]
+        y, z = c_left * y + c_mid * z, c_right * z + c_mid * y
+        for i in range(mid - 1, -1, -1):
+            j = nx - 1 - i
+            if i < mid - 1:
+                y = ys[i] + m[i, zs, :] * y
+                z = ys[j] + m[j, zs, :] * z
+            b[i, zs, :], b[j, zs, :] = y, z
+
+
+def y_pivots(kt, my, py):
+    ny = kt.shape[0] // 8
+    half = ny // 2
+
+    def both(i, state):
+        s, t, k_left, k_right = state
+        j = ny - 1 - i
+        next_left, next_right = row(kt, i + 1), row(kt, j - 1)
+        e = 0.5 * (k_left + next_left)
+        f = 0.5 * (k_right + next_right)
+        inv_e = 1.0 / (s + e)
+        inv_f = 1.0 / (t + f)
+        m_left, m_right = e * inv_e, f * inv_f
+        put(py, i, inv_e)
+        put(py, j, inv_f)
+        put(my, i, m_left)
+        put(my, j, m_right)
+        return 1.0 + s * m_left, 1.0 + t * m_right, next_left, next_right
+
+    one = jnp.ones((8, 128), F32)
+    s, t, k_left, k_right = lax.fori_loop(
+        0, half - 1, both, (one, one, row(kt, 0), row(kt, ny - 1)), unroll=7
+    )
+    e = 0.5 * (k_left + k_right)
+    inv = 1.0 / (s * t + e * (s + t))
+    put(py, half - 1, (t + e) * inv)
+    put(py, half, (s + e) * inv)
+    put(my, half - 1, e * inv)
+    put(my, half, e * inv)
+
+
+def y_pivots_kernel(nx, k, ready, my, py, kt):
+    for b in range(8):
+        turn([tile(k, nx, b, x) for x in range(nx)], kt, b)
+    y_pivots(kt, my, py)
+
+
+def y_columns_kernel(nx, k, g0, gl, kt, m, p):
+    for b in range(8):
+        turn([tile(k, nx, b, x) for x in range(nx)], kt, b)
+    y_pivots(kt, m, p)
+    ny = kt.shape[0] // 8
+    half = ny // 2
+    w = x = jnp.ones((8, 128), F32)
+    for i in range(half - 1):
+        j = ny - 1 - i
+        put(g0, i, w * row(p, i))
+        put(gl, j, x * row(p, j))
+        w, x = w * row(m, i), x * row(m, j)
+    c_left, c_right, c_mid = row(p, half - 1), row(p, half), row(m, half)
+    g_left, g_right = c_left * w, c_mid * w
+    h_left, h_right = c_mid * x, c_right * x
+    for i in range(half - 1, -1, -1):
+        j = ny - 1 - i
+        if i < half - 1:
+            m_left, m_right = row(m, i), row(m, j)
+            g_left, h_left = row(g0, i) + m_left * g_left, m_left * h_left
+            g_right, h_right = m_right * g_right, row(gl, j) + m_right * h_right
+        put(g0, i, g_left)
+        put(g0, j, g_right)
+        put(gl, i, h_left)
+        put(gl, j, h_right)
+
+
+def y_inner_kernel(dt, m, p, b):
+    ny = dt.shape[0] // 8
+    half = ny // 2
+    y, z = row(dt, 0), row(dt, ny - 1)
+    for i in range(half - 1):
+        j = ny - 1 - i
+        put(b, i, y * row(p, i))
+        put(b, j, z * row(p, j))
+        y = row(dt, i + 1) + row(m, i) * y
+        z = row(dt, j - 1) + row(m, j) * z
+    c_left, c_right, c_mid = row(p, half - 1), row(p, half), row(m, half)
+    y, z = c_left * y + c_mid * z, c_right * z + c_mid * y
+    for i in range(half - 1, -1, -1):
+        j = ny - 1 - i
+        if i < half - 1:
+            y = row(b, i) + row(m, i) * y
+            z = row(b, j) + row(m, j) * z
+        put(b, i, y)
+        put(b, j, z)
 
 
 def solve(low, diag, up, rhs):
@@ -253,6 +333,10 @@
     return q
 
 
+def far_first(group):
+    return [0] + [1, 3, 2]
+
+
 def system(blocks, nothing):
     low, diag, up, rhs = [], [], [], []
     for before, after in zip([nothing] + blocks, blocks + [nothing]):
@@ -268,7 +352,7 @@
     got, sup, inner, recv = refs[:group], refs[group], refs[group + 1], refs[group + 2]
     own = sup.shape[0] // 7
     mine = lax.rem(lax.axis_index("row"), group)
-    for step, ref in enumerate(got):
+    for step, ref in zip(far_first(group), got):
         recv[lax.rem(mine + group - step, group)] = ref[...]
     blocks = [tuple(recv[d, q * own : (q + 1) * own, :] for q in range(7)) for d in range(group)]
     low, diag, up, rhs = system(blocks, blocks[0])
@@ -301,12 +385,12 @@
 
 
 def flux_kernel(group, *refs):
-    got, inner, sends = refs[:group], refs[group], refs[group + 1 : 2 * group + 1]
-    recv, flux, send = refs[2 * group + 1 :]
+    got, inner, sends = refs[:group], refs[group], refs[group + 3 : 2 * group + 3]
+    recv, flux, send = refs[2 * group + 3 :]
     own = got[0].shape[0] // 7
     row_index = lax.axis_index("row")
     mine, outer = lax.rem(row_index, group), lax.div(row_index, group)
-    for step, ref in enumerate(got):
+    for step, ref in zip(far_first(group), got):
         recv[lax.rem(outer + group - step, group)] = ref[...]
     blocks = [tuple(recv[d, q * own : (q + 1) * own, :] for q in range(7)) for d in range(group)]
     q = solve(*system(blocks, (jnp.zeros((own, 128), F32),) * 7))
@@ -330,12 +414,11 @@
 
 def y_send_kernel(nx, group, *refs):
     got = refs[:group]
-    bx, g0x, glx, u, m, p, faces, send, b, g0, gl, dt, ql, qr = refs[group:]
+    bx, g0x, glx, u, g0, gl, faces, send, dt, ql, qr = refs[group:]
     own = got[0].shape[0] // 2
     ny = dt.shape[0] // 8
-    half = ny // 2
     mine = lax.rem(lax.axis_index("row"), group)
-    for step, ref in enumerate(got):
+    for step, ref in zip(far_first(group), got):
         start = pl.multiple_of(lax.rem(mine + group - step, group) * own, own)
         ql[pl.ds(start, own), :] = ref[0:own, :]
         qr[pl.ds(start, own), :] = ref[own : 2 * own, :]
@@ -352,64 +435,55 @@
             t,
         )
 
-    w = x = jnp.ones((8, 128), F32)
-    y, z = row(dt, 0), row(dt, ny - 1)
-    for i in range(half - 1):
-        j = ny - 1 - i
-        m_left, p_left = row(m, i), row(p, i)
-        m_right, p_right = row(m, j), row(p, j)
-        put(b, i, y * p_left)
-        put(g0, i, w * p_left)
-        put(b, j, z * p_right)
-        put(gl, j, x * p_right)
-        y = row(dt, i + 1) + m_left * y
-        w = w * m_left
-        z = row(dt, j - 1) + m_right * z
-        x = x * m_right
-    c_left, c_right, c_mid = row(p, half - 1), row(p, half), row(m, half)
-    b_left, b_right = c_left * y + c_mid * z, c_right * z + c_mid * y
-    g_left, g_right = c_left * w, c_mid * w
-    h_left, h_right = c_mid * x, c_right * x
-    for i in range(half - 1, -1, -1):
-        j = ny - 1 - i
-        if i < half - 1:
-            m_left, m_right = row(m, i), row(m, j)
-            b_left = row(b, i) + m_left * b_left
-            g_left = row(g0, i) + m_left * g_left
-            h_left = m_left * h_left
-            b_right = row(b, j) + m_right * b_right
-            g_right = m_right * g_right
-            h_right = row(gl, j) + m_right * h_right
-        put(b, i, b_left)
-        put(g0, i, g_left)
-        put(gl, i, h_left)
-        put(b, j, b_right)
-        put(g0, j, g_right)
-        put(gl, j, h_right)
+    zero = jnp.zeros((8, 128), F32)
+    b0, bl = [zero] * 4, [zero] * 4
+    for j in range(ny):
+        dj = row(dt, j)
+        b0[j % 4] = b0[j % 4] + row(g0, j) * dj
+        bl[j % 4] = bl[j % 4] + row(gl, j) * dj
     root_left, root_right = faces[0:8, :], faces[8:16, :]
     parts = [
-        root_left * root_left * g_left,
-        root_left * root_right * g_right,
-        root_right * root_right * h_right,
-        root_left * b_left,
-        root_right * b_right,
+        root_left * root_left * row(g0, 0),
+        root_left * root_right * row(g0, ny - 1),
+        root_right * root_right * row(gl, ny - 1),
+        root_left * ((b0[0] + b0[1]) + (b0[2] + b0[3])),
+        root_right * ((bl[0] + bl[1]) + (bl[2] + bl[3])),
     ]
     for q, part in enumerate(parts):
         send[q * 8 : (q + 1) * 8, :] = part
 
 
-def join_kernel(mine, other, both):
-    both[0:40, :] = mine[...]
-    both[40:80, :] = other[...]
-
-
-def finish_kernel(nx, peers, *refs):
-    got = refs[: peers // 2]
-    b, g0, gl, u, faces, out, recv, flux, whole, done, sems = refs[peers // 2 :]
+def join_kernel(mine, other, sup, mid):
+    even = lax.rem(lax.axis_index("col"), 2) == 0
+    first, second = [], []
+    for q in range(5):
+        here, there = mine[q * 8 : q * 8 + 8, :], other[q * 8 : q * 8 + 8, :]
+        first.append(jnp.where(even, here, there))
+        second.append(jnp.where(even, there, here))
+    inv = 1.0 / (1.0 + (first[2] + second[0]))
+    f = (second[3] - first[4]) * inv
+    g, h = first[1] * inv, second[1] * inv
+    parts = [
+        first[0] - first[1] * g,
+        first[1] * h,
+        second[2] - second[1] * h,
+        first[3] + first[1] * f,
+        second[4] - second[1] * f,
+    ]
+    for q, part in enumerate(parts):
+        sup[q * 8 : q * 8 + 8, :] = part
+    for q, part in enumerate((f, g, h)):
+        mid[q * 8 : q * 8 + 8, :] = part
+
+
+def finish_kernel(nx, steps, *refs):
+    peers = len(steps)
+    got = refs[:peers]
+    mid, b, g0, gl, u, faces, out, recv, flux, whole, done, sems = refs[peers:]
     col = lax.axis_index("col")
-    for n, ref in zip([0] + [a // 2 for a in [4, 2, 6]], got):
-        recv[lax.rem(col + peers - 2 * n, peers)] = ref[0:40, :]
-        recv[lax.bitwise_xor(lax.rem(col + peers - 2 * n, peers), 1)] = ref[40:80, :]
+    chip = lax.div(col, 2)
+    for step, ref in zip(steps, got):
+        recv[lax.rem(chip + peers - step, peers)] = ref[...]
     nothing = (jnp.zeros((8, 128), F32),) * 5
     low, diag, up, rhs = [], [], [], []
     before = nothing
@@ -425,8 +499,12 @@
     q = solve(low, diag, up, rhs)
     for i in range(peers + 1):
         flux[i] = q[i]
-    left = flux[col] * faces[0:8, :]
-    right = flux[col + 1] * faces[8:16, :]
+    left, right = flux[chip], flux[chip + 1]
+    inner = mid[0:8, :] + mid[8:16, :] * left + mid[16:24, :] * right
+    even = lax.rem(col, 2) == 0
+    left, right = jnp.where(even, left, inner), jnp.where(even, inner, right)
+    left = left * faces[0:8, :]
+    right = right * faces[8:16, :]
     for j in range(b.shape[0] // 8):
         put(whole, j, row(b, j) + (row(gl, j) * right - row(g0, j) * left))
     copies = []
@@ -462,9 +540,9 @@
     up = [(i, (i + 1) % colp) for i in range(colp)]
     from_left = lax.ppermute(high, "col", up)
     from_right = lax.ppermute(low, "col", [(b, a) for a, b in up])
-    mx, px, r, ends, my, py = call(
+    mx, px, g0x, glx, r, ends = call(
         functools.partial(pivots_kernel, nx),
-        [cube] * 2 + [flat, (2, nz, ny)] + [flat] * 2,
+        [cube] * 4 + [flat, (2, nz, ny)],
         (uv, kv, ut, kt),
         1 << 23,
         [flat, flat],
@@ -475,22 +553,23 @@
     for step in range(group):
         inside[step] = [(i, i // group * group + (i + step) % group) for i in range(rowp)]
         across[step] = [(i, (i + step * group) % rowp) for i in range(rowp)]
-    order = sorted(range(1, group), key=lambda step: abs(step - group // 2))
 
     def exchange(arrays, pairs):
-        got = list(arrays)
-        for step in order:
-            got[step] = lax.ppermute(arrays[step], "row", pairs[step])
-        return got
-
-    *parts, bx, g0x, glx, faces = call(
+        return [
+            lax.ppermute(arrays[step], "row", pairs[step]) if step else arrays[0]
+            for step in far_first(group)
+        ]
+
+    *parts, full, faces = call(
         functools.partial(x_send_kernel, nx, colp, group),
-        [(7 * own, ny)] * group + [cube] * 3 + [(16, 128)],
-        (low, high, from_left, from_right, r, ends, mx, px),
+        [(7 * own, ny)] * group + [flat, (16, 128)],
+        (low, high, from_left, from_right, r, ends, g0x, glx),
         1 << 22,
         [(128, 128), (group, 7 * own, ny)],
     )
     parts = exchange(parts, inside)
+    (bx,) = call(functools.partial(x_inner_kernel, nx), [cube], (full, mx, px), 1 << 21)
+    g0y, gly = call(functools.partial(y_columns_kernel, nx), [flat] * 2, (k,), 1 << 23, [flat] * 3)
     merged, inner = call(
         functools.partial(merge_kernel, group),
         [(7 * own, ny), (9 * own, ny)],
@@ -502,29 +581,34 @@
     parts = call(
         functools.partial(flux_kernel, group),
         [(2 * own, ny)] * group,
-        (*parts, inner),
+        (*parts, inner, bx, g0y),
         1 << 20,
         [(group, 7 * own, ny), (group + 1, own, ny), (group, 2 * own, ny)],
     )
     parts = exchange(parts, inside)
-    send, b, g0y, gly = call(
+    send, dt = call(
         functools.partial(y_send_kernel, nx, group),
-        [(40, 128)] + [flat] * 3,
-        (*parts, bx, g0x, glx, u, my, py, faces),
+        [(40, 128), flat],
+        (*parts, bx, g0x, glx, u, g0y, gly, faces),
         1 << 22,
-        [flat, (nz, ny), (nz, ny)],
-    )
+        [(nz, ny), (nz, ny)],
+    )
+    my, py = call(functools.partial(y_pivots_kernel, nx), [flat] * 2, (k, send), 1 << 22, [flat])
+    (b,) = call(y_inner_kernel, [flat], (dt, my, py), 1 << 22)
     other = lax.ppermute(send, "col", [(i, i ^ 1) for i in range(colp)])
-    (both,) = call(join_kernel, [(80, 128)], (send, other), 1 << 16)
-    got = [both]
-    for step in [4, 2, 6]:
-        got.append(lax.ppermute(both, "col", [(i, (i + step) % colp) for i in range(colp)]))
+    sup, mid = call(join_kernel, [(40, 128), (24, 128)], (send, other), 1 << 16)
+    chips = colp // 2
+    steps = [0, 2, 1, 3]
+    got = [
+        lax.ppermute(sup, "col", [(i, (i + 2 * step) % colp) for i in range(colp)]) if step else sup
+        for step in steps
+    ]
     (out,) = call(
-        functools.partial(finish_kernel, nx, colp),
+        functools.partial(finish_kernel, nx, steps),
         [flat],
-        (*got, b, g0y, gly, u, faces),
+        (*got, mid, b, g0y, gly, u, faces),
         1 << 22,
-        [(colp, 40, 128), (colp + 1, 8, 128), flat, flat, pltpu.SemaphoreType.DMA((8,))],
+        [(chips, 40, 128), (chips + 1, 8, 128), flat, flat, pltpu.SemaphoreType.DMA((8,))],
         out_specs=[HBM],
     )
     return out.reshape(nz, nx, ny)

time: 44 us -> 43.1 us (0.980)
  waiting for transfers between devices: 12.4 us -> 10.2 us
  Pallas kernels: 5.52 us -> 7.17 us
    ppermute x12, waiting for transfers between devices: 11.2 us -> 8.54 us  [the longest x9 7.98 us: exchange(): lax.ppermute(arrays[step], 'row', pairs[step])]
    pallas_call x8 -> x12, Pallas kernels: 5.52 us -> 7.17 us  [call(): pl.pallas_call(kernel, out_shape=[jax.ShapeDtypeStruct(s, F32) for s in o...]
    ppermute x1, waiting for transfers between devices: 0.01 us -> 0.46 us  [on_device(): from_left = lax.ppermute(high, 'col', up)]
  transfers between devices with their start and end apart: 15 -> 15, of which waited for: 8 -> 10; matrix products, arithmetic and copies ran while one was open for 0% -> 0% of each run, Pallas kernels for 3% -> 8%
where the time goes in v7:
time: 43.1 us; the launch traced here: 42.6 us
  starting transfers between devices  25.1 us (58%)
  waiting for transfers between devices  10.2 us (24%)
  Pallas kernels  7.17 us (17%)
    ppermute x9, starting transfers between devices, exchange(): lax.ppermute(arrays[step], 'row', pairs[step])  15.5 us
    ppermute x9, waiting for transfers between devices, exchange(): lax.ppermute(arrays[step], 'row', pairs[step])  7.98 us
    pallas_call x12, Pallas kernels, call(): pl.pallas_call(kernel, out_shape=[jax.ShapeDtypeStruct(s, F32) for s in o...  7.17 us
    ppermute x3, starting transfers between devices, on_device(): lax.ppermute(sup, 'col', [(i, (i + 2 * step) % colp) for i in range(colp)])  5.88 us
    ppermute x1, starting transfers between devices, on_device(): from_right = lax.ppermute(low, 'col', [(b, a) for a, b in up])  3.6 us
    ppermute x1, waiting for transfers between devices, on_device(): other = lax.ppermute(send, 'col', [(i, i ^ 1) for i in range(colp)])  1.18 us
  transfers between devices with their start and end apart: 15, of which 10 were waited for; matrix products, arithmetic and copies ran while one was open for 0% of the time, Pallas kernels for 8%

profile of v7, /device:TPU:0, one launch (start us, length us, event | category | flops | bytes accessed | tf_op | source)
XLA Modules:
  0.0 42.6 jit_solution(8943506309661123122)
XLA Ops:
  0.0 1.5 %shard_map.28 = (f32[1024,128]{1,0:T(8,128)S(1)}, f32[1024,128]{1,0:T(8,128)S(1)}, f32[1024,128]{1,0:T(8,128)S(1)}, f32[1024,128]{1,0:T(8,128)S(1)}, f32[16,128]{1,0:T(8,128)S(1)}, /*index=5*/f32[16,128]{1,0:T(8,128)S(1)}) custom-call(f32[1024,128]{1,0:T(8,128)} %bitcast.6, f32[1024,128]{1,0:T(8,128)} %bitcast.3), custom_call_target="tpu_custom_call" | custom-call | flops 1048576 | bytes 1048576 | tf_op jit(solution)/shard_map/pallas_call | solution.py:18
  1.6 3.6 %collective-permute-start.1 = (f32[16,128]{1,0:T(8,128)S(1)}, f32[16,128]{1,0:T(8,128)S(1)}, u32[]{:S(2)}, u32[]{:S(2)}) collective-permute-start(f32[16,128]{1,0:T(8,128)S(1)} %get-tuple-element.37.low), channel_id=1, source_target_pairs={{1,0},{2,1},{3,2},{4,3},{5,4},{6,5},{7,6},{0,7},{9,8},{10,9},{11,1... | collective-permute-start | bytes 24584 | tf_op jit(solution)/shard_map/ppermute | solution.py:542
  5.2 0.8 %shard_map.29 = (f32[16,64,128]{2,1,0:T(8,128)S(1)}, f32[16,64,128]{2,1,0:T(8,128)S(1)}, f32[16,64,128]{2,1,0:T(8,128)S(1)}, f32[16,64,128]{2,1,0:T(8,128)S(1)},...) custom-call(f32[1024,128]{1,0:T(8,128)S(1)} %get-tuple-element.39.u, f32[1024,128]{1,0:T(8,128)S(1)} %get-tuple-element.40.k, ...), custom_call_target="tpu_custom_call" | custom-call | flops 8388608 | bytes 1048576 | tf_op jit(solution)/shard_map/pallas_call | solution.py:18
  6.5 0.5 %shard_map.30 = (f32[112,128]{1,0:T(8,128)S(1)}, f32[112,128]{1,0:T(8,128)S(1)}, f32[112,128]{1,0:T(8,128)S(1)}, f32[112,128]{1,0:T(8,128)S(1)}, f32[1024,128]{1,0:T(8,128)S(1)}, /*index=5*/f32[16,128]{1,0:T(8,128)S(1)}) custom-call(f32[16,128]{1,0:T(8,128)S(1)} %get-tuple-element.37.low, f32[16,128]{1,0:T(8,128)S(1)} %get-tuple-element.38.high, ...), custom_call_target="tpu_custom_call" | custom-call | flops 4194304 | bytes 1048576 | tf_op jit(solution)/shard_map/pallas_call | solution.py:18
  7.1 1.6 %collective-permute-start.2 = (f32[112,128]{1,0:T(8,128)S(1)}, f32[112,128]{1,0:T(8,128)S(1)}, u32[]{:S(2)}, u32[]{:S(2)}) collective-permute-start(f32[112,128]{1,0:T(8,128)S(1)} %get-tuple-element.48), channel_id=1, source_target_pairs={{0,8},{8,16},{16,24},{24,0},{32,40},{40,48},{48,56},{56,32},{64,72... | collective-permute-start | bytes 172040 | tf_op jit(solution)/shard_map/ppermute | solution.py:559
  8.6 1.7 %collective-permute-start.3 = (f32[112,128]{1,0:T(8,128)S(1)}, f32[112,128]{1,0:T(8,128)S(1)}, u32[]{:S(2)}, u32[]{:S(2)}) collective-permute-start(f32[112,128]{1,0:T(8,128)S(1)} %get-tuple-element.49), channel_id=1, source_target_pairs={{0,24},{8,0},{16,8},{24,16},{32,56},{40,32},{48,40},{56,48},{64,88... | collective-permute-start | bytes 172040 | tf_op jit(solution)/shard_map/ppermute | solution.py:559
  10.4 1.8 %collective-permute-start.4 = (f32[112,128]{1,0:T(8,128)S(1)}, f32[112,128]{1,0:T(8,128)S(1)}, u32[]{:S(2)}, u32[]{:S(2)}) collective-permute-start(f32[112,128]{1,0:T(8,128)S(1)} %get-tuple-element.50), channel_id=1, source_target_pairs={{0,16},{8,24},{16,0},{24,8},{32,48},{40,56},{48,32},{56,40},{64,80... | collective-permute-start | bytes 172040 | tf_op jit(solution)/shard_map/ppermute | solution.py:559
  12.8 3.2 %collective-permute-done.4.refs_3_ = f32[112,128]{1,0:T(8,128)S(1)} collective-permute-done((f32[112,128]{1,0:T(8,128)S(1)}, f32[112,128]{1,0:T(8,128)S(1)}, u32[]{:S(2)}, u32[]{:S(2)}) %collective-permute-start.4) | collective-permute-done | bytes 57376 | tf_op jit(solution)/shard_map/ppermute | solution.py:559
  16.1 1.6 %collective-permute-start.5 = (f32[112,128]{1,0:T(8,128)S(1)}, f32[112,128]{1,0:T(8,128)S(1)}, u32[]{:S(2)}, u32[]{:S(2)}) collective-permute-start(f32[112,128]{1,0:T(8,128)S(1)} %get-tuple-element.51.refs_0_), channel_id=1, source_target_pairs={{0,32},{8,40},{16,48},{24,56},{32,64},{40,72},{48,80},{56,88},{64,... | collective-permute-start | bytes 172040 | tf_op jit(solution)/shard_map/ppermute | solution.py:559
  17.8 1.7 %collective-permute-start.6 = (f32[112,128]{1,0:T(8,128)S(1)}, f32[112,128]{1,0:T(8,128)S(1)}, u32[]{:S(2)}, u32[]{:S(2)}) collective-permute-start(f32[112,128]{1,0:T(8,128)S(1)} %get-tuple-element.51.refs_0_), channel_id=1, source_target_pairs={{0,96},{8,104},{16,112},{24,120},{32,0},{40,8},{48,16},{56,24},{64... | collective-permute-start | bytes 172040 | tf_op jit(solution)/shard_map/ppermute | solution.py:559
  19.4 2.0 %collective-permute-start.7 = (f32[112,128]{1,0:T(8,128)S(1)}, f32[112,128]{1,0:T(8,128)S(1)}, u32[]{:S(2)}, u32[]{:S(2)}) collective-permute-start(f32[112,128]{1,0:T(8,128)S(1)} %get-tuple-element.51.refs_0_), channel_id=1, source_target_pairs={{0,64},{8,72},{16,80},{24,88},{32,96},{40,104},{48,112},{56,120},{... | collective-permute-start | bytes 172040 | tf_op jit(solution)/shard_map/ppermute | solution.py:559
  21.4 1.1 %shard_map.33 = (f32[1024,128]{1,0:T(8,128)S(1)}, f32[1024,128]{1,0:T(8,128)S(1)}) custom-call(f32[1024,128]{1,0:T(8,128)S(1)} %bitcast.4), custom_call_target="tpu_custom_call" | custom-call | flops 8388608 | bytes 1048576 | tf_op jit(solution)/shard_map/pallas_call | solution.py:18
  22.7 2.4 %collective-permute-done.7.refs_3_ = f32[112,128]{1,0:T(8,128)S(1)} collective-permute-done((f32[112,128]{1,0:T(8,128)S(1)}, f32[112,128]{1,0:T(8,128)S(1)}, u32[]{:S(2)}, u32[]{:S(2)}) %collective-permute-start.7) | collective-permute-done | bytes 57376 | tf_op jit(solution)/shard_map/ppermute | solution.py:559
  25.2 1.9 %collective-permute-start.10 = (f32[32,128]{1,0:T(8,128)S(1)}, f32[32,128]{1,0:T(8,128)S(1)}, u32[]{:S(2)}, u32[]{:S(2)}) collective-permute-start(f32[32,128]{1,0:T(8,128)S(1)} %get-tuple-element.60), channel_id=1, source_target_pairs={{0,16},{8,24},{16,0},{24,8},{32,48},{40,56},{48,32},{56,40},{64,80... | collective-permute-start | bytes 49160 | tf_op jit(solution)/shard_map/ppermute | solution.py:559
  27.1 0.6 %collective-permute-start.8 = (f32[32,128]{1,0:T(8,128)S(1)}, f32[32,128]{1,0:T(8,128)S(1)}, u32[]{:S(2)}, u32[]{:S(2)}) collective-permute-start(f32[32,128]{1,0:T(8,128)S(1)} %get-tuple-element.58), channel_id=1, source_target_pairs={{0,8},{8,16},{16,24},{24,0},{32,40},{40,48},{48,56},{56,32},{64,72... | collective-permute-start | bytes 49160 | tf_op jit(solution)/shard_map/ppermute | solution.py:559
  27.7 2.6 %collective-permute-start.9 = (f32[32,128]{1,0:T(8,128)S(1)}, f32[32,128]{1,0:T(8,128)S(1)}, u32[]{:S(2)}, u32[]{:S(2)}) collective-permute-start(f32[32,128]{1,0:T(8,128)S(1)} %get-tuple-element.59), channel_id=1, source_target_pairs={{0,24},{8,0},{16,8},{24,16},{32,56},{40,32},{48,40},{56,48},{64,88... | collective-permute-start | bytes 49160 | tf_op jit(solution)/shard_map/ppermute | solution.py:559
  30.5 1.5 %collective-permute-done.8.refs_1_ = f32[32,128]{1,0:T(8,128)S(1)} collective-permute-done((f32[32,128]{1,0:T(8,128)S(1)}, f32[32,128]{1,0:T(8,128)S(1)}, u32[]{:S(2)}, u32[]{:S(2)}) %collective-permute-start.8) | collective-permute-done | bytes 16416 | tf_op jit(solution)/shard_map/ppermute | solution.py:559
  32.6 1.2 %collective-permute-done.11.other = f32[40,128]{1,0:T(8,128)S(1)} collective-permute-done((f32[40,128]{1,0:T(8,128)S(1)}, f32[40,128]{1,0:T(8,128)S(1)}, u32[]{:S(2)}, u32[]{:S(2)}) %collective-permute-start.11) | collective-permute-done | bytes 20512 | tf_op jit(solution)/shard_map/ppermute | solution.py:598
  33.8 2.6 %collective-permute-start.12 = (f32[40,128]{1,0:T(8,128)S(1)}, f32[40,128]{1,0:T(8,128)S(1)}, u32[]{:S(2)}, u32[]{:S(2)}) collective-permute-start(f32[40,128]{1,0:T(8,128)S(1)} %get-tuple-element.64.refs_0_), channel_id=1, source_target_pairs={{0,4},{1,5},{2,6},{3,7},{4,0},{5,1},{6,2},{7,3},{8,12},{9,13},{10,... | collective-permute-start | bytes 61448 | tf_op jit(solution)/shard_map/ppermute | solution.py:603
  36.4 0.7 %collective-permute-start.13 = (f32[40,128]{1,0:T(8,128)S(1)}, f32[40,128]{1,0:T(8,128)S(1)}, u32[]{:S(2)}, u32[]{:S(2)}) collective-permute-start(f32[40,128]{1,0:T(8,128)S(1)} %get-tuple-element.64.refs_0_), channel_id=1, source_target_pairs={{0,2},{1,3},{2,4},{3,5},{4,6},{5,7},{6,0},{7,1},{8,10},{9,11},{10,... | collective-permute-start | bytes 61448 | tf_op jit(solution)/shard_map/ppermute | solution.py:603
  37.1 2.5 %collective-permute-start.14 = (f32[40,128]{1,0:T(8,128)S(1)}, f32[40,128]{1,0:T(8,128)S(1)}, u32[]{:S(2)}, u32[]{:S(2)}) collective-permute-start(f32[40,128]{1,0:T(8,128)S(1)} %get-tuple-element.64.refs_0_), channel_id=1, source_target_pairs={{0,6},{1,7},{2,0},{3,1},{4,2},{5,3},{6,4},{7,5},{8,14},{9,15},{10,... | collective-permute-start | bytes 61448 | tf_op jit(solution)/shard_map/ppermute | solution.py:603
  39.7 0.9 %shard_map.37 = (f32[1024,128]{1,0:T(8,128)S(1)}, f32[1024,128]{1,0:T(8,128)S(1)}) custom-call(f32[1024,128]{1,0:T(8,128)S(1)} %bitcast.5, f32[40,128]{1,0:T(8,128)S(1)} %get-tuple-element.63.mine.ready), custom_call_target="tpu_custom_call" | custom-call | flops 4194304 | bytes 1048576 | tf_op jit(solution)/shard_map/pallas_call | solution.py:18
  40.9 0.6 %collective-permute-done.13.refs_2_ = f32[40,128]{1,0:T(8,128)S(1)} collective-permute-done((f32[40,128]{1,0:T(8,128)S(1)}, f32[40,128]{1,0:T(8,128)S(1)}, u32[]{:S(2)}, u32[]{:S(2)}) %collective-permute-start.13) | collective-permute-done | bytes 20512 | tf_op jit(solution)/shard_map/ppermute | solution.py:603
  41.4 1.2 %shard_map.39 = f32[1024,128]{1,0:T(8,128)} custom-call(f32[40,128]{1,0:T(8,128)S(1)} %get-tuple-element.64.refs_0_, f32[40,128]{1,0:T(8,128)S(1)} %collective-permute-done.12.refs_1_, f32[40,128]{1,0:T(8,128)S(1)} %collective-permute-done.13.refs_2_, f32[40,128]{1,0:T(8,128)S(1)} %collective-permute-done.14.refs_3_, ...), custom_call_target="tpu_custom_call" | custom-call | flops 4194304 | bytes 1048576 | tf_op jit(solution)/shard_map/pallas_call | solution.py:18
  (22 shorter events, 2.5 us)
Async XLA Ops:
  1.6 4.9 %collective-permute-start = (f32[16,128]{1,0:T(8,128)S(1)}, f32[16,128]{1,0:T(8,128)S(1)}, u32[]{:S(2)}, u32[]{:S(2)}) collective-permute-start(f32[16,128]{1,0:T(8,128)S(1)} %get-tuple-element.38.high), channel_id=1, source_target_pairs={{0,1},{1,2},{2,3},{3,4},{4,5},{5,6},{6,7},{7,0},{8,9},{9,10},{10,1... | collective-permute-start | bytes 24584 | tf_op jit(solution)/shard_map/ppermute | solution.py:541
  1.6 5.0 %collective-permute-start.1 = (f32[16,128]{1,0:T(8,128)S(1)}, f32[16,128]{1,0:T(8,128)S(1)}, u32[]{:S(2)}, u32[]{:S(2)}) collective-permute-start(f32[16,128]{1,0:T(8,128)S(1)} %get-tuple-element.37.low), channel_id=1, source_target_pairs={{1,0},{2,1},{3,2},{4,3},{5,4},{6,5},{7,6},{0,7},{9,8},{10,9},{11,1... | collective-permute-start | bytes 24584 | tf_op jit(solution)/shard_map/ppermute | solution.py:542
  6.5 14.9 %copy-start = (f32[64,16,128]{2,1,0:T(8,128)S(1)}, f32[64,16,128]{2,1,0:T(8,128)}, u32[]{:S(2)}) copy-start(f32[64,16,128]{2,1,0:T(8,128)} %param.3) | copy-start | bytes 1572868
  7.1 5.5 %collective-permute-start.2 = (f32[112,128]{1,0:T(8,128)S(1)}, f32[112,128]{1,0:T(8,128)S(1)}, u32[]{:S(2)}, u32[]{:S(2)}) collective-permute-start(f32[112,128]{1,0:T(8,128)S(1)} %get-tuple-element.48), channel_id=1, source_target_pairs={{0,8},{8,16},{16,24},{24,0},{32,40},{40,48},{48,56},{56,32},{64,72... | collective-permute-start | bytes 172040 | tf_op jit(solution)/shard_map/ppermute | solution.py:559
  8.6 4.2 %collective-permute-start.3 = (f32[112,128]{1,0:T(8,128)S(1)}, f32[112,128]{1,0:T(8,128)S(1)}, u32[]{:S(2)}, u32[]{:S(2)}) collective-permute-start(f32[112,128]{1,0:T(8,128)S(1)} %get-tuple-element.49), channel_id=1, source_target_pairs={{0,24},{8,0},{16,8},{24,16},{32,56},{40,32},{48,40},{56,48},{64,88... | collective-permute-start | bytes 172040 | tf_op jit(solution)/shard_map/ppermute | solution.py:559
  10.4 5.7 %collective-permute-start.4 = (f32[112,128]{1,0:T(8,128)S(1)}, f32[112,128]{1,0:T(8,128)S(1)}, u32[]{:S(2)}, u32[]{:S(2)}) collective-permute-start(f32[112,128]{1,0:T(8,128)S(1)} %get-tuple-element.50), channel_id=1, source_target_pairs={{0,16},{8,24},{16,0},{24,8},{32,48},{40,56},{48,32},{56,40},{64,80... | collective-permute-start | bytes 172040 | tf_op jit(solution)/shard_map/ppermute | solution.py:559
  16.1 6.6 %collective-permute-start.5 = (f32[112,128]{1,0:T(8,128)S(1)}, f32[112,128]{1,0:T(8,128)S(1)}, u32[]{:S(2)}, u32[]{:S(2)}) collective-permute-start(f32[112,128]{1,0:T(8,128)S(1)} %get-tuple-element.51.refs_0_), channel_id=1, source_target_pairs={{0,32},{8,40},{16,48},{24,56},{32,64},{40,72},{48,80},{56,88},{64,... | collective-permute-start | bytes 172040 | tf_op jit(solution)/shard_map/ppermute | solution.py:559
  17.8 4.9 %collective-permute-start.6 = (f32[112,128]{1,0:T(8,128)S(1)}, f32[112,128]{1,0:T(8,128)S(1)}, u32[]{:S(2)}, u32[]{:S(2)}) collective-permute-start(f32[112,128]{1,0:T(8,128)S(1)} %get-tuple-element.51.refs_0_), channel_id=1, source_target_pairs={{0,96},{8,104},{16,112},{24,120},{32,0},{40,8},{48,16},{56,24},{64... | collective-permute-start | bytes 172040 | tf_op jit(solution)/shard_map/ppermute | solution.py:559
  19.4 5.7 %collective-permute-start.7 = (f32[112,128]{1,0:T(8,128)S(1)}, f32[112,128]{1,0:T(8,128)S(1)}, u32[]{:S(2)}, u32[]{:S(2)}) collective-permute-start(f32[112,128]{1,0:T(8,128)S(1)} %get-tuple-element.51.refs_0_), channel_id=1, source_target_pairs={{0,64},{8,72},{16,80},{24,88},{32,96},{40,104},{48,112},{56,120},{... | collective-permute-start | bytes 172040 | tf_op jit(solution)/shard_map/ppermute | solution.py:559
  25.1 6.9 %copy-start.1 = (f32[64,16,128]{2,1,0:T(8,128)S(1)}, f32[64,16,128]{2,1,0:T(8,128)}, u32[]{:S(2)}) copy-start(f32[64,16,128]{2,1,0:T(8,128)} %param.2) | copy-start | bytes 1572868
  25.2 5.3 %collective-permute-start.10 = (f32[32,128]{1,0:T(8,128)S(1)}, f32[32,128]{1,0:T(8,128)S(1)}, u32[]{:S(2)}, u32[]{:S(2)}) collective-permute-start(f32[32,128]{1,0:T(8,128)S(1)} %get-tuple-element.60), channel_id=1, source_target_pairs={{0,16},{8,24},{16,0},{24,8},{32,48},{40,56},{48,32},{56,40},{64,80... | collective-permute-start | bytes 49160 | tf_op jit(solution)/shard_map/ppermute | solution.py:559
  27.1 4.9 %collective-permute-start.8 = (f32[32,128]{1,0:T(8,128)S(1)}, f32[32,128]{1,0:T(8,128)S(1)}, u32[]{:S(2)}, u32[]{:S(2)}) collective-permute-start(f32[32,128]{1,0:T(8,128)S(1)} %get-tuple-element.58), channel_id=1, source_target_pairs={{0,8},{8,16},{16,24},{24,0},{32,40},{40,48},{48,56},{56,32},{64,72... | collective-permute-start | bytes 49160 | tf_op jit(solution)/shard_map/ppermute | solution.py:559
  27.7 4.4 %collective-permute-start.9 = (f32[32,128]{1,0:T(8,128)S(1)}, f32[32,128]{1,0:T(8,128)S(1)}, u32[]{:S(2)}, u32[]{:S(2)}) collective-permute-start(f32[32,128]{1,0:T(8,128)S(1)} %get-tuple-element.59), channel_id=1, source_target_pairs={{0,24},{8,0},{16,8},{24,16},{32,56},{40,32},{48,40},{56,48},{64,88... | collective-permute-start | bytes 49160 | tf_op jit(solution)/shard_map/ppermute | solution.py:559
  32.5 1.3 %collective-permute-start.11 = (f32[40,128]{1,0:T(8,128)S(1)}, f32[40,128]{1,0:T(8,128)S(1)}, u32[]{:S(2)}, u32[]{:S(2)}) collective-permute-start(f32[40,128]{1,0:T(8,128)S(1)} %get-tuple-element.63.mine.ready), channel_id=1, source_target_pairs={{0,1},{1,0},{2,3},{3,2},{4,5},{5,4},{6,7},{7,6},{8,9},{9,8},{10,11... | collective-permute-start | bytes 61448 | tf_op jit(solution)/shard_map/ppermute | solution.py:598
  33.8 7.1 %collective-permute-start.12 = (f32[40,128]{1,0:T(8,128)S(1)}, f32[40,128]{1,0:T(8,128)S(1)}, u32[]{:S(2)}, u32[]{:S(2)}) collective-permute-start(f32[40,128]{1,0:T(8,128)S(1)} %get-tuple-element.64.refs_0_), channel_id=1, source_target_pairs={{0,4},{1,5},{2,6},{3,7},{4,0},{5,1},{6,2},{7,3},{8,12},{9,13},{10,... | collective-permute-start | bytes 61448 | tf_op jit(solution)/shard_map/ppermute | solution.py:603
  36.4 5.0 %collective-permute-start.13 = (f32[40,128]{1,0:T(8,128)S(1)}, f32[40,128]{1,0:T(8,128)S(1)}, u32[]{:S(2)}, u32[]{:S(2)}) collective-permute-start(f32[40,128]{1,0:T(8,128)S(1)} %get-tuple-element.64.refs_0_), channel_id=1, source_target_pairs={{0,2},{1,3},{2,4},{3,5},{4,6},{5,7},{6,0},{7,1},{8,10},{9,11},{10,... | collective-permute-start | bytes 61448 | tf_op jit(solution)/shard_map/ppermute | solution.py:603
  37.1 4.3 %collective-permute-start.14 = (f32[40,128]{1,0:T(8,128)S(1)}, f32[40,128]{1,0:T(8,128)S(1)}, u32[]{:S(2)}, u32[]{:S(2)}) collective-permute-start(f32[40,128]{1,0:T(8,128)S(1)} %get-tuple-element.64.refs_0_), channel_id=1, source_target_pairs={{0,6},{1,7},{2,0},{3,1},{4,2},{5,3},{6,4},{7,5},{8,14},{9,15},{10,... | collective-permute-start | bytes 61448 | tf_op jit(solution)/shard_map/ppermute | solution.py:603

commit v8 on v7

--- a/solution.py
+++ b/solution.py
@@ -333,8 +333,8 @@
     return q
 
 
-def far_first(group):
-    return [0] + [1, 3, 2]
+def shift_order(group):
+    return [1, 3, 2, 0]
 
 
 def system(blocks, nothing):
@@ -352,7 +352,7 @@
     got, sup, inner, recv = refs[:group], refs[group], refs[group + 1], refs[group + 2]
     own = sup.shape[0] // 7
     mine = lax.rem(lax.axis_index("row"), group)
-    for step, ref in zip(far_first(group), got):
+    for step, ref in zip(shift_order(group), got):
         recv[lax.rem(mine + group - step, group)] = ref[...]
     blocks = [tuple(recv[d, q * own : (q + 1) * own, :] for q in range(7)) for d in range(group)]
     low, diag, up, rhs = system(blocks, blocks[0])
@@ -390,7 +390,7 @@
     own = got[0].shape[0] // 7
     row_index = lax.axis_index("row")
     mine, outer = lax.rem(row_index, group), lax.div(row_index, group)
-    for step, ref in zip(far_first(group), got):
+    for step, ref in zip(shift_order(group), got):
         recv[lax.rem(outer + group - step, group)] = ref[...]
     blocks = [tuple(recv[d, q * own : (q + 1) * own, :] for q in range(7)) for d in range(group)]
     q = solve(*system(blocks, (jnp.zeros((own, 128), F32),) * 7))
@@ -418,7 +418,7 @@
     own = got[0].shape[0] // 2
     ny = dt.shape[0] // 8
     mine = lax.rem(lax.axis_index("row"), group)
-    for step, ref in zip(far_first(group), got):
+    for step, ref in zip(shift_order(group), got):
         start = pl.multiple_of(lax.rem(mine + group - step, group) * own, own)
         ql[pl.ds(start, own), :] = ref[0:own, :]
         qr[pl.ds(start, own), :] = ref[own : 2 * own, :]
@@ -551,13 +551,17 @@
     own = nz // group
     inside, across = {}, {}
     for step in range(group):
-        inside[step] = [(i, i // group * group + (i + step) % group) for i in range(rowp)]
+        inside[step] = [
+            (i * colp + c, (i // group * group + (i + step) % group) * colp + (c ^ 1))
+            for i in range(rowp)
+            for c in range(colp)
+        ]
         across[step] = [(i, (i + step * group) % rowp) for i in range(rowp)]
 
-    def exchange(arrays, pairs):
+    def exchange(arrays, pairs, axes):
         return [
-            lax.ppermute(arrays[step], "row", pairs[step]) if step else arrays[0]
-            for step in far_first(group)
+            lax.ppermute(arrays[step], axes, pairs[step]) if step or axes != "row" else arrays[0]
+            for step in shift_order(group)
         ]
 
     *parts, full, faces = call(
@@ -567,7 +571,7 @@
         1 << 22,
         [(128, 128), (group, 7 * own, ny)],
     )
-    parts = exchange(parts, inside)
+    parts = exchange(parts, inside, ("row", "col"))
     (bx,) = call(functools.partial(x_inner_kernel, nx), [cube], (full, mx, px), 1 << 21)
     g0y, gly = call(functools.partial(y_columns_kernel, nx), [flat] * 2, (k,), 1 << 23, [flat] * 3)
     merged, inner = call(
@@ -577,7 +581,7 @@
         1 << 20,
         [(group, 7 * own, ny)],
     )
-    parts = exchange([merged] * group, across)
+    parts = exchange([merged] * group, across, "row")
     parts = call(
         functools.partial(flux_kernel, group),
         [(2 * own, ny)] * group,
@@ -585,7 +589,7 @@
         1 << 20,
         [(group, 7 * own, ny), (group + 1, own, ny), (group, 2 * own, ny)],
     )
-    parts = exchange(parts, inside)
+    parts = exchange(parts, inside, ("row", "col"))
     send, dt = call(
         functools.partial(y_send_kernel, nx, group),
         [(40, 128), flat],

time: 43.1 us -> 42.3 us (0.981)
  starting transfers between devices: 25.1 us -> 23.7 us
  waiting for transfers between devices: 10.2 us -> 11.3 us
    ppermute x9 -> x11, starting transfers between devices: 15.5 us -> 13.4 us  [exchange(): lax.ppermute(arrays[step], axes, pairs[step])]
    ppermute x9 -> x11, waiting for transfers between devices: 7.98 us -> 9.31 us  [exchange(): lax.ppermute(arrays[step], axes, pairs[step])]
  transfers between devices with their start and end apart: 15 -> 17, of which waited for: 10 -> 11; matrix products, arithmetic and copies ran while one was open for 0% -> 0% of each run, Pallas kernels for 8% -> 8%
where the time goes in v8:
time: 42.3 us; the launch traced here: 42.2 us
  starting transfers between devices  23.7 us (56%)
  waiting for transfers between devices  11.3 us (27%)
  Pallas kernels  7.16 us (17%)
    ppermute x11, starting transfers between devices, exchange(): lax.ppermute(arrays[step], axes, pairs[step])  13.4 us
    ppermute x11, waiting for transfers between devices, exchange(): lax.ppermute(arrays[step], axes, pairs[step])  9.31 us
    pallas_call x12, Pallas kernels, call(): pl.pallas_call(kernel, out_shape=[jax.ShapeDtypeStruct(s, F32) for s in o...  7.16 us
    ppermute x3, starting transfers between devices, on_device(): lax.ppermute(sup, 'col', [(i, (i + 2 * step) % colp) for i in range(colp)])  6.29 us
    ppermute x1, starting transfers between devices, on_device(): from_right = lax.ppermute(low, 'col', [(b, a) for a, b in up])  3.6 us
    ppermute x1, waiting for transfers between devices, on_device(): other = lax.ppermute(send, 'col', [(i, i ^ 1) for i in range(colp)])  0.86 us
  transfers between devices with their start and end apart: 17, of which 11 were waited for; matrix products, arithmetic and copies ran while one was open for 0% of the time, Pallas kernels for 8%

profile of v8, /device:TPU:0, one launch (start us, length us, event | category | flops | bytes accessed | tf_op | source)
XLA Modules:
  0.0 42.2 jit_solution(14751965461627811348)
XLA Ops:
  0.0 1.5 %shard_map.28 = (f32[1024,128]{1,0:T(8,128)S(1)}, f32[1024,128]{1,0:T(8,128)S(1)}, f32[1024,128]{1,0:T(8,128)S(1)}, f32[1024,128]{1,0:T(8,128)S(1)}, f32[16,128]{1,0:T(8,128)S(1)}, /*index=5*/f32[16,128]{1,0:T(8,128)S(1)}) custom-call(f32[1024,128]{1,0:T(8,128)} %bitcast.6, f32[1024,128]{1,0:T(8,128)} %bitcast.3), custom_call_target="tpu_custom_call" | custom-call | flops 1048576 | bytes 1048576 | tf_op jit(solution)/shard_map/pallas_call | solution.py:18
  1.6 3.6 %collective-permute-start.1 = (f32[16,128]{1,0:T(8,128)S(1)}, f32[16,128]{1,0:T(8,128)S(1)}, u32[]{:S(2)}, u32[]{:S(2)}) collective-permute-start(f32[16,128]{1,0:T(8,128)S(1)} %get-tuple-element.37.low), channel_id=1, source_target_pairs={{1,0},{2,1},{3,2},{4,3},{5,4},{6,5},{7,6},{0,7},{9,8},{10,9},{11,1... | collective-permute-start | bytes 24584 | tf_op jit(solution)/shard_map/ppermute | solution.py:542
  5.2 0.8 %shard_map.29 = (f32[16,64,128]{2,1,0:T(8,128)S(1)}, f32[16,64,128]{2,1,0:T(8,128)S(1)}, f32[16,64,128]{2,1,0:T(8,128)S(1)}, f32[16,64,128]{2,1,0:T(8,128)S(1)},...) custom-call(f32[1024,128]{1,0:T(8,128)S(1)} %get-tuple-element.39.u, f32[1024,128]{1,0:T(8,128)S(1)} %get-tuple-element.40.k, ...), custom_call_target="tpu_custom_call" | custom-call | flops 8388608 | bytes 1048576 | tf_op jit(solution)/shard_map/pallas_call | solution.py:18
  6.0 0.5 %collective-permute-done.from_left = f32[16,128]{1,0:T(8,128)S(1)} collective-permute-done((f32[16,128]{1,0:T(8,128)S(1)}, f32[16,128]{1,0:T(8,128)S(1)}, u32[]{:S(2)}, u32[]{:S(2)}) %collective-permute-start) | collective-permute-done | bytes 8224 | tf_op jit(solution)/shard_map/ppermute | solution.py:541
  6.5 0.5 %shard_map.30 = (f32[112,128]{1,0:T(8,128)S(1)}, f32[112,128]{1,0:T(8,128)S(1)}, f32[112,128]{1,0:T(8,128)S(1)}, f32[112,128]{1,0:T(8,128)S(1)}, f32[1024,128]{1,0:T(8,128)S(1)}, /*index=5*/f32[16,128]{1,0:T(8,128)S(1)}) custom-call(f32[16,128]{1,0:T(8,128)S(1)} %get-tuple-element.37.low, f32[16,128]{1,0:T(8,128)S(1)} %get-tuple-element.38.high, ...), custom_call_target="tpu_custom_call" | custom-call | flops 4194304 | bytes 1048576 | tf_op jit(solution)/shard_map/pallas_call | solution.py:18
  7.1 1.4 %collective-permute-start.2 = (f32[112,128]{1,0:T(8,128)S(1)}, f32[112,128]{1,0:T(8,128)S(1)}, u32[]{:S(2)}, u32[]{:S(2)}) collective-permute-start(f32[112,128]{1,0:T(8,128)S(1)} %get-tuple-element.47), channel_id=1, source_target_pairs={{0,9},{1,8},{2,11},{3,10},{4,13},{5,12},{6,15},{7,14},{8,17},{9,16... | collective-permute-start | bytes 172040 | tf_op jit(solution)/shard_map/ppermute | solution.py:563
  8.5 1.6 %collective-permute-start.3 = (f32[112,128]{1,0:T(8,128)S(1)}, f32[112,128]{1,0:T(8,128)S(1)}, u32[]{:S(2)}, u32[]{:S(2)}) collective-permute-start(f32[112,128]{1,0:T(8,128)S(1)} %get-tuple-element.48), channel_id=1, source_target_pairs={{0,25},{1,24},{2,27},{3,26},{4,29},{5,28},{6,31},{7,30},{8,1},{9,0... | collective-permute-start | bytes 172040 | tf_op jit(solution)/shard_map/ppermute | solution.py:563
  10.1 1.7 %collective-permute-start.4 = (f32[112,128]{1,0:T(8,128)S(1)}, f32[112,128]{1,0:T(8,128)S(1)}, u32[]{:S(2)}, u32[]{:S(2)}) collective-permute-start(f32[112,128]{1,0:T(8,128)S(1)} %get-tuple-element.49), channel_id=1, source_target_pairs={{0,17},{1,16},{2,19},{3,18},{4,21},{5,20},{6,23},{7,22},{8,25},{9,... | collective-permute-start | bytes 172040 | tf_op jit(solution)/shard_map/ppermute | solution.py:563
  12.2 3.2 %collective-permute-done.4.refs_2_ = f32[112,128]{1,0:T(8,128)S(1)} collective-permute-done((f32[112,128]{1,0:T(8,128)S(1)}, f32[112,128]{1,0:T(8,128)S(1)}, u32[]{:S(2)}, u32[]{:S(2)}) %collective-permute-start.4) | collective-permute-done | bytes 57376 | tf_op jit(solution)/shard_map/ppermute | solution.py:563
  15.5 1.6 %collective-permute-start.6 = (f32[112,128]{1,0:T(8,128)S(1)}, f32[112,128]{1,0:T(8,128)S(1)}, u32[]{:S(2)}, u32[]{:S(2)}) collective-permute-start(f32[112,128]{1,0:T(8,128)S(1)} %get-tuple-element.51.refs_3_), channel_id=1, source_target_pairs={{0,32},{8,40},{16,48},{24,56},{32,64},{40,72},{48,80},{56,88},{64,... | collective-permute-start | bytes 172040 | tf_op jit(solution)/shard_map/ppermute | solution.py:563
  17.1 1.7 %collective-permute-start.7 = (f32[112,128]{1,0:T(8,128)S(1)}, f32[112,128]{1,0:T(8,128)S(1)}, u32[]{:S(2)}, u32[]{:S(2)}) collective-permute-start(f32[112,128]{1,0:T(8,128)S(1)} %get-tuple-element.51.refs_3_), channel_id=1, source_target_pairs={{0,96},{8,104},{16,112},{24,120},{32,0},{40,8},{48,16},{56,24},{64... | collective-permute-start | bytes 172040 | tf_op jit(solution)/shard_map/ppermute | solution.py:563
  18.8 2.0 %collective-permute-start.8 = (f32[112,128]{1,0:T(8,128)S(1)}, f32[112,128]{1,0:T(8,128)S(1)}, u32[]{:S(2)}, u32[]{:S(2)}) collective-permute-start(f32[112,128]{1,0:T(8,128)S(1)} %get-tuple-element.51.refs_3_), channel_id=1, source_target_pairs={{0,64},{8,72},{16,80},{24,88},{32,96},{40,104},{48,112},{56,120},{... | collective-permute-start | bytes 172040 | tf_op jit(solution)/shard_map/ppermute | solution.py:563
  20.7 1.1 %shard_map.33 = (f32[1024,128]{1,0:T(8,128)S(1)}, f32[1024,128]{1,0:T(8,128)S(1)}) custom-call(f32[1024,128]{1,0:T(8,128)S(1)} %bitcast.4), custom_call_target="tpu_custom_call" | custom-call | flops 8388608 | bytes 1048576 | tf_op jit(solution)/shard_map/pallas_call | solution.py:18
  22.1 2.4 %collective-permute-done.8.refs_2_ = f32[112,128]{1,0:T(8,128)S(1)} collective-permute-done((f32[112,128]{1,0:T(8,128)S(1)}, f32[112,128]{1,0:T(8,128)S(1)}, u32[]{:S(2)}, u32[]{:S(2)}) %collective-permute-start.8) | collective-permute-done | bytes 57376 | tf_op jit(solution)/shard_map/ppermute | solution.py:563
  24.6 2.1 %collective-permute-start.11 = (f32[32,128]{1,0:T(8,128)S(1)}, f32[32,128]{1,0:T(8,128)S(1)}, u32[]{:S(2)}, u32[]{:S(2)}) collective-permute-start(f32[32,128]{1,0:T(8,128)S(1)} %get-tuple-element.59), channel_id=1, source_target_pairs={{0,17},{1,16},{2,19},{3,18},{4,21},{5,20},{6,23},{7,22},{8,25},{9,... | collective-permute-start | bytes 49160 | tf_op jit(solution)/shard_map/ppermute | solution.py:563
  26.7 1.0 %collective-permute-start.9 = (f32[32,128]{1,0:T(8,128)S(1)}, f32[32,128]{1,0:T(8,128)S(1)}, u32[]{:S(2)}, u32[]{:S(2)}) collective-permute-start(f32[32,128]{1,0:T(8,128)S(1)} %get-tuple-element.57), channel_id=1, source_target_pairs={{0,9},{1,8},{2,11},{3,10},{4,13},{5,12},{6,15},{7,14},{8,17},{9,16... | collective-permute-start | bytes 49160 | tf_op jit(solution)/shard_map/ppermute | solution.py:563
  27.8 1.6 %collective-permute-done.11.refs_2_ = f32[32,128]{1,0:T(8,128)S(1)} collective-permute-done((f32[32,128]{1,0:T(8,128)S(1)}, f32[32,128]{1,0:T(8,128)S(1)}, u32[]{:S(2)}, u32[]{:S(2)}) %collective-permute-start.11) | collective-permute-done | bytes 16416 | tf_op jit(solution)/shard_map/ppermute | solution.py:563
  29.4 1.9 %collective-permute-done.9.refs_0_ = f32[32,128]{1,0:T(8,128)S(1)} collective-permute-done((f32[32,128]{1,0:T(8,128)S(1)}, f32[32,128]{1,0:T(8,128)S(1)}, u32[]{:S(2)}, u32[]{:S(2)}) %collective-permute-start.9) | collective-permute-done | bytes 16416 | tf_op jit(solution)/shard_map/ppermute | solution.py:563
  32.1 0.9 %collective-permute-done.13.other = f32[40,128]{1,0:T(8,128)S(1)} collective-permute-done((f32[40,128]{1,0:T(8,128)S(1)}, f32[40,128]{1,0:T(8,128)S(1)}, u32[]{:S(2)}, u32[]{:S(2)}) %collective-permute-start.13) | collective-permute-done | bytes 20512 | tf_op jit(solution)/shard_map/ppermute | solution.py:602
  33.0 3.1 %collective-permute-start.14 = (f32[40,128]{1,0:T(8,128)S(1)}, f32[40,128]{1,0:T(8,128)S(1)}, u32[]{:S(2)}, u32[]{:S(2)}) collective-permute-start(f32[40,128]{1,0:T(8,128)S(1)} %get-tuple-element.64.refs_0_), channel_id=1, source_target_pairs={{0,4},{1,5},{2,6},{3,7},{4,0},{5,1},{6,2},{7,3},{8,12},{9,13},{10,... | collective-permute-start | bytes 61448 | tf_op jit(solution)/shard_map/ppermute | solution.py:607
  36.4 2.9 %collective-permute-start.16 = (f32[40,128]{1,0:T(8,128)S(1)}, f32[40,128]{1,0:T(8,128)S(1)}, u32[]{:S(2)}, u32[]{:S(2)}) collective-permute-start(f32[40,128]{1,0:T(8,128)S(1)} %get-tuple-element.64.refs_0_), channel_id=1, source_target_pairs={{0,6},{1,7},{2,0},{3,1},{4,2},{5,3},{6,4},{7,5},{8,14},{9,15},{10,... | collective-permute-start | bytes 61448 | tf_op jit(solution)/shard_map/ppermute | solution.py:607
  39.3 0.9 %shard_map.37 = (f32[1024,128]{1,0:T(8,128)S(1)}, f32[1024,128]{1,0:T(8,128)S(1)}) custom-call(f32[1024,128]{1,0:T(8,128)S(1)} %bitcast.5, f32[40,128]{1,0:T(8,128)S(1)} %get-tuple-element.63.mine.ready), custom_call_target="tpu_custom_call" | custom-call | flops 4194304 | bytes 1048576 | tf_op jit(solution)/shard_map/pallas_call | solution.py:18
  40.5 0.6 %collective-permute-done.15.refs_2_ = f32[40,128]{1,0:T(8,128)S(1)} collective-permute-done((f32[40,128]{1,0:T(8,128)S(1)}, f32[40,128]{1,0:T(8,128)S(1)}, u32[]{:S(2)}, u32[]{:S(2)}) %collective-permute-start.15) | collective-permute-done | bytes 20512 | tf_op jit(solution)/shard_map/ppermute | solution.py:607
  41.0 1.2 %shard_map.39 = f32[1024,128]{1,0:T(8,128)} custom-call(f32[40,128]{1,0:T(8,128)S(1)} %get-tuple-element.64.refs_0_, f32[40,128]{1,0:T(8,128)S(1)} %collective-permute-done.14.refs_1_, f32[40,128]{1,0:T(8,128)S(1)} %collective-permute-done.15.refs_2_, f32[40,128]{1,0:T(8,128)S(1)} %collective-permute-done.16.refs_3_, ...), custom_call_target="tpu_custom_call" | custom-call | flops 4194304 | bytes 1048576 | tf_op jit(solution)/shard_map/pallas_call | solution.py:18
  (26 shorter events, 2.6 us)
Async XLA Ops:
  1.6 4.9 %collective-permute-start = (f32[16,128]{1,0:T(8,128)S(1)}, f32[16,128]{1,0:T(8,128)S(1)}, u32[]{:S(2)}, u32[]{:S(2)}) collective-permute-start(f32[16,128]{1,0:T(8,128)S(1)} %get-tuple-element.38.high), channel_id=1, source_target_pairs={{0,1},{1,2},{2,3},{3,4},{4,5},{5,6},{6,7},{7,0},{8,9},{9,10},{10,1... | collective-permute-start | bytes 24584 | tf_op jit(solution)/shard_map/ppermute | solution.py:541
  1.6 5.0 %collective-permute-start.1 = (f32[16,128]{1,0:T(8,128)S(1)}, f32[16,128]{1,0:T(8,128)S(1)}, u32[]{:S(2)}, u32[]{:S(2)}) collective-permute-start(f32[16,128]{1,0:T(8,128)S(1)} %get-tuple-element.37.low), channel_id=1, source_target_pairs={{1,0},{2,1},{3,2},{4,3},{5,4},{6,5},{7,6},{0,7},{9,8},{10,9},{11,1... | collective-permute-start | bytes 24584 | tf_op jit(solution)/shard_map/ppermute | solution.py:542
  6.5 14.2 %copy-start = (f32[64,16,128]{2,1,0:T(8,128)S(1)}, f32[64,16,128]{2,1,0:T(8,128)}, u32[]{:S(2)}) copy-start(f32[64,16,128]{2,1,0:T(8,128)} %param.3) | copy-start | bytes 1572868
  7.1 5.1 %collective-permute-start.2 = (f32[112,128]{1,0:T(8,128)S(1)}, f32[112,128]{1,0:T(8,128)S(1)}, u32[]{:S(2)}, u32[]{:S(2)}) collective-permute-start(f32[112,128]{1,0:T(8,128)S(1)} %get-tuple-element.47), channel_id=1, source_target_pairs={{0,9},{1,8},{2,11},{3,10},{4,13},{5,12},{6,15},{7,14},{8,17},{9,16... | collective-permute-start | bytes 172040 | tf_op jit(solution)/shard_map/ppermute | solution.py:563
  8.5 3.8 %collective-permute-start.3 = (f32[112,128]{1,0:T(8,128)S(1)}, f32[112,128]{1,0:T(8,128)S(1)}, u32[]{:S(2)}, u32[]{:S(2)}) collective-permute-start(f32[112,128]{1,0:T(8,128)S(1)} %get-tuple-element.48), channel_id=1, source_target_pairs={{0,25},{1,24},{2,27},{3,26},{4,29},{5,28},{6,31},{7,30},{8,1},{9,0... | collective-permute-start | bytes 172040 | tf_op jit(solution)/shard_map/ppermute | solution.py:563
  10.1 5.3 %collective-permute-start.4 = (f32[112,128]{1,0:T(8,128)S(1)}, f32[112,128]{1,0:T(8,128)S(1)}, u32[]{:S(2)}, u32[]{:S(2)}) collective-permute-start(f32[112,128]{1,0:T(8,128)S(1)} %get-tuple-element.49), channel_id=1, source_target_pairs={{0,17},{1,16},{2,19},{3,18},{4,21},{5,20},{6,23},{7,22},{8,25},{9,... | collective-permute-start | bytes 172040 | tf_op jit(solution)/shard_map/ppermute | solution.py:563
  11.7 3.6 %collective-permute-start.5 = (f32[112,128]{1,0:T(8,128)S(1)}, f32[112,128]{1,0:T(8,128)S(1)}, u32[]{:S(2)}, u32[]{:S(2)}) collective-permute-start(f32[112,128]{1,0:T(8,128)S(1)} %get-tuple-element.50), channel_id=1, source_target_pairs={{0,1},{1,0},{2,3},{3,2},{4,5},{5,4},{6,7},{7,6},{8,9},{9,8},{10,11... | collective-permute-start | bytes 172040 | tf_op jit(solution)/shard_map/ppermute | solution.py:563
  15.5 6.6 %collective-permute-start.6 = (f32[112,128]{1,0:T(8,128)S(1)}, f32[112,128]{1,0:T(8,128)S(1)}, u32[]{:S(2)}, u32[]{:S(2)}) collective-permute-start(f32[112,128]{1,0:T(8,128)S(1)} %get-tuple-element.51.refs_3_), channel_id=1, source_target_pairs={{0,32},{8,40},{16,48},{24,56},{32,64},{40,72},{48,80},{56,88},{64,... | collective-permute-start | bytes 172040 | tf_op jit(solution)/shard_map/ppermute | solution.py:563
  17.1 4.9 %collective-permute-start.7 = (f32[112,128]{1,0:T(8,128)S(1)}, f32[112,128]{1,0:T(8,128)S(1)}, u32[]{:S(2)}, u32[]{:S(2)}) collective-permute-start(f32[112,128]{1,0:T(8,128)S(1)} %get-tuple-element.51.refs_3_), channel_id=1, source_target_pairs={{0,96},{8,104},{16,112},{24,120},{32,0},{40,8},{48,16},{56,24},{64... | collective-permute-start | bytes 172040 | tf_op jit(solution)/shard_map/ppermute | solution.py:563
  18.8 5.7 %collective-permute-start.8 = (f32[112,128]{1,0:T(8,128)S(1)}, f32[112,128]{1,0:T(8,128)S(1)}, u32[]{:S(2)}, u32[]{:S(2)}) collective-permute-start(f32[112,128]{1,0:T(8,128)S(1)} %get-tuple-element.51.refs_3_), channel_id=1, source_target_pairs={{0,64},{8,72},{16,80},{24,88},{32,96},{40,104},{48,112},{56,120},{... | collective-permute-start | bytes 172040 | tf_op jit(solution)/shard_map/ppermute | solution.py:563
  24.4 6.8 %copy-start.1 = (f32[64,16,128]{2,1,0:T(8,128)S(1)}, f32[64,16,128]{2,1,0:T(8,128)}, u32[]{:S(2)}) copy-start(f32[64,16,128]{2,1,0:T(8,128)} %param.2) | copy-start | bytes 1572868
  24.5 3.2 %collective-permute-start.10 = (f32[32,128]{1,0:T(8,128)S(1)}, f32[32,128]{1,0:T(8,128)S(1)}, u32[]{:S(2)}, u32[]{:S(2)}) collective-permute-start(f32[32,128]{1,0:T(8,128)S(1)} %get-tuple-element.58), channel_id=1, source_target_pairs={{0,25},{1,24},{2,27},{3,26},{4,29},{5,28},{6,31},{7,30},{8,1},{9,0... | collective-permute-start | bytes 49160 | tf_op jit(solution)/shard_map/ppermute | solution.py:563
  24.6 4.7 %collective-permute-start.11 = (f32[32,128]{1,0:T(8,128)S(1)}, f32[32,128]{1,0:T(8,128)S(1)}, u32[]{:S(2)}, u32[]{:S(2)}) collective-permute-start(f32[32,128]{1,0:T(8,128)S(1)} %get-tuple-element.59), channel_id=1, source_target_pairs={{0,17},{1,16},{2,19},{3,18},{4,21},{5,20},{6,23},{7,22},{8,25},{9,... | collective-permute-start | bytes 49160 | tf_op jit(solution)/shard_map/ppermute | solution.py:563
  26.7 2.7 %collective-permute-start.12 = (f32[32,128]{1,0:T(8,128)S(1)}, f32[32,128]{1,0:T(8,128)S(1)}, u32[]{:S(2)}, u32[]{:S(2)}) collective-permute-start(f32[32,128]{1,0:T(8,128)S(1)} %get-tuple-element.60), channel_id=1, source_target_pairs={{0,1},{1,0},{2,3},{3,2},{4,5},{5,4},{6,7},{7,6},{8,9},{9,8},{10,11... | collective-permute-start | bytes 49160 | tf_op jit(solution)/shard_map/ppermute | solution.py:563
  26.7 4.6 %collective-permute-start.9 = (f32[32,128]{1,0:T(8,128)S(1)}, f32[32,128]{1,0:T(8,128)S(1)}, u32[]{:S(2)}, u32[]{:S(2)}) collective-permute-start(f32[32,128]{1,0:T(8,128)S(1)} %get-tuple-element.57), channel_id=1, source_target_pairs={{0,9},{1,8},{2,11},{3,10},{4,13},{5,12},{6,15},{7,14},{8,17},{9,16... | collective-permute-start | bytes 49160 | tf_op jit(solution)/shard_map/ppermute | solution.py:563
  31.7 1.3 %collective-permute-start.13 = (f32[40,128]{1,0:T(8,128)S(1)}, f32[40,128]{1,0:T(8,128)S(1)}, u32[]{:S(2)}, u32[]{:S(2)}) collective-permute-start(f32[40,128]{1,0:T(8,128)S(1)} %get-tuple-element.63.mine.ready), channel_id=1, source_target_pairs={{0,1},{1,0},{2,3},{3,2},{4,5},{5,4},{6,7},{7,6},{8,9},{9,8},{10,11... | collective-permute-start | bytes 61448 | tf_op jit(solution)/shard_map/ppermute | solution.py:602
  33.0 7.5 %collective-permute-start.14 = (f32[40,128]{1,0:T(8,128)S(1)}, f32[40,128]{1,0:T(8,128)S(1)}, u32[]{:S(2)}, u32[]{:S(2)}) collective-permute-start(f32[40,128]{1,0:T(8,128)S(1)} %get-tuple-element.64.refs_0_), channel_id=1, source_target_pairs={{0,4},{1,5},{2,6},{3,7},{4,0},{5,1},{6,2},{7,3},{8,12},{9,13},{10,... | collective-permute-start | bytes 61448 | tf_op jit(solution)/shard_map/ppermute | solution.py:607
  36.0 5.0 %collective-permute-start.15 = (f32[40,128]{1,0:T(8,128)S(1)}, f32[40,128]{1,0:T(8,128)S(1)}, u32[]{:S(2)}, u32[]{:S(2)}) collective-permute-start(f32[40,128]{1,0:T(8,128)S(1)} %get-tuple-element.64.refs_0_), channel_id=1, source_target_pairs={{0,2},{1,3},{2,4},{3,5},{4,6},{5,7},{6,0},{7,1},{8,10},{9,11},{10,... | collective-permute-start | bytes 61448 | tf_op jit(solution)/shard_map/ppermute | solution.py:607
  36.4 4.6 %collective-permute-start.16 = (f32[40,128]{1,0:T(8,128)S(1)}, f32[40,128]{1,0:T(8,128)S(1)}, u32[]{:S(2)}, u32[]{:S(2)}) collective-permute-start(f32[40,128]{1,0:T(8,128)S(1)} %get-tuple-element.64.refs_0_), channel_id=1, source_target_pairs={{0,6},{1,7},{2,0},{3,1},{4,2},{5,3},{6,4},{7,5},{8,14},{9,15},{10,... | collective-permute-start | bytes 61448 | tf_op jit(solution)/shard_map/ppermute | solution.py:607

commit v9 on v8

--- a/solution.py
+++ b/solution.py
@@ -337,6 +337,10 @@
     return [1, 3, 2, 0]
 
 
+def across_order(group):
+    return [1, 2, 3, 0]
+
+
 def system(blocks, nothing):
     low, diag, up, rhs = [], [], [], []
     for before, after in zip([nothing] + blocks, blocks + [nothing]):
@@ -390,7 +394,7 @@
     own = got[0].shape[0] // 7
     row_index = lax.axis_index("row")
     mine, outer = lax.rem(row_index, group), lax.div(row_index, group)
-    for step, ref in zip(shift_order(group), got):
+    for step, ref in zip(across_order(group), got):
         recv[lax.rem(outer + group - step, group)] = ref[...]
     blocks = [tuple(recv[d, q * own : (q + 1) * own, :] for q in range(7)) for d in range(group)]
     q = solve(*system(blocks, (jnp.zeros((own, 128), F32),) * 7))
@@ -561,7 +565,7 @@
     def exchange(arrays, pairs, axes):
         return [
             lax.ppermute(arrays[step], axes, pairs[step]) if step or axes != "row" else arrays[0]
-            for step in shift_order(group)
+            for step in (across_order if axes == "row" else shift_order)(group)
         ]
 
     *parts, full, faces = call(

time: 42.3 us -> 42.1 us (level)
  waiting for transfers between devices: 11.3 us -> 10.4 us
  starting transfers between devices: 23.7 us -> 24.3 us
    ppermute x11, waiting for transfers between devices: 9.31 us -> 8.45 us  [exchange(): lax.ppermute(arrays[step], axes, pairs[step])]
    ppermute x11, starting transfers between devices: 13.4 us -> 14 us  [exchange(): lax.ppermute(arrays[step], axes, pairs[step])]
  transfers between devices with their start and end apart: 17 -> 17, of which waited for: 11 -> 12; matrix products, arithmetic and copies ran while one was open for 0% -> 0% of each run, Pallas kernels for 8% -> 8%
where the time goes in v9:
time: 42.1 us; the launch traced here: 42 us
  starting transfers between devices  24.3 us (58%)
  waiting for transfers between devices  10.4 us (25%)
  Pallas kernels  7.16 us (17%)
    ppermute x11, starting transfers between devices, exchange(): lax.ppermute(arrays[step], axes, pairs[step])  14 us
    ppermute x11, waiting for transfers between devices, exchange(): lax.ppermute(arrays[step], axes, pairs[step])  8.45 us
    pallas_call x12, Pallas kernels, call(): pl.pallas_call(kernel, out_shape=[jax.ShapeDtypeStruct(s, F32) for s in o...  7.16 us
    ppermute x3, starting transfers between devices, on_device(): lax.ppermute(sup, 'col', [(i, (i + 2 * step) % colp) for i in range(colp)])  6.29 us
    ppermute x1, starting transfers between devices, on_device(): from_right = lax.ppermute(low, 'col', [(b, a) for a, b in up])  3.6 us
    ppermute x1, waiting for transfers between devices, on_device(): other = lax.ppermute(send, 'col', [(i, i ^ 1) for i in range(colp)])  0.86 us
  transfers between devices with their start and end apart: 17, of which 12 were waited for; matrix products, arithmetic and copies ran while one was open for 0% of the time, Pallas kernels for 8%

profile of v9, /device:TPU:0, one launch (start us, length us, event | category | flops | bytes accessed | tf_op | source)
XLA Modules:
  0.0 42.0 jit_solution(17516298621520881384)
XLA Ops:
  0.0 1.5 %shard_map.28 = (f32[1024,128]{1,0:T(8,128)S(1)}, f32[1024,128]{1,0:T(8,128)S(1)}, f32[1024,128]{1,0:T(8,128)S(1)}, f32[1024,128]{1,0:T(8,128)S(1)}, f32[16,128]{1,0:T(8,128)S(1)}, /*index=5*/f32[16,128]{1,0:T(8,128)S(1)}) custom-call(f32[1024,128]{1,0:T(8,128)} %bitcast.6, f32[1024,128]{1,0:T(8,128)} %bitcast.3), custom_call_target="tpu_custom_call" | custom-call | flops 1048576 | bytes 1048576 | tf_op jit(solution)/shard_map/pallas_call | solution.py:18
  1.6 3.6 %collective-permute-start.1 = (f32[16,128]{1,0:T(8,128)S(1)}, f32[16,128]{1,0:T(8,128)S(1)}, u32[]{:S(2)}, u32[]{:S(2)}) collective-permute-start(f32[16,128]{1,0:T(8,128)S(1)} %get-tuple-element.37.low), channel_id=1, source_target_pairs={{1,0},{2,1},{3,2},{4,3},{5,4},{6,5},{7,6},{0,7},{9,8},{10,9},{11,1... | collective-permute-start | bytes 24584 | tf_op jit(solution)/shard_map/ppermute | solution.py:546
  5.2 0.8 %shard_map.29 = (f32[16,64,128]{2,1,0:T(8,128)S(1)}, f32[16,64,128]{2,1,0:T(8,128)S(1)}, f32[16,64,128]{2,1,0:T(8,128)S(1)}, f32[16,64,128]{2,1,0:T(8,128)S(1)},...) custom-call(f32[1024,128]{1,0:T(8,128)S(1)} %get-tuple-element.39.u, f32[1024,128]{1,0:T(8,128)S(1)} %get-tuple-element.40.k, ...), custom_call_target="tpu_custom_call" | custom-call | flops 8388608 | bytes 1048576 | tf_op jit(solution)/shard_map/pallas_call | solution.py:18
  6.5 0.5 %shard_map.30 = (f32[112,128]{1,0:T(8,128)S(1)}, f32[112,128]{1,0:T(8,128)S(1)}, f32[112,128]{1,0:T(8,128)S(1)}, f32[112,128]{1,0:T(8,128)S(1)}, f32[1024,128]{1,0:T(8,128)S(1)}, /*index=5*/f32[16,128]{1,0:T(8,128)S(1)}) custom-call(f32[16,128]{1,0:T(8,128)S(1)} %get-tuple-element.37.low, f32[16,128]{1,0:T(8,128)S(1)} %get-tuple-element.38.high, ...), custom_call_target="tpu_custom_call" | custom-call | flops 4194304 | bytes 1048576 | tf_op jit(solution)/shard_map/pallas_call | solution.py:18
  7.1 1.4 %collective-permute-start.2 = (f32[112,128]{1,0:T(8,128)S(1)}, f32[112,128]{1,0:T(8,128)S(1)}, u32[]{:S(2)}, u32[]{:S(2)}) collective-permute-start(f32[112,128]{1,0:T(8,128)S(1)} %get-tuple-element.47), channel_id=1, source_target_pairs={{0,9},{1,8},{2,11},{3,10},{4,13},{5,12},{6,15},{7,14},{8,17},{9,16... | collective-permute-start | bytes 172040 | tf_op jit(solution)/shard_map/ppermute | solution.py:567
  8.5 1.6 %collective-permute-start.3 = (f32[112,128]{1,0:T(8,128)S(1)}, f32[112,128]{1,0:T(8,128)S(1)}, u32[]{:S(2)}, u32[]{:S(2)}) collective-permute-start(f32[112,128]{1,0:T(8,128)S(1)} %get-tuple-element.48), channel_id=1, source_target_pairs={{0,25},{1,24},{2,27},{3,26},{4,29},{5,28},{6,31},{7,30},{8,1},{9,0... | collective-permute-start | bytes 172040 | tf_op jit(solution)/shard_map/ppermute | solution.py:567
  10.1 1.7 %collective-permute-start.4 = (f32[112,128]{1,0:T(8,128)S(1)}, f32[112,128]{1,0:T(8,128)S(1)}, u32[]{:S(2)}, u32[]{:S(2)}) collective-permute-start(f32[112,128]{1,0:T(8,128)S(1)} %get-tuple-element.49), channel_id=1, source_target_pairs={{0,17},{1,16},{2,19},{3,18},{4,21},{5,20},{6,23},{7,22},{8,25},{9,... | collective-permute-start | bytes 172040 | tf_op jit(solution)/shard_map/ppermute | solution.py:567
  12.2 3.2 %collective-permute-done.4.refs_2_ = f32[112,128]{1,0:T(8,128)S(1)} collective-permute-done((f32[112,128]{1,0:T(8,128)S(1)}, f32[112,128]{1,0:T(8,128)S(1)}, u32[]{:S(2)}, u32[]{:S(2)}) %collective-permute-start.4) | collective-permute-done | bytes 57376 | tf_op jit(solution)/shard_map/ppermute | solution.py:567
  15.5 1.6 %collective-permute-start.6 = (f32[112,128]{1,0:T(8,128)S(1)}, f32[112,128]{1,0:T(8,128)S(1)}, u32[]{:S(2)}, u32[]{:S(2)}) collective-permute-start(f32[112,128]{1,0:T(8,128)S(1)} %get-tuple-element.51.refs_3_), channel_id=1, source_target_pairs={{0,32},{8,40},{16,48},{24,56},{32,64},{40,72},{48,80},{56,88},{64,... | collective-permute-start | bytes 172040 | tf_op jit(solution)/shard_map/ppermute | solution.py:567
  17.1 2.9 %collective-permute-start.7 = (f32[112,128]{1,0:T(8,128)S(1)}, f32[112,128]{1,0:T(8,128)S(1)}, u32[]{:S(2)}, u32[]{:S(2)}) collective-permute-start(f32[112,128]{1,0:T(8,128)S(1)} %get-tuple-element.51.refs_3_), channel_id=1, source_target_pairs={{0,64},{8,72},{16,80},{24,88},{32,96},{40,104},{48,112},{56,120},{... | collective-permute-start | bytes 172040 | tf_op jit(solution)/shard_map/ppermute | solution.py:567
  20.0 1.3 %collective-permute-start.8 = (f32[112,128]{1,0:T(8,128)S(1)}, f32[112,128]{1,0:T(8,128)S(1)}, u32[]{:S(2)}, u32[]{:S(2)}) collective-permute-start(f32[112,128]{1,0:T(8,128)S(1)} %get-tuple-element.51.refs_3_), channel_id=1, source_target_pairs={{0,96},{8,104},{16,112},{24,120},{32,0},{40,8},{48,16},{56,24},{64... | collective-permute-start | bytes 172040 | tf_op jit(solution)/shard_map/ppermute | solution.py:567
  21.4 1.1 %shard_map.33 = (f32[1024,128]{1,0:T(8,128)S(1)}, f32[1024,128]{1,0:T(8,128)S(1)}) custom-call(f32[1024,128]{1,0:T(8,128)S(1)} %bitcast.4), custom_call_target="tpu_custom_call" | custom-call | flops 8388608 | bytes 1048576 | tf_op jit(solution)/shard_map/pallas_call | solution.py:18
  22.6 0.6 %collective-permute-done.7.refs_1_ = f32[112,128]{1,0:T(8,128)S(1)} collective-permute-done((f32[112,128]{1,0:T(8,128)S(1)}, f32[112,128]{1,0:T(8,128)S(1)}, u32[]{:S(2)}, u32[]{:S(2)}) %collective-permute-start.7) | collective-permute-done | bytes 57376 | tf_op jit(solution)/shard_map/ppermute | solution.py:567
  23.3 0.9 %collective-permute-done.8.refs_2_ = f32[112,128]{1,0:T(8,128)S(1)} collective-permute-done((f32[112,128]{1,0:T(8,128)S(1)}, f32[112,128]{1,0:T(8,128)S(1)}, u32[]{:S(2)}, u32[]{:S(2)}) %collective-permute-start.8) | collective-permute-done | bytes 57376 | tf_op jit(solution)/shard_map/ppermute | solution.py:567
  24.4 2.1 %collective-permute-start.11 = (f32[32,128]{1,0:T(8,128)S(1)}, f32[32,128]{1,0:T(8,128)S(1)}, u32[]{:S(2)}, u32[]{:S(2)}) collective-permute-start(f32[32,128]{1,0:T(8,128)S(1)} %get-tuple-element.59), channel_id=1, source_target_pairs={{0,17},{1,16},{2,19},{3,18},{4,21},{5,20},{6,23},{7,22},{8,25},{9,... | collective-permute-start | bytes 49160 | tf_op jit(solution)/shard_map/ppermute | solution.py:567
  26.4 1.0 %collective-permute-start.9 = (f32[32,128]{1,0:T(8,128)S(1)}, f32[32,128]{1,0:T(8,128)S(1)}, u32[]{:S(2)}, u32[]{:S(2)}) collective-permute-start(f32[32,128]{1,0:T(8,128)S(1)} %get-tuple-element.57), channel_id=1, source_target_pairs={{0,9},{1,8},{2,11},{3,10},{4,13},{5,12},{6,15},{7,14},{8,17},{9,16... | collective-permute-start | bytes 49160 | tf_op jit(solution)/shard_map/ppermute | solution.py:567
  27.5 1.6 %collective-permute-done.11.refs_2_ = f32[32,128]{1,0:T(8,128)S(1)} collective-permute-done((f32[32,128]{1,0:T(8,128)S(1)}, f32[32,128]{1,0:T(8,128)S(1)}, u32[]{:S(2)}, u32[]{:S(2)}) %collective-permute-start.11) | collective-permute-done | bytes 16416 | tf_op jit(solution)/shard_map/ppermute | solution.py:567
  29.1 1.9 %collective-permute-done.9.refs_0_ = f32[32,128]{1,0:T(8,128)S(1)} collective-permute-done((f32[32,128]{1,0:T(8,128)S(1)}, f32[32,128]{1,0:T(8,128)S(1)}, u32[]{:S(2)}, u32[]{:S(2)}) %collective-permute-start.9) | collective-permute-done | bytes 16416 | tf_op jit(solution)/shard_map/ppermute | solution.py:567
  31.8 0.9 %collective-permute-done.13.other = f32[40,128]{1,0:T(8,128)S(1)} collective-permute-done((f32[40,128]{1,0:T(8,128)S(1)}, f32[40,128]{1,0:T(8,128)S(1)}, u32[]{:S(2)}, u32[]{:S(2)}) %collective-permute-start.13) | collective-permute-done | bytes 20512 | tf_op jit(solution)/shard_map/ppermute | solution.py:606
  32.7 3.1 %collective-permute-start.14 = (f32[40,128]{1,0:T(8,128)S(1)}, f32[40,128]{1,0:T(8,128)S(1)}, u32[]{:S(2)}, u32[]{:S(2)}) collective-permute-start(f32[40,128]{1,0:T(8,128)S(1)} %get-tuple-element.64.refs_0_), channel_id=1, source_target_pairs={{0,4},{1,5},{2,6},{3,7},{4,0},{5,1},{6,2},{7,3},{8,12},{9,13},{10,... | collective-permute-start | bytes 61448 | tf_op jit(solution)/shard_map/ppermute | solution.py:611
  36.1 2.9 %collective-permute-start.16 = (f32[40,128]{1,0:T(8,128)S(1)}, f32[40,128]{1,0:T(8,128)S(1)}, u32[]{:S(2)}, u32[]{:S(2)}) collective-permute-start(f32[40,128]{1,0:T(8,128)S(1)} %get-tuple-element.64.refs_0_), channel_id=1, source_target_pairs={{0,6},{1,7},{2,0},{3,1},{4,2},{5,3},{6,4},{7,5},{8,14},{9,15},{10,... | collective-permute-start | bytes 61448 | tf_op jit(solution)/shard_map/ppermute | solution.py:611
  39.0 0.9 %shard_map.37 = (f32[1024,128]{1,0:T(8,128)S(1)}, f32[1024,128]{1,0:T(8,128)S(1)}) custom-call(f32[1024,128]{1,0:T(8,128)S(1)} %bitcast.5, f32[40,128]{1,0:T(8,128)S(1)} %get-tuple-element.63.mine.ready), custom_call_target="tpu_custom_call" | custom-call | flops 4194304 | bytes 1048576 | tf_op jit(solution)/shard_map/pallas_call | solution.py:18
  40.2 0.6 %collective-permute-done.15.refs_2_ = f32[40,128]{1,0:T(8,128)S(1)} collective-permute-done((f32[40,128]{1,0:T(8,128)S(1)}, f32[40,128]{1,0:T(8,128)S(1)}, u32[]{:S(2)}, u32[]{:S(2)}) %collective-permute-start.15) | collective-permute-done | bytes 20512 | tf_op jit(solution)/shard_map/ppermute | solution.py:611
  40.8 1.2 %shard_map.39 = f32[1024,128]{1,0:T(8,128)} custom-call(f32[40,128]{1,0:T(8,128)S(1)} %get-tuple-element.64.refs_0_, f32[40,128]{1,0:T(8,128)S(1)} %collective-permute-done.14.refs_1_, f32[40,128]{1,0:T(8,128)S(1)} %collective-permute-done.15.refs_2_, f32[40,128]{1,0:T(8,128)S(1)} %collective-permute-done.16.refs_3_, ...), custom_call_target="tpu_custom_call" | custom-call | flops 4194304 | bytes 1048576 | tf_op jit(solution)/shard_map/pallas_call | solution.py:18
  (26 shorter events, 3.0 us)
Async XLA Ops:
  1.6 4.9 %collective-permute-start = (f32[16,128]{1,0:T(8,128)S(1)}, f32[16,128]{1,0:T(8,128)S(1)}, u32[]{:S(2)}, u32[]{:S(2)}) collective-permute-start(f32[16,128]{1,0:T(8,128)S(1)} %get-tuple-element.38.high), channel_id=1, source_target_pairs={{0,1},{1,2},{2,3},{3,4},{4,5},{5,6},{6,7},{7,0},{8,9},{9,10},{10,1... | collective-permute-start | bytes 24584 | tf_op jit(solution)/shard_map/ppermute | solution.py:545
  1.6 5.0 %collective-permute-start.1 = (f32[16,128]{1,0:T(8,128)S(1)}, f32[16,128]{1,0:T(8,128)S(1)}, u32[]{:S(2)}, u32[]{:S(2)}) collective-permute-start(f32[16,128]{1,0:T(8,128)S(1)} %get-tuple-element.37.low), channel_id=1, source_target_pairs={{1,0},{2,1},{3,2},{4,3},{5,4},{6,5},{7,6},{0,7},{9,8},{10,9},{11,1... | collective-permute-start | bytes 24584 | tf_op jit(solution)/shard_map/ppermute | solution.py:546
  6.5 14.8 %copy-start = (f32[64,16,128]{2,1,0:T(8,128)S(1)}, f32[64,16,128]{2,1,0:T(8,128)}, u32[]{:S(2)}) copy-start(f32[64,16,128]{2,1,0:T(8,128)} %param.3) | copy-start | bytes 1572868
  7.1 5.1 %collective-permute-start.2 = (f32[112,128]{1,0:T(8,128)S(1)}, f32[112,128]{1,0:T(8,128)S(1)}, u32[]{:S(2)}, u32[]{:S(2)}) collective-permute-start(f32[112,128]{1,0:T(8,128)S(1)} %get-tuple-element.47), channel_id=1, source_target_pairs={{0,9},{1,8},{2,11},{3,10},{4,13},{5,12},{6,15},{7,14},{8,17},{9,16... | collective-permute-start | bytes 172040 | tf_op jit(solution)/shard_map/ppermute | solution.py:567
  8.5 3.8 %collective-permute-start.3 = (f32[112,128]{1,0:T(8,128)S(1)}, f32[112,128]{1,0:T(8,128)S(1)}, u32[]{:S(2)}, u32[]{:S(2)}) collective-permute-start(f32[112,128]{1,0:T(8,128)S(1)} %get-tuple-element.48), channel_id=1, source_target_pairs={{0,25},{1,24},{2,27},{3,26},{4,29},{5,28},{6,31},{7,30},{8,1},{9,0... | collective-permute-start | bytes 172040 | tf_op jit(solution)/shard_map/ppermute | solution.py:567
  10.1 5.3 %collective-permute-start.4 = (f32[112,128]{1,0:T(8,128)S(1)}, f32[112,128]{1,0:T(8,128)S(1)}, u32[]{:S(2)}, u32[]{:S(2)}) collective-permute-start(f32[112,128]{1,0:T(8,128)S(1)} %get-tuple-element.49), channel_id=1, source_target_pairs={{0,17},{1,16},{2,19},{3,18},{4,21},{5,20},{6,23},{7,22},{8,25},{9,... | collective-permute-start | bytes 172040 | tf_op jit(solution)/shard_map/ppermute | solution.py:567
  11.7 3.6 %collective-permute-start.5 = (f32[112,128]{1,0:T(8,128)S(1)}, f32[112,128]{1,0:T(8,128)S(1)}, u32[]{:S(2)}, u32[]{:S(2)}) collective-permute-start(f32[112,128]{1,0:T(8,128)S(1)} %get-tuple-element.50), channel_id=1, source_target_pairs={{0,1},{1,0},{2,3},{3,2},{4,5},{5,4},{6,7},{7,6},{8,9},{9,8},{10,11... | collective-permute-start | bytes 172040 | tf_op jit(solution)/shard_map/ppermute | solution.py:567
  15.5 7.2 %collective-permute-start.6 = (f32[112,128]{1,0:T(8,128)S(1)}, f32[112,128]{1,0:T(8,128)S(1)}, u32[]{:S(2)}, u32[]{:S(2)}) collective-permute-start(f32[112,128]{1,0:T(8,128)S(1)} %get-tuple-element.51.refs_3_), channel_id=1, source_target_pairs={{0,32},{8,40},{16,48},{24,56},{32,64},{40,72},{48,80},{56,88},{64,... | collective-permute-start | bytes 172040 | tf_op jit(solution)/shard_map/ppermute | solution.py:567
  17.1 6.2 %collective-permute-start.7 = (f32[112,128]{1,0:T(8,128)S(1)}, f32[112,128]{1,0:T(8,128)S(1)}, u32[]{:S(2)}, u32[]{:S(2)}) collective-permute-start(f32[112,128]{1,0:T(8,128)S(1)} %get-tuple-element.51.refs_3_), channel_id=1, source_target_pairs={{0,64},{8,72},{16,80},{24,88},{32,96},{40,104},{48,112},{56,120},{... | collective-permute-start | bytes 172040 | tf_op jit(solution)/shard_map/ppermute | solution.py:567
  20.0 4.2 %collective-permute-start.8 = (f32[112,128]{1,0:T(8,128)S(1)}, f32[112,128]{1,0:T(8,128)S(1)}, u32[]{:S(2)}, u32[]{:S(2)}) collective-permute-start(f32[112,128]{1,0:T(8,128)S(1)} %get-tuple-element.51.refs_3_), channel_id=1, source_target_pairs={{0,96},{8,104},{16,112},{24,120},{32,0},{40,8},{48,16},{56,24},{64... | collective-permute-start | bytes 172040 | tf_op jit(solution)/shard_map/ppermute | solution.py:567
  24.2 6.8 %copy-start.1 = (f32[64,16,128]{2,1,0:T(8,128)S(1)}, f32[64,16,128]{2,1,0:T(8,128)}, u32[]{:S(2)}) copy-start(f32[64,16,128]{2,1,0:T(8,128)} %param.2) | copy-start | bytes 1572868
  24.3 3.2 %collective-permute-start.10 = (f32[32,128]{1,0:T(8,128)S(1)}, f32[32,128]{1,0:T(8,128)S(1)}, u32[]{:S(2)}, u32[]{:S(2)}) collective-permute-start(f32[32,128]{1,0:T(8,128)S(1)} %get-tuple-element.58), channel_id=1, source_target_pairs={{0,25},{1,24},{2,27},{3,26},{4,29},{5,28},{6,31},{7,30},{8,1},{9,0... | collective-permute-start | bytes 49160 | tf_op jit(solution)/shard_map/ppermute | solution.py:567
  24.4 4.7 %collective-permute-start.11 = (f32[32,128]{1,0:T(8,128)S(1)}, f32[32,128]{1,0:T(8,128)S(1)}, u32[]{:S(2)}, u32[]{:S(2)}) collective-permute-start(f32[32,128]{1,0:T(8,128)S(1)} %get-tuple-element.59), channel_id=1, source_target_pairs={{0,17},{1,16},{2,19},{3,18},{4,21},{5,20},{6,23},{7,22},{8,25},{9,... | collective-permute-start | bytes 49160 | tf_op jit(solution)/shard_map/ppermute | solution.py:567
  26.4 2.7 %collective-permute-start.12 = (f32[32,128]{1,0:T(8,128)S(1)}, f32[32,128]{1,0:T(8,128)S(1)}, u32[]{:S(2)}, u32[]{:S(2)}) collective-permute-start(f32[32,128]{1,0:T(8,128)S(1)} %get-tuple-element.60), channel_id=1, source_target_pairs={{0,1},{1,0},{2,3},{3,2},{4,5},{5,4},{6,7},{7,6},{8,9},{9,8},{10,11... | collective-permute-start | bytes 49160 | tf_op jit(solution)/shard_map/ppermute | solution.py:567
  26.4 4.6 %collective-permute-start.9 = (f32[32,128]{1,0:T(8,128)S(1)}, f32[32,128]{1,0:T(8,128)S(1)}, u32[]{:S(2)}, u32[]{:S(2)}) collective-permute-start(f32[32,128]{1,0:T(8,128)S(1)} %get-tuple-element.57), channel_id=1, source_target_pairs={{0,9},{1,8},{2,11},{3,10},{4,13},{5,12},{6,15},{7,14},{8,17},{9,16... | collective-permute-start | bytes 49160 | tf_op jit(solution)/shard_map/ppermute | solution.py:567
  31.4 1.3 %collective-permute-start.13 = (f32[40,128]{1,0:T(8,128)S(1)}, f32[40,128]{1,0:T(8,128)S(1)}, u32[]{:S(2)}, u32[]{:S(2)}) collective-permute-start(f32[40,128]{1,0:T(8,128)S(1)} %get-tuple-element.63.mine.ready), channel_id=1, source_target_pairs={{0,1},{1,0},{2,3},{3,2},{4,5},{5,4},{6,7},{7,6},{8,9},{9,8},{10,11... | collective-permute-start | bytes 61448 | tf_op jit(solution)/shard_map/ppermute | solution.py:606
  32.7 7.5 %collective-permute-start.14 = (f32[40,128]{1,0:T(8,128)S(1)}, f32[40,128]{1,0:T(8,128)S(1)}, u32[]{:S(2)}, u32[]{:S(2)}) collective-permute-start(f32[40,128]{1,0:T(8,128)S(1)} %get-tuple-element.64.refs_0_), channel_id=1, source_target_pairs={{0,4},{1,5},{2,6},{3,7},{4,0},{5,1},{6,2},{7,3},{8,12},{9,13},{10,... | collective-permute-start | bytes 61448 | tf_op jit(solution)/shard_map/ppermute | solution.py:611
  35.8 5.0 %collective-permute-start.15 = (f32[40,128]{1,0:T(8,128)S(1)}, f32[40,128]{1,0:T(8,128)S(1)}, u32[]{:S(2)}, u32[]{:S(2)}) collective-permute-start(f32[40,128]{1,0:T(8,128)S(1)} %get-tuple-element.64.refs_0_), channel_id=1, source_target_pairs={{0,2},{1,3},{2,4},{3,5},{4,6},{5,7},{6,0},{7,1},{8,10},{9,11},{10,... | collective-permute-start | bytes 61448 | tf_op jit(solution)/shard_map/ppermute | solution.py:611
  36.1 4.6 %collective-permute-start.16 = (f32[40,128]{1,0:T(8,128)S(1)}, f32[40,128]{1,0:T(8,128)S(1)}, u32[]{:S(2)}, u32[]{:S(2)}) collective-permute-start(f32[40,128]{1,0:T(8,128)S(1)} %get-tuple-element.64.refs_0_), channel_id=1, source_target_pairs={{0,6},{1,7},{2,0},{3,1},{4,2},{5,3},{6,4},{7,5},{8,14},{9,15},{10,... | collective-permute-start | bytes 61448 | tf_op jit(solution)/shard_map/ppermute | solution.py:611
